TPU v7x, 32 devices: a whole 2x2x4 slice. The times are simulated.
32 devices in a mesh: parts: 2 (over y), expert: 4 (over z), tensor: 4 (over x, core).
Axes of the slice: x: 2, y: 2, z: 4, core: 2. Of those that a mesh axis runs over, the one named last changes fastest.
Arguments:
- mamba_input: bfloat16 [128, 4096], P(('parts', 'expert'), 'tensor'), parts along dimension 0, may hold values from -5 to 5
- mamba_gate: bfloat16 [128, 4096], P(('parts', 'expert'), 'tensor'), parts along dimension 0, may hold values from -5 to 5
- conv_state: bfloat16 [128, 3, 4096], P(('parts', 'expert'), None, 'tensor'), parts along dimension 0, may hold values from -5 to 5
- scan_state: float32 [128, 16, 4096], P(('parts', 'expert'), None, 'tensor'), parts along dimension 0, may hold values from -6 to 6
- conv_weight: float32 [4, 4096], P(None, 'tensor'), may hold values from -3 to 3
- conv_bias: float32 [4096], P('tensor'), may hold values from -0.5 to 0.5
- state_proj: bfloat16 [288, 4096], P(None, 'tensor'), may hold values from -0.09375 to 0.09375
- step_proj: bfloat16 [256, 4096], P(None, 'tensor'), may hold values from -0.375 to 0.375
- step_bias: float32 [4096], P('tensor'), may hold values from -4.5 to -1
- decay_log: float32 [16, 4096], P(None, 'tensor'), may hold values from 0 to 2.8
- skip_gain: float32 [4096], P('tensor'), may hold values from 0.5 to 2
- queries: bfloat16 [128, 32, 128], P(('parts', 'expert'), 'tensor'), parts along dimension 0, may hold values from -48 to 48
- new_entry: bfloat16 [128, 8, 256], P(('parts', 'expert'), 'tensor'), parts along dimension 0, may hold values from -4 to 4
- past_entries: bfloat16 [128, 8, 128, 256], P(('parts', 'expert'), 'tensor'), parts along dimension 0, may hold values from -4 to 4
- lengths: int32 [128], P(('parts', 'expert')), parts along dimension 0, may hold values from 2 to 128, as said below
- expert_input: bfloat16 [128, 2048], P(('parts', 'expert'), 'tensor'), parts along dimension 0, may hold values from -5 to 5
- routes: int32 [128, 2], P(('parts', 'expert')), parts along dimension 0, may hold values from 0 to 7, as said below
- slots: int32 [128, 2], P(('parts', 'expert')), parts along dimension 0, may hold values from 0 to 7, as said below
- gates: float32 [128, 2], P(('parts', 'expert')), parts along dimension 0, may hold values from 0.1 to 1
- inner_weights: bfloat16 [8, 2, 8192, 2048], P('expert', None, 'tensor'), may hold values from -0.125 to 0.125
- outer_weights: bfloat16 [8, 8192, 2048], P('expert', 'tensor'), may hold values from -0.09375 to 0.09375
Outputs:
- mamba_out: bfloat16 [128, 4096], P(('parts', 'expert'), 'tensor'), parts along dimension 0
- next_state: float32 [128, 16, 4096], P(('parts', 'expert'), None, 'tensor'), parts along dimension 0
- attention_out: bfloat16 [128, 4096], P(('parts', 'expert'), 'tensor'), parts along dimension 0
- expert_out: bfloat16 [128, 2048], P(('parts', 'expert'), 'tensor'), parts along dimension 0
There are 2 independent parts, one for each index of `parts`. A program takes and returns all parts, laid end to end along the dimension named above; an argument that names none is the same for every part. Nothing has to cross between parts.
Inputs may be any that keep to these rules, and one draw needn't show every extreme that they name: `routes`: A row names 2 different experts. Within the 16 rows of one device (aligned blocks) no expert is named more than 8 times, and one expert, the same in all blocks, is named exactly 8 times in every block. slots[t, k] numbers the rows of t's block that name expert routes[t, k]: within a block the slots of one expert are distinct. `lengths`: every block of 16 sequences holds one of length 128.
All inputs are finite; a program needn't handle non-finite values.
Results may differ from a plain program's by a relative error of at most 0.006.
Values may be sent and summed in bfloat16 or wider, within the bound.
No kernel may reach another device: no remote copies, remote signals or barrier semaphores. Data moves between devices by JAX's collectives and lax.ppermute only.
A program may use at most 128 MiB of HBM per device.

v0:
```python
import jax
import jax.numpy as jnp
from jax import lax
from jax.sharding import PartitionSpec as P

EXPERTS = 8


def mamba_step(
    mamba_input,
    mamba_gate,
    conv_state,
    scan_state,
    conv_weight,
    conv_bias,
    state_proj,
    step_proj,
    step_bias,
    decay_log,
    skip_gain,
):
    window = jnp.concatenate(
        [conv_state.astype(jnp.float32), mamba_input.astype(jnp.float32)[:, None, :]], axis=1
    )
    conv_act = jax.nn.silu(jnp.sum(window * conv_weight[None], axis=1) + conv_bias)
    local_mix = lax.dot_general(
        conv_act.astype(jnp.bfloat16),
        state_proj,
        (((1,), (1,)), ((), ())),
        preferred_element_type=jnp.float32,
    )
    mixing = lax.psum(local_mix, "tensor")
    low_rank = step_proj.shape[0]
    states = decay_log.shape[0]
    step_size = jax.nn.softplus(
        jnp.dot(
            mixing[:, :low_rank].astype(jnp.bfloat16), step_proj, preferred_element_type=jnp.float32
        )
        + step_bias
    )
    in_coef = mixing[:, low_rank : low_rank + states]
    out_coef = mixing[:, low_rank + states :]
    decay_rate = jnp.exp(-step_size[:, None, :] * jnp.exp(decay_log)[None])
    next_state = decay_rate * scan_state + (step_size * conv_act)[:, None, :] * in_coef[:, :, None]
    mixed_out = jnp.sum(next_state * out_coef[:, :, None], axis=1) + skip_gain * conv_act
    return (
        (mixed_out * jax.nn.silu(mamba_gate.astype(jnp.float32))).astype(jnp.bfloat16),
        next_state,
    )


def attend(queries, new_entry, past_entries, lengths):
    seq_count, head_count, head_size = queries.shape
    groups = past_entries.shape[1]
    per_group = head_count // groups
    positions = past_entries.shape[2]
    scaling = head_size ** (-0.5)
    query_rows = queries.reshape(seq_count, groups, per_group, head_size)
    scores = (
        jnp.einsum(
            "sgqd,sgld->sgql",
            query_rows,
            past_entries[..., :head_size],
            preferred_element_type=jnp.float32,
        )
        * scaling
    )
    own_score = (
        jnp.einsum(
            "sgqd,sgd->sgq",
            query_rows,
            new_entry[..., :head_size],
            preferred_element_type=jnp.float32,
        )
        * scaling
    )
    live_mask = jnp.arange(positions, dtype=jnp.int32)[None, :] < lengths[:, None]
    scores = jnp.where(live_mask[:, None, None, :], scores, -jnp.inf)
    highest = jnp.maximum(jnp.max(scores, axis=3), own_score)
    weights = jnp.exp(scores - highest[..., None])
    own_weight = jnp.exp(own_score - highest)
    denominator = jnp.sum(weights, axis=3) + own_weight
    weights_low = (weights / denominator[..., None]).astype(jnp.bfloat16)
    own_low = (own_weight / denominator).astype(jnp.bfloat16)
    mixed_out = jnp.einsum(
        "sgql,sgld->sgqd",
        weights_low,
        past_entries[..., head_size:],
        preferred_element_type=jnp.float32,
    )
    mixed_out = (
        mixed_out
        + own_low.astype(jnp.float32)[..., None]
        * new_entry[..., head_size:].astype(jnp.float32)[:, :, None, :]
    )
    return mixed_out.reshape(seq_count, head_count * head_size).astype(jnp.bfloat16)


def shards(
    mamba_input,
    mamba_gate,
    conv_state,
    scan_state,
    conv_weight,
    conv_bias,
    state_proj,
    step_proj,
    step_bias,
    decay_log,
    skip_gain,
    queries,
    new_entry,
    past_entries,
    lengths,
    expert_input,
    routes,
    slots,
    gates,
    inner_weights,
    outer_weights,
):
    peer_count = lax.axis_size("expert")
    token_count = routes.shape[0]
    capacity = max(2, 4 * token_count // EXPERTS)
    replicas = max(1, peer_count // EXPERTS)
    local_rows = inner_weights.shape[0]
    total_rows = peer_count * local_rows
    row_expert = jnp.arange(total_rows, dtype=jnp.int32) // replicas
    slot_index = jnp.arange(capacity, dtype=jnp.int32)
    matches = (row_expert[:, None, None, None] == routes[None, None, :, :]) & (
        slot_index[None, :, None, None] == slots[None, None, :, :]
    )
    send_table = jnp.any(matches, axis=3).astype(jnp.bfloat16)
    weight_table = jnp.sum(jnp.where(matches, gates[None, None, :, :], 0.0), axis=3)
    features = lax.all_gather(expert_input, "tensor", axis=1, tiled=True)
    outgoing = jnp.einsum(
        "rcb,bd->rcd", send_table, features, preferred_element_type=jnp.float32
    ).astype(jnp.bfloat16)
    outgoing = outgoing.reshape(peer_count, local_rows, capacity, features.shape[1])
    gate_rows = inner_weights[:, 0]
    up_rows = inner_weights[:, 1]
    received = lax.all_to_all(outgoing, "expert", split_axis=0, concat_axis=0, tiled=True)
    gate_val = jnp.einsum("nlcd,lfd->nlcf", received, gate_rows, preferred_element_type=jnp.float32)
    up_val = jnp.einsum("nlcd,lfd->nlcf", received, up_rows, preferred_element_type=jnp.float32)
    hidden = (jax.nn.silu(gate_val) * up_val).astype(jnp.bfloat16)
    partial_value = jnp.einsum(
        "nlcf,lfd->nlcd", hidden, outer_weights, preferred_element_type=jnp.float32
    )
    share_sum = lax.psum_scatter(partial_value, "tensor", scatter_dimension=3, tiled=True)
    returned = lax.all_to_all(share_sum, "expert", split_axis=0, concat_axis=0, tiled=True)
    returned = returned.reshape(total_rows, capacity, returned.shape[3])
    merged = jnp.einsum("rcb,rcd->bd", weight_table, returned, precision=lax.Precision.HIGHEST)
    expert_out = merged.astype(jnp.bfloat16)
    mamba_out, next_state = mamba_step(
        mamba_input,
        mamba_gate,
        conv_state,
        scan_state,
        conv_weight,
        conv_bias,
        state_proj,
        step_proj,
        step_bias,
        decay_log,
        skip_gain,
    )
    attention_out = attend(queries, new_entry, past_entries, lengths)
    return (mamba_out, next_state, attention_out, expert_out)


def solution(mesh):
    return jax.shard_map(
        shards,
        mesh=mesh,
        in_specs=(
            P(("parts", "expert"), "tensor"),
            P(("parts", "expert"), "tensor"),
            P(("parts", "expert"), None, "tensor"),
            P(("parts", "expert"), None, "tensor"),
            P(None, "tensor"),
            P("tensor"),
            P(None, "tensor"),
            P(None, "tensor"),
            P("tensor"),
            P(None, "tensor"),
            P("tensor"),
            P(("parts", "expert"), "tensor", None),
            P(("parts", "expert"), "tensor", None),
            P(("parts", "expert"), "tensor", None, None),
            P(("parts", "expert")),
            P(("parts", "expert"), "tensor"),
            P(("parts", "expert"), None),
            P(("parts", "expert"), None),
            P(("parts", "expert"), None),
            P("expert", None, "tensor", None),
            P("expert", "tensor", None),
        ),
        out_specs=(
            P(("parts", "expert"), "tensor"),
            P(("parts", "expert"), None, "tensor"),
            P(("parts", "expert"), "tensor"),
            P(("parts", "expert"), "tensor"),
        ),
        check_vma=False,
    )
```

profile of v0, /device:TPU:0, one launch (start us, length us, event | category | flops | bytes accessed | tf_op | source)
XLA Modules:
  0.0 100.1 jit_solution(2538967461487775858)
XLA Ops:
  7.2 0.0 copy-start
  7.2 0.7 iota_compare_fusion
  7.9 0.7 iota_compare_fusion.1
  8.6 6.4 %all_gather.3 = bf16[16,2048]{1,0:T(8,128)(2,1)S(1)} all-gather(bf16[16,512]{1,0:T(8,128)(2,1)} %param.36), channel_id=1, replica_groups=mesh['parts'=2,'expert'=4,'tensor'=4] {'tensor'}, dimensions={1}, use_global_device_ids=true | all-gather | bytes 81920 | tf_op jit(solution)/shard_map/all_gather | solution.py:135
  15.1 0.9 convolution_convert_fusion
  16.0 5.3 %all-to-all-start = ((bf16[4,2,8,2048]{3,2,1,0:T(8,128)(2,1)}), bf16[4,2,8,2048]{3,2,1,0:T(8,128)(2,1)S(1)}, u32[]{:S(2)}, u32[]{:S(2)}) async-start(bf16[4,2,8,2048]{3,2,1,0:T(8,128)(2,1)} %bitcast.6), calls=%async_computation | async-start | bytes 524288 | tf_op jit(solution)/shard_map/all_to_all | solution.py:142
  21.3 0.0 reduce-scatter.2.cloned.1.call-start
  21.3 0.7 iota_compare_fusion.2
  22.0 0.7 slice_bitcast_fusion
  22.8 0.9 fusion.42
  23.7 2.0 %fusion.49 = (f32[16,2,4]{2,1,0:T(2,128)S(1)}, f32[16,2,4,128]{3,2,1,0:T(4,128)S(1)}) fusion(bf16[16,2,4,128]{3,2,1,0:T(4,128)(2,1)} %bitcast.69, bf16[16,2,128,256]{3,2,1,0:T(8,128)(2,1)} %param.34, pred[16,128]{1,0:T(8,128)(4,1)S(1)} %iota_compare_fusion.2), kind=kOutput, calls=%fused_computation.64 | convolution fusion | flops 4243328 | bytes 1149440 | tf_op jit(solution)/shard_map/sgqd,sgld->sgql/dot_general | solution.py:60
  25.7 0.2 fusion.37
  26.0 0.9 exp.29
  26.8 1.7 %fusion.24 = bf16[16,2,4,128]{3,2,1,0:T(4,128)(2,1)S(1)} fusion(bf16[16,2,128,256]{3,2,1,0:T(8,128)(2,1)} %param.34, f32[16,2,4,128]{3,2,1,0:T(4,128)S(1)} %get-tuple-element.15, f32[16,2,128]{2,1,0:T(2,128)S(1)} %get-tuple-element.13, f32[16,2,4]{2,1,0:T(2,128)S(1)} %get-tuple-element.9, f32[16,2,4]{2,1,0:T(2,128)S(1)} %get-tuple-element.8, ...), kind=kOutput, calls=%fused_computation.18 | convolution fusion | flops 4292608 | bytes 1164800 | tf_op jit(solution)/shard_map/sgql,sgld->sgqd/dot_general | solution.py:85
  28.5 0.6 convert_element_type.48
  29.1 0.9 multiply_reduce_fusion.1
  30.1 0.6 all-to-all-done
  30.7 8.4 %fusion.11 = f32[4,2,8,2048]{3,2,0,1:T(8,128)S(1)} fusion(bf16[2,2,2048,2048]{3,2,1,0:T(8,128)(2,1)} %param.40, bf16[4,2,8,2048]{3,2,1,0:T(8,128)(2,1)S(1)} %all-to-all-done), kind=kOutput, calls=%fused_computation.9 | convolution fusion | flops 536870912 | bytes 17563648 | tf_op jit(solution)/shard_map/nlcd,lfd->nlcf/dot_general | solution.py:143
  39.1 8.7 %fusion.20 = bf16[4,2,8,2048]{3,2,0,1:T(8,128)(2,1)S(1)} fusion(bf16[2,2,2048,2048]{3,2,1,0:T(8,128)(2,1)} %param.40, f32[4,2,8,2048]{3,2,0,1:T(8,128)S(1)} %fusion.11, bf16[4,2,8,2048]{3,2,1,0:T(8,128)(2,1)S(1)} %all-to-all-done), kind=kOutput, calls=%fused_computation.13 | convolution fusion | flops 537657344 | bytes 17825792 | tf_op jit(solution)/shard_map/nlcd,lfd->nlcf/dot_general | solution.py:144
  47.8 0.0 copy-start.3
  47.8 0.0 copy-start.5
  47.8 0.0 copy-start.6
  47.8 0.0 copy-start.7
  47.9 0.0 copy-start.1
  47.9 0.0 copy-start.2
  47.9 0.0 copy-start.4
  47.9 9.5 %fusion.8 = f32[4,2,8,2048]{3,2,0,1:T(8,128)} fusion(bf16[4,2,8,2048]{3,2,0,1:T(8,128)(2,1)S(1)} %fusion.20, bf16[2,2048,2048]{2,1,0:T(8,128)(2,1)} %param.41), kind=kOutput, calls=%fused_computation.8 | convolution fusion | flops 536870912 | bytes 17563648 | tf_op jit(solution)/shard_map/nlcf,lfd->nlcd/dot_general | solution.py:146
  57.4 0.0 reduce-scatter.2.cloned.1.call-update
  57.5 0.0 copy-done
  57.5 0.0 copy-done.3
  57.5 0.3 fusion.40
  57.7 10.7 %psum.7 = f32[16,288]{1,0:T(8,128)S(1)} all-reduce(f32[16,288]{1,0:T(8,128)S(1)} %fusion.40), channel_id=1, replica_groups=mesh['parts'=2,'expert'=4,'tensor'=4] {'tensor'}, use_global_device_ids=true, to_apply=%region_1.2 | all-reduce | flops 4608 | bytes 36864 | tf_op jit(solution)/shard_map/psum | solution.py:32
  68.4 0.0 copy-done.5
  68.5 0.1 fusion.48
  68.6 0.0 copy-done.6
  68.6 0.0 copy-done.7
  68.6 0.2 fusion.47
  68.8 0.0 copy-done.1
  68.8 1.5 %multiply_reduce_fusion = (f32[16,1024]{1,0:T(8,128)S(1)}, f32[16,16,1024]{2,1,0:T(8,128)}) fusion(f32[16,16]{1,0:T(8,128)S(1)} %get-tuple-element.11, f32[16,16]{1,0:T(8,128)S(1)} %get-tuple-element.10, f32[16,1024]{1,0:T(8,128)S(1)} %get-tuple-element.7, f32[16,16,1024]{2,1,0:T(8,128)S(1)} %copy-done.1, f32[16,1024]{1,0:T(8,128)S(1)} %exp.29, ...), kind=kLoop, calls=%fused_computation.23 | loop fusion | flops 1556480 | bytes 2361344 | tf_op jit(solution)/shard_map/reduce_sum | solution.py:45
  70.3 9.9 %reduce-scatter.2.cloned.1.call-done = f32[4,2,8,512]{3,2,0,1:T(8,128)} async-done(((f32[4,2,8,2048]{3,2,0,1:T(8,128)}), f32[4,2,8,512]{3,2,0,1:T(8,128)}) %reduce-scatter.2.cloned.1.call-update) | async-done | bytes 131088 | tf_op jit(solution)/shard_map/reduce_scatter | solution.py:149
  80.2 1.5 %copy.50 = f32[4,2,8,512]{3,2,1,0:T(8,128)} copy(f32[4,2,8,512]{3,2,0,1:T(8,128)} %reduce-scatter.2.cloned.1.call-done) | data formatting | bytes 262144 | tf_op jit(solution)/shard_map/reduce_scatter | solution.py:149
  81.7 4.6 %all-to-all-start.1 = ((f32[4,2,8,512]{3,2,1,0:T(8,128)}), f32[4,2,8,512]{3,2,1,0:T(8,128)S(1)}, u32[]{:S(2)}, u32[]{:S(2)}) async-start(f32[4,2,8,512]{3,2,1,0:T(8,128)} %copy.50), calls=%async_computation.2 | async-start | bytes 262144 | tf_op jit(solution)/shard_map/all_to_all | solution.py:150
  86.3 0.0 copy-done.2
  86.3 0.0 copy-done.4
  86.3 0.7 fusion.36
  87.0 5.4 %all-to-all-done.1 = f32[4,2,8,512]{3,2,1,0:T(8,128)S(1)} async-done(((f32[4,2,8,512]{3,2,1,0:T(8,128)}), f32[4,2,8,512]{3,2,1,0:T(8,128)S(1)}, u32[]{:S(2)}, u32[]{:S(2)}) %all-to-all-start.1) | async-done | bytes 131104 | tf_op jit(solution)/shard_map/all_to_all | solution.py:150
  92.4 0.8 fusion.25
  (4 shorter events, 0.1 us)
Async XLA Ops:
  7.2 50.3 %copy-start = (bf16[288,1024]{1,0:T(8,128)(2,1)S(1)}, bf16[288,1024]{1,0:T(8,128)(2,1)}, u32[]{:S(2)}) copy-start(bf16[288,1024]{1,0:T(8,128)(2,1)} %param.27) | copy-start | bytes 1769476
  16.0 14.7 %all-to-all-start = ((bf16[4,2,8,2048]{3,2,1,0:T(8,128)(2,1)}), bf16[4,2,8,2048]{3,2,1,0:T(8,128)(2,1)S(1)}, u32[]{:S(2)}, u32[]{:S(2)}) async-start(bf16[4,2,8,2048]{3,2,1,0:T(8,128)(2,1)} %bitcast.6), calls=%async_computation | async-start | bytes 524288 | tf_op jit(solution)/shard_map/all_to_all | solution.py:142
  21.3 58.9 %reduce-scatter.2.cloned.1.call-start = ((), (), s32[]{:S(2)}) async-start(), calls=%async_computation.3 | async-start | bytes 655360 | tf_op jit(solution)/shard_map/reduce_scatter | solution.py:149
  47.8 9.7 %copy-start.3 = (f32[1024]{0:T(1024)S(1)}, f32[1024]{0:T(1024)}, u32[]{:S(2)}) copy-start(f32[1024]{0:T(1024)} %param.26) | copy-start | bytes 12292
  47.8 20.6 %copy-start.5 = (f32[16,2]{0,1:T(2,128)S(1)}, f32[16,2]{0,1:T(2,128)}, u32[]{:S(2)}) copy-start(f32[16,2]{0,1:T(2,128)} %param.39) | copy-start | bytes 388
  47.8 20.7 %copy-start.6 = (bf16[256,1024]{1,0:T(8,128)(2,1)S(1)}, bf16[256,1024]{1,0:T(8,128)(2,1)}, u32[]{:S(2)}) copy-start(bf16[256,1024]{1,0:T(8,128)(2,1)} %param.28) | copy-start | bytes 1572868
  47.8 20.7 %copy-start.7 = (f32[1024]{0:T(1024)S(1)}, f32[1024]{0:T(1024)}, u32[]{:S(2)}) copy-start(f32[1024]{0:T(1024)} %param.29) | copy-start | bytes 12292
  47.9 20.9 %copy-start.1 = (f32[16,16,1024]{2,1,0:T(8,128)S(1)}, f32[16,16,1024]{2,1,0:T(8,128)}, u32[]{:S(2)}) copy-start(f32[16,16,1024]{2,1,0:T(8,128)} %param.24) | copy-start | bytes 3145732
  47.9 38.5 %copy-start.2 = (bf16[16,1024]{1,0:T(8,128)(2,1)S(1)}, bf16[16,1024]{1,0:T(8,128)(2,1)}, u32[]{:S(2)}) copy-start(bf16[16,1024]{1,0:T(8,128)(2,1)} %param.22) | copy-start | bytes 98308
  47.9 38.5 %copy-start.4 = (f32[1024]{0:T(1024)S(1)}, f32[1024]{0:T(1024)}, u32[]{:S(2)}) copy-start(f32[1024]{0:T(1024)} %param.31) | copy-start | bytes 12292
  81.7 10.7 %all-to-all-start.1 = ((f32[4,2,8,512]{3,2,1,0:T(8,128)}), f32[4,2,8,512]{3,2,1,0:T(8,128)S(1)}, u32[]{:S(2)}, u32[]{:S(2)}) async-start(f32[4,2,8,512]{3,2,1,0:T(8,128)} %copy.50), calls=%async_computation.2 | async-start | bytes 262144 | tf_op jit(solution)/shard_map/all_to_all | solution.py:150
Sparse Core Ops, SparseCore 0:
  57.6 22.5 reduce-scatter.1
where the time goes:
time: 101 us; the launch traced here: 100 us
  matrix products  33.4 us (33%)
  blocking collectives  17.1 us (17%)
  waiting for transfers between devices  16 us (16%)
  between operations  14.2 us (14%)
  starting transfers between devices  9.95 us (10%)
  other arithmetic  6.26 us (6%)
  local copies, waits for them, and re-layouts  3.17 us (3%)
    psum x1, blocking collectives, mamba_step(): mixing = lax.psum(local_mix, 'tensor')  10.7 us
    reduce_scatter x1, waiting for transfers between devices, shards(): lax.psum_scatter(partial_value, 'tensor', scatter_dimension=3, tiled=True)  9.91 us
    dot_general x1, matrix products, shards(): jnp.einsum('nlcf,lfd->nlcd', hidden, outer_weights, preferred_element_typ...  9.55 us
    dot_general x1, matrix products, shards(): jnp.einsum('nlcd,lfd->nlcf', received, up_rows, preferred_element_type=jn...  8.68 us
    dot_general x1, matrix products, shards(): jnp.einsum('nlcd,lfd->nlcf', received, gate_rows, preferred_element_type=...  8.42 us
    all_gather x1, blocking collectives, shards(): features = lax.all_gather(expert_input, 'tensor', axis=1, tiled=True)  6.44 us
    all_to_all x1, waiting for transfers between devices, shards(): lax.all_to_all(share_sum, 'expert', split_axis=0, concat_axis=0, tiled=True)  5.4 us
    all_to_all x1, starting transfers between devices, shards(): lax.all_to_all(outgoing, 'expert', split_axis=0, concat_axis=0, tiled=True)  5.34 us
  transfers between devices with their start and end apart: 3, of which 3 were waited for; matrix products, arithmetic and copies ran while one was open for 11% of the time, Pallas kernels for 0%

commit v1 on v0

v1 whole, which is shorter than its diff:
```python
import functools

import jax
import jax.numpy as jnp
from jax import lax
from jax.experimental import pallas as pl
from jax.experimental.pallas import tpu as pltpu
from jax.sharding import PartitionSpec as P

EXPERTS = 8
LANES = 128
F32 = jnp.float32
BF16 = jnp.bfloat16

HBM_SPEC = pl.BlockSpec(memory_space=pl.ANY)
VMEM_SPEC = pl.BlockSpec(memory_space=pltpu.VMEM)


def silu(v):
    return v / (1.0 + jnp.exp(-v))


def split_bf16(v):
    high = v.astype(BF16)
    return high, (v - high.astype(F32)).astype(BF16)


def partner(index, step, count):
    if count & (count - 1) == 0:
        return index ^ step
    return (index + step) % count


def returner(index, step, count):
    if count & (count - 1) == 0:
        return index ^ step
    return (index - step) % count


def exchange(blocks, axis, back=False):
    count = lax.axis_size(axis)
    rule = returner if back else partner
    out = {0: blocks[0]}
    for step in range(count - 1, 0, -1):
        pairs = [(i, rule(i, step, count)) for i in range(count)]
        out[step] = lax.ppermute(blocks[step], axis, pairs)
    return [out[step] for step in range(count)]


def front_kernel(
    width,
    past_hbm, queries_hbm, entry_hbm, lengths_ref, state_hbm, input_hbm,
    taps_hbm, bias_hbm, proj_hbm,
    attn_hbm, act_ref, mix_ref,
    past, queries, entry, state, inputs, taps, bias, proj, heads, attn, sems,
):
    seqs, head_count, size = queries.shape
    groups = past.shape[1]
    per_group = head_count // groups
    positions = past.shape[2]
    parts = 4 if seqs % 4 == 0 else 1
    part = seqs // parts
    small = [
        pltpu.make_async_copy(src, dst, sems.at[n])
        for n, (src, dst) in enumerate((
            (queries_hbm, queries), (entry_hbm, entry), (state_hbm, state),
            (input_hbm, inputs), (taps_hbm, taps), (bias_hbm, bias), (proj_hbm, proj),
        ))
    ]
    large = [
        pltpu.make_async_copy(
            past_hbm.at[pl.ds(n * part, part)], past.at[pl.ds(n * part, part)],
            sems.at[len(small) + n],
        )
        for n in range(parts)
    ]
    for copy in small + large:
        copy.start()
    for copy in small:
        copy.wait()

    total = bias[...]
    for k in range(taps.shape[0] - 1):
        total = total + state[:, k, :].astype(F32) * taps[k : k + 1, :]
    total = total + inputs[...].astype(F32) * taps[taps.shape[0] - 1 :, :]
    act = silu(total)
    act_ref[...] = act
    mix = lax.dot_general(
        act.astype(BF16), proj[...], (((1,), (1,)), ((), ())), preferred_element_type=F32
    )
    outputs = mix.shape[1]
    spans = -(-outputs // width)
    row = 0
    for piece in split_bf16(mix):
        for span in range(spans):
            cut = piece[:, span * width : min(outputs, (span + 1) * width)]
            if cut.shape[1] < width:
                cut = jnp.concatenate(
                    [cut.astype(F32), jnp.zeros((seqs, width - cut.shape[1]), F32)], axis=1
                ).astype(BF16)
            mix_ref[row : row + seqs, :] = cut
            row += seqs

    scaling = size ** (-0.5)
    rows = lax.broadcasted_iota(jnp.int32, (head_count, positions), 0) // per_group
    owner = lax.broadcasted_iota(jnp.int32, (head_count, size), 0) // per_group
    position = lax.broadcasted_iota(jnp.int32, (head_count, positions), 1)

    def pick(values, index):
        result = values[0]
        for g in range(1, groups):
            result = jnp.where(index == g, values[g], result)
        return result

    for n in range(parts):
        large[n].wait()
        for s in range(n * part, (n + 1) * part):
            query = queries[s]
            scores = pick(
                [
                    lax.dot_general(
                        query, past[s, g, :, :size], (((1,), (1,)), ((), ())),
                        preferred_element_type=F32,
                    )
                    for g in range(groups)
                ],
                rows,
            ) * scaling
            keys = pick(
                [
                    jnp.broadcast_to(entry[s, g : g + 1, :size].astype(F32), (head_count, size))
                    for g in range(groups)
                ],
                owner,
            )
            own = jnp.sum(query.astype(F32) * keys, axis=1, keepdims=True) * scaling
            scores = jnp.where(position < lengths_ref[s], scores, -jnp.inf)
            highest = jnp.maximum(jnp.max(scores, axis=1, keepdims=True), own)
            weights = jnp.exp(scores - highest)
            own_weight = jnp.exp(own - highest)
            denominator = jnp.sum(weights, axis=1, keepdims=True) + own_weight
            low = (weights / denominator).astype(BF16)
            own_low = (own_weight / denominator).astype(BF16).astype(F32)
            mixed = pick(
                [
                    lax.dot_general(
                        low, past[s, g, :, size:], (((1,), (0,)), ((), ())),
                        preferred_element_type=F32,
                    )
                    for g in range(groups)
                ],
                owner,
            )
            values = pick(
                [
                    jnp.broadcast_to(entry[s, g : g + 1, size:].astype(F32), (head_count, size))
                    for g in range(groups)
                ],
                owner,
            )
            heads[s] = mixed + own_low * values
    for h in range(head_count):
        attn[:, h * size : (h + 1) * size] = heads[:, h, :].astype(BF16)
    store = pltpu.make_async_copy(attn, attn_hbm, sems.at[len(small) + parts])
    store.start()
    store.wait()


def front(
    queries, new_entry, past_entries, lengths, conv_state, mamba_input,
    conv_weight, conv_bias, state_proj, width,
):
    seqs, head_count, size = queries.shape
    channels = mamba_input.shape[1]
    outputs = state_proj.shape[0]
    spans = -(-outputs // width)
    vmem = lambda a: pltpu.VMEM(a.shape, a.dtype)
    bias = conv_bias.reshape(1, channels)
    return pl.pallas_call(
        functools.partial(front_kernel, width),
        out_shape=(
            jax.ShapeDtypeStruct((seqs, head_count * size), BF16),
            jax.ShapeDtypeStruct((seqs, channels), F32),
            jax.ShapeDtypeStruct((2 * spans * seqs, width), BF16),
        ),
        in_specs=[
            HBM_SPEC, HBM_SPEC, HBM_SPEC, pl.BlockSpec(memory_space=pltpu.SMEM),
            HBM_SPEC, HBM_SPEC, HBM_SPEC, HBM_SPEC, HBM_SPEC,
        ],
        out_specs=(HBM_SPEC, VMEM_SPEC, VMEM_SPEC),
        scratch_shapes=[
            vmem(past_entries), vmem(queries), vmem(new_entry), vmem(conv_state),
            vmem(mamba_input), vmem(conv_weight), vmem(bias), vmem(state_proj),
            pltpu.VMEM((seqs, head_count, size), F32),
            pltpu.VMEM((seqs, head_count * size), BF16),
            pltpu.SemaphoreType.DMA((16,)),
        ],
        cost_estimate=pl.CostEstimate(
            flops=6 * 10**9, bytes_accessed=4 * 10**6, transcendentals=0
        ),
        name="front",
    )(
        past_entries, queries, new_entry, lengths, conv_state, mamba_input,
        conv_weight, bias, state_proj,
    )


def expert_kernel(
    chunk, count, axes,
    gathered, *rest,
):
    peers, ways = axes
    tables = rest[:peers]
    inner_hbm, outer_hbm = rest[peers : peers + 2]
    outs = rest[peers + 2 : peers + 2 + ways]
    inner, outer, features, total, sems = rest[peers + 2 + ways :]
    experts, _, hidden_units, _ = inner.shape
    tokens = features.shape[0]
    width = gathered.shape[2]
    copies = []
    for e in range(experts):
        for c in range(count):
            span = pl.ds(c * chunk, chunk)
            group = []
            for n, (src, dst) in enumerate((
                (inner_hbm.at[e, 0, span], inner.at[e, 0, span]),
                (inner_hbm.at[e, 1, span], inner.at[e, 1, span]),
                (outer_hbm.at[e, span], outer.at[e, span]),
            )):
                group.append(pltpu.make_async_copy(src, dst, sems.at[e * count + c, n]))
            copies.append(group)
    for group in copies:
        for copy in group:
            copy.start()
    for t in range(ways):
        features[:, t * width : (t + 1) * width] = gathered[t, :tokens, :]
    table = jnp.concatenate([ref[:, width:].astype(F32) for ref in tables], axis=0)
    lane = lax.broadcasted_iota(jnp.int32, table.shape, 1)
    replicas = max(1, peers // EXPERTS)
    first = lax.axis_index("expert") * experts
    for e in range(experts):
        name = (first + e) // replicas
        chosen = (lane == name) | (lane == name + EXPERTS)
        gain = jnp.sum(jnp.where(chosen, table, 0.0), axis=1, keepdims=True)
        for c in range(count):
            group = copies[e * count + c]
            span = slice(c * chunk, (c + 1) * chunk)
            group[0].wait()
            gate = lax.dot_general(
                features[...], inner[e, 0, span], (((1,), (1,)), ((), ())),
                preferred_element_type=F32,
            )
            group[1].wait()
            up = lax.dot_general(
                features[...], inner[e, 1, span], (((1,), (1,)), ((), ())),
                preferred_element_type=F32,
            )
            hidden = (silu(gate) * up).astype(BF16)
            group[2].wait()
            value = gain * jnp.dot(hidden, outer[e, span], preferred_element_type=F32)
            if e == 0 and c == 0:
                total[...] = value
            else:
                total[...] += value
    me = lax.axis_index("tensor")
    for step in range(ways):
        start = pl.multiple_of(partner(me, step, ways) * width, LANES)
        outs[step][...] = total[:, pl.ds(start, width)].astype(outs[step].dtype)


def run_experts(gathered, packed, inner_weights, outer_weights):
    ways, rows, width = gathered.shape
    peers = len(packed)
    tokens = sum(p.shape[0] for p in packed)
    experts, _, hidden_units, features = inner_weights.shape
    chunk = min(512, hidden_units)
    count = hidden_units // chunk
    work = 6 * tokens * experts * hidden_units * features
    moved = 2 * (inner_weights.size + outer_weights.size)
    return pl.pallas_call(
        functools.partial(expert_kernel, chunk, count, (peers, ways)),
        out_shape=tuple(
            jax.ShapeDtypeStruct((tokens, width), F32 if step == 0 else BF16)
            for step in range(ways)
        ),
        in_specs=[VMEM_SPEC] * (1 + peers) + [HBM_SPEC, HBM_SPEC],
        out_specs=(VMEM_SPEC,) * ways,
        scratch_shapes=[
            pltpu.VMEM(inner_weights.shape, BF16),
            pltpu.VMEM(outer_weights.shape, BF16),
            pltpu.VMEM((tokens, features), BF16),
            pltpu.VMEM((tokens, features), F32),
            pltpu.SemaphoreType.DMA((experts * count, 3)),
        ],
        compiler_params=pltpu.CompilerParams(vmem_limit_bytes=56 * 2**20),
        cost_estimate=pl.CostEstimate(
            flops=work, bytes_accessed=moved, transcendentals=0
        ),
        name="experts",
    )(gathered, *packed, inner_weights, outer_weights)


def state_kernel(
    tokens, seqs, low_rank,
    gathered, act, gate, scan, step_proj, step_bias, decay, skip,
    out, next_state,
    square,
):
    ways, rows, width = gathered.shape
    states = decay.shape[0]
    spans = (rows - tokens) // (2 * seqs)
    pieces = []
    for span in range(spans):
        piece = None
        for t in range(ways):
            for half in range(2):
                row = tokens + (half * spans + span) * seqs
                part = gathered[t, row : row + seqs, :].astype(F32)
                piece = part if piece is None else piece + part
        pieces.append(piece)
    mixing = pieces[0] if spans == 1 else jnp.concatenate(pieces, axis=1)
    square[...] = jnp.zeros_like(square)
    square[:seqs, :] = mixing[:, low_rank : low_rank + LANES]
    columns = square[...].T
    step = (
        jnp.dot(mixing[:, :low_rank].astype(BF16), step_proj[...], preferred_element_type=F32)
        + step_bias[...]
    )
    step_size = jnp.maximum(step, 0.0) + jnp.log1p(jnp.exp(-jnp.abs(step)))
    rates = jnp.exp(decay[...])
    drive = step_size * act[...]
    results = []
    for s in range(seqs):
        in_coef = columns[:states, s : s + 1]
        out_coef = columns[states : 2 * states, s : s + 1]
        new = jnp.exp(-step_size[s : s + 1, :] * rates) * scan[s] + drive[s : s + 1, :] * in_coef
        next_state[s] = new
        results.append(jnp.sum(new * out_coef, axis=0, keepdims=True))
    mixed = jnp.concatenate(results, axis=0) + skip[...] * act[...]
    out[...] = (mixed * silu(gate[...].astype(F32))).astype(BF16)


def update_state(
    gathered, tokens, act, mamba_gate, scan_state, step_proj, step_bias, decay_log, skip_gain
):
    seqs, states, channels = scan_state.shape
    low_rank = step_proj.shape[0]
    block = min(512, channels)
    lane_block = lambda rows: pl.BlockSpec((rows, block), lambda c: (0, c))
    state_block = pl.BlockSpec((seqs, states, block), lambda c: (0, 0, c))
    return pl.pallas_call(
        functools.partial(state_kernel, tokens, seqs, low_rank),
        grid=(channels // block,),
        out_shape=(
            jax.ShapeDtypeStruct((seqs, channels), BF16),
            jax.ShapeDtypeStruct(scan_state.shape, F32),
        ),
        in_specs=[
            pl.BlockSpec(gathered.shape, lambda c: (0, 0, 0)),
            lane_block(seqs), lane_block(seqs), state_block,
            lane_block(low_rank), lane_block(1), lane_block(states), lane_block(1),
        ],
        out_specs=(lane_block(seqs), state_block),
        scratch_shapes=[pltpu.VMEM((LANES, LANES), F32)],
        cost_estimate=pl.CostEstimate(
            flops=3 * 10**9, bytes_accessed=3 * 10**6, transcendentals=0
        ),
        name="state",
    )(
        gathered, act, mamba_gate, scan_state, step_proj,
        step_bias.reshape(1, channels), decay_log, skip_gain.reshape(1, channels),
    )


def shards(
    mamba_input,
    mamba_gate,
    conv_state,
    scan_state,
    conv_weight,
    conv_bias,
    state_proj,
    step_proj,
    step_bias,
    decay_log,
    skip_gain,
    queries,
    new_entry,
    past_entries,
    lengths,
    expert_input,
    routes,
    slots,
    gates,
    inner_weights,
    outer_weights,
):
    del slots
    peers = lax.axis_size("expert")
    ways = lax.axis_size("tensor")
    seqs, width = expert_input.shape
    tokens = peers * seqs

    lane = lax.broadcasted_iota(jnp.int32, (seqs, LANES), 1)
    weight = jnp.zeros((seqs, LANES), F32)
    for k in range(routes.shape[1]):
        weight = weight + jnp.where(lane % EXPERTS == routes[:, k : k + 1], gates[:, k : k + 1], 0.0)
    high, low = split_bf16(weight)
    table = jnp.where(lane < EXPERTS, high, jnp.where(lane < 2 * EXPERTS, low, 0))
    packed = jnp.concatenate([expert_input, table.astype(BF16)], axis=1)
    packed = exchange([packed] * peers, "expert")

    attention_out, act, mix = front(
        queries, new_entry, past_entries, lengths, conv_state, mamba_input,
        conv_weight, conv_bias, state_proj, width,
    )
    mine = jnp.concatenate([p[:, :width] for p in packed] + [mix], axis=0)
    gathered = lax.all_gather(mine, "tensor", axis=0)
    partial = run_experts(gathered, packed, inner_weights, outer_weights)

    arrived = exchange(partial, "tensor")
    share = arrived[0]
    for part in arrived[1:]:
        share = share + part.astype(F32)
    mamba_out, next_state = update_state(
        gathered, tokens, act, mamba_gate, scan_state, step_proj, step_bias, decay_log, skip_gain
    )
    blocks = [share[n * seqs : (n + 1) * seqs] for n in range(peers)]
    blocks = [blocks[0]] + [block.astype(BF16) for block in blocks[1:]]
    returned = exchange(blocks, "expert", back=True)
    merged = returned[0]
    for part in returned[1:]:
        merged = merged + part.astype(F32)
    return (mamba_out, next_state, attention_out, merged.astype(BF16))


def solution(mesh):
    return jax.shard_map(
        shards,
        mesh=mesh,
        in_specs=(
            P(("parts", "expert"), "tensor"),
            P(("parts", "expert"), "tensor"),
            P(("parts", "expert"), None, "tensor"),
            P(("parts", "expert"), None, "tensor"),
            P(None, "tensor"),
            P("tensor"),
            P(None, "tensor"),
            P(None, "tensor"),
            P("tensor"),
            P(None, "tensor"),
            P("tensor"),
            P(("parts", "expert"), "tensor", None),
            P(("parts", "expert"), "tensor", None),
            P(("parts", "expert"), "tensor", None, None),
            P(("parts", "expert")),
            P(("parts", "expert"), "tensor"),
            P(("parts", "expert"), None),
            P(("parts", "expert"), None),
            P(("parts", "expert"), None),
            P("expert", None, "tensor", None),
            P("expert", "tensor", None),
        ),
        out_specs=(
            P(("parts", "expert"), "tensor"),
            P(("parts", "expert"), None, "tensor"),
            P(("parts", "expert"), "tensor"),
            P(("parts", "expert"), "tensor"),
        ),
        check_vma=False,
    )
```

time: 101 us -> 63.9 us (0.63)
  matrix products: 33.4 us -> 0 us
  Pallas kernels: 0 us -> 32.1 us
  between operations: 14.2 us -> 0.81 us
  waiting for transfers between devices: 16 us -> 5.29 us
  blocking collectives: 17.1 us -> 7.11 us
  other arithmetic: 6.26 us -> 2.37 us
  starting transfers between devices: 9.95 us -> 11.8 us
    dot_general x10 -> x0, matrix products: 33.4 us -> none  [the longest x1 9.55 us: shards(): jnp.einsum('nlcf,lfd->nlcd', hidden, outer_weights, preferred_element_typ...]
    pallas_call x0 -> x3, Pallas kernels: none -> 32.1 us  [the longest x1 19.6 us: run_experts(): pl.pallas_call(functools.partial(expert_kernel, chunk, count, (peers, way...]
    ppermute x0 -> x9, starting transfers between devices: none -> 11.8 us  [exchange(): out[step] = lax.ppermute(blocks[step], axis, pairs)]
    psum x1 -> x0, blocking collectives: 10.7 us -> none  [mamba_step(): mixing = lax.psum(local_mix, 'tensor')]
    all_to_all x2 -> x0, starting transfers between devices: 9.94 us -> none  [the longest x1 5.34 us: shards(): lax.all_to_all(outgoing, 'expert', split_axis=0, concat_axis=0, tiled=True)]
    reduce_scatter x1 -> x0, waiting for transfers between devices: 9.91 us -> none  [shards(): lax.psum_scatter(partial_value, 'tensor', scatter_dimension=3, tiled=True)]
    all_to_all x2 -> x0, waiting for transfers between devices: 6.02 us -> none  [the longest x1 5.4 us: shards(): lax.all_to_all(share_sum, 'expert', split_axis=0, concat_axis=0, tiled=True)]
    ppermute x0 -> x9, waiting for transfers between devices: none -> 5.29 us  [exchange(): out[step] = lax.ppermute(blocks[step], axis, pairs)]
  transfers between devices with their start and end apart: 3 -> 9, of which waited for: 3 -> 3; matrix products, arithmetic and copies ran while one was open for 11% -> 3% of each run, Pallas kernels for 0% -> 20%
where the time goes in v1:
time: 63.9 us; the launch traced here: 63.4 us
  Pallas kernels  32.1 us (50%)
  starting transfers between devices  11.8 us (18%)
  blocking collectives  7.11 us (11%)
  waiting for transfers between devices  5.29 us (8%)
  local copies, waits for them, and re-layouts  3.96 us (6%)
  other arithmetic  2.37 us (4%)
  between operations  0.81 us (1%)
    pallas_call x1, Pallas kernels, run_experts(): pl.pallas_call(functools.partial(expert_kernel, chunk, count, (peers, way...  19.6 us
    ppermute x9, starting transfers between devices, exchange(): out[step] = lax.ppermute(blocks[step], axis, pairs)  11.8 us
    pallas_call x1, Pallas kernels, front(): pl.pallas_call(functools.partial(front_kernel, width), out_shape=(jax.Sha...  9.33 us
    all_gather x1, blocking collectives, shards(): gathered = lax.all_gather(mine, 'tensor', axis=0)  7.11 us
    ppermute x9, waiting for transfers between devices, exchange(): out[step] = lax.ppermute(blocks[step], axis, pairs)  5.29 us
    pallas_call x1, Pallas kernels, update_state(): pl.pallas_call(functools.partial(state_kernel, tokens, seqs, low_rank), g...  3.11 us
    unnamed x15, local copies, waits for them, and re-layouts  1.67 us
  transfers between devices with their start and end apart: 9, of which 3 were waited for; matrix products, arithmetic and copies ran while one was open for 3% of the time, Pallas kernels for 20%

profile of v1, /device:TPU:0, one launch (start us, length us, event | category | flops | bytes accessed | tf_op | source)
XLA Modules:
  0.0 63.4 jit_solution(2566733888329784192)
XLA Ops:
  0.6 0.0 copy-start.4
  0.7 0.8 %slice_bitcast_fusion.3 = (s32[16]{0:T(128)S(1)}, s32[16]{0:T(128)S(1)}) fusion(s32[16,2]{0,1:T(2,128)} %param.37), kind=kLoop, calls=%fused_computation.23 | loop fusion | bytes 256 | tf_op jit(solution)/shard_map/eq | solution.py:407
  1.4 0.8 %slice_bitcast_fusion.2 = (f32[16]{0:T(128)S(1)}, f32[16]{0:T(128)S(1)}) fusion(f32[16,2]{0,1:T(2,128)} %param.38), kind=kLoop, calls=%fused_computation.22 | loop fusion | bytes 256 | tf_op jit(solution)/shard_map/jit(_where)/broadcast_in_dim | solution.py:407
  2.2 0.1 fusion.5
  2.3 0.7 %pad_maximum_fusion.rest_0_ = bf16[16,640]{1,0:T(8,128)(2,1)S(1)} fusion(bf16[16,128]{1,0:T(8,128)(2,1)S(1)} %fusion.5, bf16[16,512]{1,0:T(8,128)(2,1)} %param.36), kind=kLoop, calls=%fused_computation.5 | loop fusion | flops 40960 | bytes 40960 | tf_op jit(solution)/shard_map/concatenate | solution.py:410
  3.0 0.0 copy-start
  3.0 5.1 %collective-permute-start.2 = (bf16[16,640]{1,0:T(8,128)(2,1)S(1)}, bf16[16,640]{1,0:T(8,128)(2,1)S(1)}, u32[]{:S(2)}, u32[]{:S(2)}) collective-permute-start(bf16[16,640]{1,0:T(8,128)(2,1)S(1)} %pad_maximum_fusion.rest_0_), channel_id=1, source_target_pairs={{0,12},{4,8},{8,4},{12,0},{1,13},{5,9},{9,5},{13,1},{2,14},{6,10},... | collective-permute-start | bytes 61448 | tf_op jit(solution)/shard_map/ppermute | solution.py:46
  8.1 0.0 collective-permute-start.1
  8.1 0.6 collective-permute-start
  8.6 1.6 %copy.24.state_hbm = bf16[16,3,1024]{2,1,0:T(4,128)(2,1)} copy(bf16[16,3,1024]{2,0,1:T(8,128)(2,1)} %param.23) | data formatting | bytes 196608 | tf_op args[2]
  10.3 9.3 %front.1 = (bf16[16,1024]{1,0:T(8,128)(2,1)}, f32[16,1024]{1,0:T(8,128)}, bf16[32,512]{1,0:T(8,128)(2,1)}) custom-call(bf16[16,2,128,256]{3,2,1,0:T(8,128)(2,1)} %past_hbm.1, bf16[16,8,128]{2,1,0:T(8,128)(2,1)} %queries_hbm.1, bf16[16,2,256]{2,1,0:T(2,128)(2,1)} %entry_hbm.1, s32[16]{0:T(128)} %lengths_ref.1, bf16[16,3,1024]{2,1,0:T(4,128)(2,1)} %copy.24.state_hbm, ...), custom_call_target="tpu_custom_call" | custom-call | flops 6000000000 | bytes 4000000 | tf_op jit(solution)/shard_map/front/pallas_call | solution.py:179
  19.6 0.0 copy-done.4
  19.6 0.0 collective-permute-done.rest_1_
  19.6 0.0 copy-start.3
  19.7 0.0 collective-permute-done.1.rest_2_
  19.7 0.0 copy-start.2
  19.7 0.0 collective-permute-done.2.rest_3_
  19.7 0.0 copy-start.1
  19.7 0.8 %constant_dynamic-update-slice_fusion = bf16[96,512]{1,0:T(8,128)(2,1)S(1)} fusion(bf16[96,512]{1,0:T(8,128)(2,1)S(1)} %slice_dynamic-update-slice_fusion, bf16[32,512]{1,0:T(8,128)(2,1)} %get-tuple-element.13), kind=kLoop, calls=%fused_computation.9 | loop fusion | bytes 65536 | tf_op jit(solution)/shard_map/concatenate | solution.py:417
  20.5 7.1 %all-gather = bf16[384,512]{1,0:T(8,128)(2,1)} all-gather(bf16[96,512]{1,0:T(8,128)(2,1)S(1)} %constant_dynamic-update-slice_fusion), channel_id=2, replica_groups=mesh['parts'=2,'expert'=4,'tensor'=4] {'tensor'}, dimensions={0}, use_global_device_ids=true | all-gather | bytes 491520 | tf_op jit(solution)/shard_map/all_gather | solution.py:418
  27.6 0.0 copy-done
  27.6 0.0 copy-done.3
  27.6 0.0 copy-done.2
  27.6 0.0 copy-done.1
  27.6 19.6 %experts.1 = (f32[64,512]{1,0:T(8,128)}, bf16[64,512]{1,0:T(8,128)(2,1)}, bf16[64,512]{1,0:T(8,128)(2,1)}, bf16[64,512]{1,0:T(8,128)(2,1)}) custom-call(bf16[4,96,512]{2,1,0:T(8,128)(2,1)} %bitcast.12, bf16[16,640]{1,0:T(8,128)(2,1)} %copy-done, bf16[16,640]{1,0:T(8,128)(2,1)} %copy-done.3, bf16[16,640]{1,0:T(8,128)(2,1)} %copy-done.2, ...), custom_call_target="tpu_custom_call" | custom-call | flops 3221225472 | bytes 50331648 | tf_op jit(solution)/shard_map/experts/pallas_call | solution.py:280
  47.3 0.4 collective-permute-start.3
  47.7 1.2 %collective-permute-start.4 = (bf16[64,512]{1,0:T(8,128)(2,1)}, bf16[64,512]{1,0:T(8,128)(2,1)S(1)}, u32[]{:S(2)}, u32[]{:S(2)}) collective-permute-start(bf16[64,512]{1,0:T(8,128)(2,1)} %get-tuple-element.20), channel_id=1, source_target_pairs={{0,2},{1,3},{2,0},{3,1},{4,6},{5,7},{6,4},{7,5},{8,10},{9,11},{10,... | collective-permute-start | bytes 196616 | tf_op jit(solution)/shard_map/ppermute | solution.py:46
  48.8 0.3 collective-permute-start.5
  49.2 0.0 collective-permute-done.3
  49.2 3.0 %collective-permute-done.4 = bf16[64,512]{1,0:T(8,128)(2,1)S(1)} collective-permute-done((bf16[64,512]{1,0:T(8,128)(2,1)}, bf16[64,512]{1,0:T(8,128)(2,1)S(1)}, u32[]{:S(2)}, u32[]{:S(2)}) %collective-permute-start.4) | collective-permute-done | bytes 65568 | tf_op jit(solution)/shard_map/ppermute | solution.py:46
  52.2 1.2 %collective-permute-done.5 = bf16[64,512]{1,0:T(8,128)(2,1)S(1)} collective-permute-done((bf16[64,512]{1,0:T(8,128)(2,1)}, bf16[64,512]{1,0:T(8,128)(2,1)S(1)}, u32[]{:S(2)}, u32[]{:S(2)}) %collective-permute-start.5) | collective-permute-done | bytes 65568 | tf_op jit(solution)/shard_map/ppermute | solution.py:46
  53.4 0.9 %fusion.6 = (bf16[64,512]{1,0:T(8,128)(2,1)S(1)}, f32[64,512]{1,0:T(8,128)S(1)}) fusion(bf16[64,512]{1,0:T(8,128)(2,1)S(1)} %collective-permute-done.5, bf16[64,512]{1,0:T(8,128)(2,1)S(1)} %collective-permute-done.4, f32[64,512]{1,0:T(8,128)} %get-tuple-element.18, bf16[64,512]{1,0:T(8,128)(2,1)S(1)} %collective-permute-done.3), kind=kLoop, calls=%fused_computation.27 | loop fusion | flops 229376 | bytes 524288 | tf_op jit(solution)/shard_map/convert.2
  54.4 1.3 %collective-permute-start.6 = (bf16[16,512]{1,0:T(8,128)(2,1)S(1)}, bf16[16,512]{1,0:T(8,128)(2,1)S(1)}, u32[]{:S(2)}, u32[]{:S(2)}) collective-permute-start(bf16[16,512]{1,0:T(8,128)(2,1)S(1)} %get-tuple-element.24), channel_id=1, source_target_pairs={{0,4},{4,0},{8,12},{12,8},{1,5},{5,1},{9,13},{13,9},{2,6},{6,2},{1... | collective-permute-start | bytes 49160 | tf_op jit(solution)/shard_map/ppermute | solution.py:46
  55.7 2.4 %collective-permute-start.8 = (bf16[16,512]{1,0:T(8,128)(2,1)S(1)}, bf16[16,512]{1,0:T(8,128)(2,1)S(1)}, u32[]{:S(2)}, u32[]{:S(2)}) collective-permute-start(bf16[16,512]{1,0:T(8,128)(2,1)S(1)} %get-tuple-element.25), channel_id=1, source_target_pairs={{0,12},{4,8},{8,4},{12,0},{1,13},{5,9},{9,5},{13,1},{2,14},{6,10},... | collective-permute-start | bytes 49160 | tf_op jit(solution)/shard_map/ppermute | solution.py:46
  58.1 0.5 collective-permute-start.7
  58.6 3.1 %state.1 = (bf16[16,1024]{1,0:T(8,128)(2,1)}, f32[16,16,1024]{2,1,0:T(8,128)}) custom-call(bf16[4,96,512]{2,1,0:T(8,128)(2,1)} %bitcast.13, f32[16,1024]{1,0:T(8,128)} %get-tuple-element.14.act, bf16[16,1024]{1,0:T(8,128)(2,1)} %gate.1, f32[16,16,1024]{2,1,0:T(8,128)} %scan.1, bf16[256,1024]{1,0:T(8,128)(2,1)} %step_proj.1, f32[1,1024]{1,0:T(1,128)} %bitcast.15, ...), custom_call_target="tpu_custom_call" | custom-call | flops 3000000000 | bytes 3000000 | tf_op jit(solution)/shard_map/state/pallas_call | solution.py:351
  61.7 0.0 collective-permute-done.6
  61.7 0.0 collective-permute-done.8
  61.8 1.0 %collective-permute-done.7 = bf16[16,512]{1,0:T(8,128)(2,1)S(1)} collective-permute-done((bf16[16,512]{1,0:T(8,128)(2,1)S(1)}, bf16[16,512]{1,0:T(8,128)(2,1)S(1)}, u32[]{:S(2)}, u32[]{:S(2)}) %collective-permute-start.7) | collective-permute-done | bytes 16416 | tf_op jit(solution)/shard_map/ppermute | solution.py:46
  62.8 0.6 fusion.2
  (8 shorter events, 0.0 us)
Async XLA Ops:
  0.6 19.0 %copy-start.4 = (bf16[16,512]{1,0:T(8,128)(2,1)S(1)}, bf16[16,512]{1,0:T(8,128)(2,1)}, u32[]{:S(2)}) copy-start(bf16[16,512]{1,0:T(8,128)(2,1)} %param.36) | copy-start | bytes 49156
  3.0 24.6 %copy-start = (bf16[16,640]{1,0:T(8,128)(2,1)}, bf16[16,640]{1,0:T(8,128)(2,1)S(1)}, u32[]{:S(2)}) copy-start(bf16[16,640]{1,0:T(8,128)(2,1)S(1)} %pad_maximum_fusion.rest_0_) | copy-start | bytes 61444
  3.0 16.7 %collective-permute-start.2 = (bf16[16,640]{1,0:T(8,128)(2,1)S(1)}, bf16[16,640]{1,0:T(8,128)(2,1)S(1)}, u32[]{:S(2)}, u32[]{:S(2)}) collective-permute-start(bf16[16,640]{1,0:T(8,128)(2,1)S(1)} %pad_maximum_fusion.rest_0_), channel_id=1, source_target_pairs={{0,12},{4,8},{8,4},{12,0},{1,13},{5,9},{9,5},{13,1},{2,14},{6,10},... | collective-permute-start | bytes 61448 | tf_op jit(solution)/shard_map/ppermute | solution.py:46
  8.1 11.6 %collective-permute-start.1 = (bf16[16,640]{1,0:T(8,128)(2,1)S(1)}, bf16[16,640]{1,0:T(8,128)(2,1)S(1)}, u32[]{:S(2)}, u32[]{:S(2)}) collective-permute-start(bf16[16,640]{1,0:T(8,128)(2,1)S(1)} %pad_maximum_fusion.rest_0_), channel_id=1, source_target_pairs={{0,8},{4,12},{8,0},{12,4},{1,9},{5,13},{9,1},{13,5},{2,10},{6,14},... | collective-permute-start | bytes 61448 | tf_op jit(solution)/shard_map/ppermute | solution.py:46
  8.1 11.6 %collective-permute-start = (bf16[16,640]{1,0:T(8,128)(2,1)S(1)}, bf16[16,640]{1,0:T(8,128)(2,1)S(1)}, u32[]{:S(2)}, u32[]{:S(2)}) collective-permute-start(bf16[16,640]{1,0:T(8,128)(2,1)S(1)} %pad_maximum_fusion.rest_0_), channel_id=1, source_target_pairs={{0,4},{4,0},{8,12},{12,8},{1,5},{5,1},{9,13},{13,9},{2,6},{6,2},{1... | collective-permute-start | bytes 61448 | tf_op jit(solution)/shard_map/ppermute | solution.py:46
  19.6 8.0 %copy-start.3 = (bf16[16,640]{1,0:T(8,128)(2,1)}, bf16[16,640]{1,0:T(8,128)(2,1)S(1)}, u32[]{:S(2)}) copy-start(bf16[16,640]{1,0:T(8,128)(2,1)S(1)} %collective-permute-done.rest_1_) | copy-start | bytes 61444
  19.7 7.9 %copy-start.2 = (bf16[16,640]{1,0:T(8,128)(2,1)}, bf16[16,640]{1,0:T(8,128)(2,1)S(1)}, u32[]{:S(2)}) copy-start(bf16[16,640]{1,0:T(8,128)(2,1)S(1)} %collective-permute-done.1.rest_2_) | copy-start | bytes 61444
  19.7 7.9 %copy-start.1 = (bf16[16,640]{1,0:T(8,128)(2,1)}, bf16[16,640]{1,0:T(8,128)(2,1)S(1)}, u32[]{:S(2)}) copy-start(bf16[16,640]{1,0:T(8,128)(2,1)S(1)} %collective-permute-done.2.rest_3_) | copy-start | bytes 61444
  47.3 1.9 %collective-permute-start.3 = (bf16[64,512]{1,0:T(8,128)(2,1)}, bf16[64,512]{1,0:T(8,128)(2,1)S(1)}, u32[]{:S(2)}, u32[]{:S(2)}) collective-permute-start(bf16[64,512]{1,0:T(8,128)(2,1)} %get-tuple-element.19), channel_id=1, source_target_pairs={{0,1},{1,0},{2,3},{3,2},{4,5},{5,4},{6,7},{7,6},{8,9},{9,8},{10,11... | collective-permute-start | bytes 196616 | tf_op jit(solution)/shard_map/ppermute | solution.py:46
  47.7 4.6 %collective-permute-start.4 = (bf16[64,512]{1,0:T(8,128)(2,1)}, bf16[64,512]{1,0:T(8,128)(2,1)S(1)}, u32[]{:S(2)}, u32[]{:S(2)}) collective-permute-start(bf16[64,512]{1,0:T(8,128)(2,1)} %get-tuple-element.20), channel_id=1, source_target_pairs={{0,2},{1,3},{2,0},{3,1},{4,6},{5,7},{6,4},{7,5},{8,10},{9,11},{10,... | collective-permute-start | bytes 196616 | tf_op jit(solution)/shard_map/ppermute | solution.py:46
  48.8 4.6 %collective-permute-start.5 = (bf16[64,512]{1,0:T(8,128)(2,1)}, bf16[64,512]{1,0:T(8,128)(2,1)S(1)}, u32[]{:S(2)}, u32[]{:S(2)}) collective-permute-start(bf16[64,512]{1,0:T(8,128)(2,1)} %get-tuple-element.21), channel_id=1, source_target_pairs={{0,3},{1,2},{2,1},{3,0},{4,7},{5,6},{6,5},{7,4},{8,11},{9,10},{10,... | collective-permute-start | bytes 196616 | tf_op jit(solution)/shard_map/ppermute | solution.py:46
  54.4 7.3 %collective-permute-start.6 = (bf16[16,512]{1,0:T(8,128)(2,1)S(1)}, bf16[16,512]{1,0:T(8,128)(2,1)S(1)}, u32[]{:S(2)}, u32[]{:S(2)}) collective-permute-start(bf16[16,512]{1,0:T(8,128)(2,1)S(1)} %get-tuple-element.24), channel_id=1, source_target_pairs={{0,4},{4,0},{8,12},{12,8},{1,5},{5,1},{9,13},{13,9},{2,6},{6,2},{1... | collective-permute-start | bytes 49160 | tf_op jit(solution)/shard_map/ppermute | solution.py:46
  55.7 6.0 %collective-permute-start.8 = (bf16[16,512]{1,0:T(8,128)(2,1)S(1)}, bf16[16,512]{1,0:T(8,128)(2,1)S(1)}, u32[]{:S(2)}, u32[]{:S(2)}) collective-permute-start(bf16[16,512]{1,0:T(8,128)(2,1)S(1)} %get-tuple-element.25), channel_id=1, source_target_pairs={{0,12},{4,8},{8,4},{12,0},{1,13},{5,9},{9,5},{13,1},{2,14},{6,10},... | collective-permute-start | bytes 49160 | tf_op jit(solution)/shard_map/ppermute | solution.py:46
  58.1 4.6 %collective-permute-start.7 = (bf16[16,512]{1,0:T(8,128)(2,1)S(1)}, bf16[16,512]{1,0:T(8,128)(2,1)S(1)}, u32[]{:S(2)}, u32[]{:S(2)}) collective-permute-start(bf16[16,512]{1,0:T(8,128)(2,1)S(1)} %get-tuple-element.26), channel_id=1, source_target_pairs={{0,8},{4,12},{8,0},{12,4},{1,9},{5,13},{9,1},{13,5},{2,10},{6,14},... | collective-permute-start | bytes 49160 | tf_op jit(solution)/shard_map/ppermute | solution.py:46

commit v2 on v1

v2 whole, which is shorter than its diff:
```python
import functools

import jax
import jax.numpy as jnp
from jax import lax
from jax.experimental import pallas as pl
from jax.experimental.pallas import tpu as pltpu
from jax.sharding import PartitionSpec as P

EXPERTS = 8
LANES = 128
F32 = jnp.float32
BF16 = jnp.bfloat16

HBM_SPEC = pl.BlockSpec(memory_space=pl.ANY)
VMEM_SPEC = pl.BlockSpec(memory_space=pltpu.VMEM)


def silu(v):
    return v / (1.0 + jnp.exp(-v))


def split_bf16(v):
    high = v.astype(BF16)
    return high, (v - high.astype(F32)).astype(BF16)


def partner(index, step, count):
    if count & (count - 1) == 0:
        return index ^ step
    return (index + step) % count


def returner(index, step, count):
    if count & (count - 1) == 0:
        return index ^ step
    return (index - step) % count


def exchange(blocks, axis, back=False):
    count = lax.axis_size(axis)
    rule = returner if back else partner
    out = {0: blocks[0]}
    for step in range(count - 1, 0, -1):
        pairs = [(i, rule(i, step, count)) for i in range(count)]
        out[step] = lax.ppermute(blocks[step], axis, pairs)
    return [out[step] for step in range(count)]


def on_chip(value):
    return pltpu.with_memory_space_constraint(value, pltpu.VMEM)


def off_chip(*values):
    return [pltpu.with_memory_space_constraint(value, pltpu.HBM) for value in values]


def limit(mebibytes):
    return pltpu.CompilerParams(vmem_limit_bytes=mebibytes * 2**20)


def scratch_like(*arrays):
    return [pltpu.VMEM(a.shape, a.dtype) for a in arrays]


def pack_kernel(tokens_hbm, routes_hbm, gates_hbm, packed, tokens, routes, gates, square, sems):
    copies = [
        pltpu.make_async_copy(src, dst, sems.at[n])
        for n, (src, dst) in enumerate((
            (tokens_hbm, tokens), (routes_hbm, routes), (gates_hbm, gates)
        ))
    ]
    for copy in copies:
        copy.start()
    seqs, width = tokens.shape
    square[...] = jnp.zeros_like(square)
    row = lax.broadcasted_iota(jnp.int32, (LANES, seqs), 0)
    copies[1].wait()
    copies[2].wait()
    weight = jnp.zeros((LANES, seqs), F32)
    for k in range(routes.shape[0]):
        weight = weight + jnp.where(
            row % EXPERTS == routes[k : k + 1, :], gates[k : k + 1, :], 0.0
        )
    high = weight.astype(BF16).astype(F32)
    square[:, :seqs] = jnp.where(
        row < EXPERTS, high, jnp.where(row < 2 * EXPERTS, weight - high, 0.0)
    )
    packed[:, width:] = square[...].T[:seqs, :].astype(BF16)
    copies[0].wait()
    packed[:, :width] = tokens[...]


def pack(expert_input, routes, gates):
    seqs, width = expert_input.shape
    operands = (expert_input, routes.T, gates.T)
    return pl.pallas_call(
        pack_kernel,
        out_shape=pltpu.VMEM((seqs, width + LANES), BF16),
        in_specs=[HBM_SPEC] * 3,
        out_specs=VMEM_SPEC,
        scratch_shapes=scratch_like(*operands) + [
            pltpu.VMEM((LANES, LANES), F32), pltpu.SemaphoreType.DMA((3,)),
        ],
        compiler_params=limit(4),
        name="pack",
    )(*off_chip(*operands))


def front_kernel(
    width, ready, chunk,
    state_hbm, input_hbm, taps_hbm, bias_hbm, proj_hbm, inner_hbm, outer_hbm,
    act_ref, mix_ref, inner, outer,
    state, inputs, taps, bias, proj, sems,
):
    small = [
        pltpu.make_async_copy(src, dst, sems.at[n])
        for n, (src, dst) in enumerate((
            (state_hbm, state), (input_hbm, inputs), (taps_hbm, taps),
            (bias_hbm, bias), (proj_hbm, proj),
        ))
    ]
    large = []
    for c in range(ready):
        span = pl.ds(c * chunk, chunk)
        for n, (src, dst) in enumerate((
            (inner_hbm.at[0, 0, span], inner.at[c, 0]),
            (inner_hbm.at[0, 1, span], inner.at[c, 1]),
            (outer_hbm.at[0, span], outer.at[c]),
        )):
            large.append(
                pltpu.make_async_copy(src, dst, sems.at[len(small) + 3 * c + n])
            )
    for copy in small + large:
        copy.start()
    for copy in small[:4]:
        copy.wait()
    seqs = inputs.shape[0]
    total = bias[...]
    for k in range(taps.shape[0] - 1):
        total = total + state[k].astype(F32) * taps[k : k + 1, :]
    total = total + inputs[...].astype(F32) * taps[taps.shape[0] - 1 :, :]
    act = silu(total)
    act_ref[...] = act
    small[4].wait()
    mix = lax.dot_general(
        act.astype(BF16), proj[...], (((1,), (1,)), ((), ())), preferred_element_type=F32
    )
    outputs = mix.shape[1]
    spans = -(-outputs // width)
    row = 0
    for piece in split_bf16(mix):
        for span in range(spans):
            cut = piece[:, span * width : min(outputs, (span + 1) * width)]
            if cut.shape[1] < width:
                cut = jnp.concatenate(
                    [cut.astype(F32), jnp.zeros((seqs, width - cut.shape[1]), F32)], axis=1
                ).astype(BF16)
            mix_ref[row : row + seqs, :] = cut
            row += seqs
    for copy in large:
        copy.wait()


def front(
    conv_state, mamba_input, conv_weight, conv_bias, state_proj, inner_weights, outer_weights,
    width, ready, chunk,
):
    seqs, channels = mamba_input.shape
    features = inner_weights.shape[3]
    spans = -(-state_proj.shape[0] // width)
    operands = (
        jnp.swapaxes(conv_state, 0, 1), mamba_input, conv_weight,
        conv_bias.reshape(1, channels), state_proj,
    )
    return pl.pallas_call(
        functools.partial(front_kernel, width, ready, chunk),
        out_shape=(
            pltpu.VMEM((seqs, channels), F32),
            pltpu.VMEM((2 * spans * seqs, width), BF16),
            pltpu.VMEM((ready, 2, chunk, features), BF16),
            pltpu.VMEM((ready, chunk, features), BF16),
        ),
        in_specs=[HBM_SPEC] * 7,
        out_specs=(VMEM_SPEC,) * 4,
        scratch_shapes=scratch_like(*operands) + [
            pltpu.SemaphoreType.DMA((len(operands) + 3 * ready,)),
        ],
        compiler_params=limit(4),
        cost_estimate=pl.CostEstimate(
            flops=4 * 10**9, bytes_accessed=14 * 10**6, transcendentals=0
        ),
        name="front",
    )(*off_chip(*operands, inner_weights, outer_weights))


def attend_kernel(
    past_hbm, queries_hbm, entry_hbm, lengths_ref, out_hbm,
    past, queries, entry, scores, own, heads, out, sems,
):
    seqs, head_count, size = queries.shape
    groups = entry.shape[1]
    per_group = head_count // groups
    positions = past.shape[1] // groups
    parts = 4 if seqs % 4 == 0 else 1
    part = seqs // parts
    small = [
        pltpu.make_async_copy(queries_hbm, queries, sems.at[parts]),
        pltpu.make_async_copy(entry_hbm, entry, sems.at[parts + 1]),
    ]
    large = [
        pltpu.make_async_copy(
            past_hbm.at[pl.ds(n * part, part)], past.at[pl.ds(n * part, part)], sems.at[n]
        )
        for n in range(parts)
    ]
    for copy in small + large:
        copy.start()
    scaling = size ** (-0.5)
    group_of = lambda lanes: lax.broadcasted_iota(jnp.int32, (head_count, lanes), 0) // per_group
    position = lax.broadcasted_iota(jnp.int32, (head_count, positions), 1)

    def pick(values, index):
        result = values[0]
        for g in range(1, groups):
            result = jnp.where(index == g, values[g], result)
        return result

    def entry_rows(s, lanes):
        return pick(
            [
                jnp.broadcast_to(entry[s, g : g + 1, lanes].astype(F32), (head_count, size))
                for g in range(groups)
            ],
            group_of(size),
        )

    for copy in small:
        copy.wait()
    for n in range(parts):
        large[n].wait()
        for s in range(n * part, (n + 1) * part):
            every = lax.dot_general(
                queries[s], past[s, :, :size], (((1,), (1,)), ((), ())),
                preferred_element_type=F32,
            )
            mine = pick(
                [every[:, g * positions : (g + 1) * positions] for g in range(groups)],
                group_of(positions),
            )
            scores[s] = jnp.where(position < lengths_ref[s], mine * scaling, -jnp.inf)
            own[s] = queries[s].astype(F32) * entry_rows(s, slice(0, size))
    score = scores[...]
    own_score = jnp.sum(own[...], axis=2, keepdims=True) * scaling
    highest = jnp.maximum(jnp.max(score, axis=2, keepdims=True), own_score)
    weights = jnp.exp(score - highest)
    own_weight = jnp.exp(own_score - highest)
    denominator = jnp.sum(weights, axis=2, keepdims=True) + own_weight
    scores[...] = weights / denominator
    own[...] = jnp.broadcast_to(own_weight / denominator, own.shape)
    for s in range(seqs):
        low = scores[s]
        spread = [
            jnp.where(group_of(positions) == g, low, 0.0).astype(BF16) for g in range(groups)
        ]
        spread = spread[0] if groups == 1 else jnp.concatenate(spread, axis=1)
        mixed = jnp.dot(spread, past[s, :, size:], preferred_element_type=F32)
        heads[s] = mixed + own[s].astype(BF16).astype(F32) * entry_rows(s, slice(size, None))
    for h in range(head_count):
        out[:, h * size : (h + 1) * size] = heads[:, h, :].astype(BF16)
    store = pltpu.make_async_copy(out, out_hbm, sems.at[parts + 2])
    store.start()
    store.wait()


def attend(queries, new_entry, past_entries, lengths):
    seqs, head_count, size = queries.shape
    past = past_entries.reshape(seqs, -1, 2 * size)
    positions = past_entries.shape[2]
    return pl.pallas_call(
        attend_kernel,
        out_shape=jax.ShapeDtypeStruct((seqs, head_count * size), BF16),
        in_specs=[HBM_SPEC, HBM_SPEC, HBM_SPEC, pl.BlockSpec(memory_space=pltpu.SMEM)],
        out_specs=HBM_SPEC,
        scratch_shapes=scratch_like(past, queries, new_entry) + [
            pltpu.VMEM((seqs, head_count, positions), F32),
            pltpu.VMEM((seqs, head_count, size), F32),
            pltpu.VMEM((seqs, head_count, size), F32),
            pltpu.VMEM((seqs, head_count * size), BF16),
            pltpu.SemaphoreType.DMA((8,)),
        ],
        compiler_params=limit(8),
        cost_estimate=pl.CostEstimate(
            flops=4 * 10**9, bytes_accessed=2 * 10**6, transcendentals=0
        ),
        name="attend",
    )(*off_chip(past, queries, new_entry), lengths)


def expert_kernel(chunk, ready, peers, ways, gathered, *rest):
    tables = rest[:peers]
    inner_ready, outer_ready, inner_hbm, outer_hbm = rest[peers : peers + 4]
    outs = rest[peers + 4 : peers + 4 + ways]
    inner, outer, features, hidden, total, sems = rest[peers + 4 + ways :]
    experts, _, hidden_units, _ = inner_hbm.shape
    count = hidden_units // chunk
    tokens = features.shape[0]
    width = gathered.shape[2]
    copies = []
    for step in range(ready, experts * count):
        e, c = divmod(step, count)
        span = pl.ds(c * chunk, chunk)
        slot = step - ready
        copies.append([
            pltpu.make_async_copy(src, dst, sems.at[slot, n])
            for n, (src, dst) in enumerate((
                (inner_hbm.at[e, 0, span], inner.at[slot, 0]),
                (inner_hbm.at[e, 1, span], inner.at[slot, 1]),
                (outer_hbm.at[e, span], outer.at[slot]),
            ))
        ])
    for group in copies:
        for copy in group:
            copy.start()
    for t in range(ways):
        features[:, t * width : (t + 1) * width] = gathered[t, :tokens, :]
    table = jnp.concatenate([ref[:, width:].astype(F32) for ref in tables], axis=0)
    lane = lax.broadcasted_iota(jnp.int32, table.shape, 1)
    replicas = max(1, peers // EXPERTS)
    first = lax.axis_index("expert") * experts
    piece = min(256, chunk)
    contract = (((1,), (1,)), ((), ()))
    for step in range(experts * count):
        e, c = divmod(step, count)
        if c == 0:
            name = (first + e) // replicas
            chosen = (lane == name) | (lane == name + EXPERTS)
            gain = jnp.sum(jnp.where(chosen, table, 0.0), axis=1, keepdims=True)
        if step < ready:
            weights, down = inner_ready.at[step], outer_ready.at[step]
        else:
            weights, down = inner.at[step - ready], outer.at[step - ready]
            for copy in copies[step - ready]:
                copy.wait()
        for p in range(0, chunk, piece):
            gate = lax.dot_general(
                weights[0, p : p + piece], features[...], contract, preferred_element_type=F32
            )
            up = lax.dot_general(
                weights[1, p : p + piece], features[...], contract, preferred_element_type=F32
            )
            hidden[p : p + piece, :] = (silu(gate) * up).astype(BF16)
        value = gain * lax.dot_general(
            hidden[...], down[...], (((0,), (0,)), ((), ())), preferred_element_type=F32
        )
        if step == 0:
            total[...] = value
        else:
            total[...] += value
    me = lax.axis_index("tensor")
    for step in range(ways):
        start = pl.multiple_of(partner(me, step, ways) * width, LANES)
        outs[step][...] = total[:, pl.ds(start, width)].astype(outs[step].dtype)


def run_experts(gathered, packed, inner_ready, outer_ready, inner_weights, outer_weights):
    ways, rows, width = gathered.shape
    peers = len(packed)
    tokens = sum(p.shape[0] for p in packed)
    experts, _, hidden_units, features = inner_weights.shape
    ready, chunk, _ = outer_ready.shape
    left = max(1, experts * hidden_units // chunk - ready)
    work = 6 * tokens * experts * hidden_units * features
    moved = 2 * (inner_weights.size + outer_weights.size)
    return pl.pallas_call(
        functools.partial(expert_kernel, chunk, ready, peers, ways),
        out_shape=tuple(
            pltpu.VMEM((tokens, width), F32 if step == 0 else BF16) for step in range(ways)
        ),
        in_specs=[VMEM_SPEC] * (3 + peers) + [HBM_SPEC, HBM_SPEC],
        out_specs=(VMEM_SPEC,) * ways,
        scratch_shapes=[
            pltpu.VMEM((left, 2, chunk, features), BF16),
            pltpu.VMEM((left, chunk, features), BF16),
            pltpu.VMEM((tokens, features), BF16),
            pltpu.VMEM((chunk, tokens), BF16),
            pltpu.VMEM((tokens, features), F32),
            pltpu.SemaphoreType.DMA((left, 3)),
        ],
        compiler_params=limit(44),
        cost_estimate=pl.CostEstimate(
            flops=work, bytes_accessed=moved, transcendentals=0
        ),
        name="experts",
    )(
        on_chip(gathered), *[on_chip(p) for p in packed], on_chip(inner_ready),
        on_chip(outer_ready), *off_chip(inner_weights, outer_weights),
    )


def state_kernel(
    tokens, seqs, low_rank,
    gathered, act, gate, scan, step_proj, step_bias, decay, skip,
    out, next_state,
    square,
):
    ways, rows, width = gathered.shape
    states = decay.shape[0]
    spans = (rows - tokens) // (2 * seqs)
    pieces = []
    for span in range(spans):
        piece = None
        for t in range(ways):
            for half in range(2):
                row = tokens + (half * spans + span) * seqs
                part = gathered[t, row : row + seqs, :].astype(F32)
                piece = part if piece is None else piece + part
        pieces.append(piece)
    mixing = pieces[0] if spans == 1 else jnp.concatenate(pieces, axis=1)
    square[...] = jnp.zeros_like(square)
    square[:seqs, :] = mixing[:, low_rank : low_rank + LANES]
    columns = square[...].T
    step = (
        jnp.dot(mixing[:, :low_rank].astype(BF16), step_proj[...], preferred_element_type=F32)
        + step_bias[...]
    )
    step_size = jnp.maximum(step, 0.0) + jnp.log1p(jnp.exp(-jnp.abs(step)))
    rates = jnp.exp(decay[...])
    drive = step_size * act[...]
    results = []
    for s in range(seqs):
        in_coef = columns[:states, s : s + 1]
        out_coef = columns[states : 2 * states, s : s + 1]
        new = jnp.exp(-step_size[s : s + 1, :] * rates) * scan[s] + drive[s : s + 1, :] * in_coef
        next_state[s] = new
        results.append(jnp.sum(new * out_coef, axis=0, keepdims=True))
    mixed = jnp.concatenate(results, axis=0) + skip[...] * act[...]
    out[...] = (mixed * silu(gate[...].astype(F32))).astype(BF16)


def update_state(
    gathered, tokens, act, mamba_gate, scan_state, step_proj, step_bias, decay_log, skip_gain
):
    seqs, states, channels = scan_state.shape
    low_rank = step_proj.shape[0]
    block = min(512, channels)
    lane_block = lambda rows: pl.BlockSpec((rows, block), lambda c: (0, c))
    state_block = pl.BlockSpec((seqs, states, block), lambda c: (0, 0, c))
    return pl.pallas_call(
        functools.partial(state_kernel, tokens, seqs, low_rank),
        grid=(channels // block,),
        out_shape=(
            jax.ShapeDtypeStruct((seqs, channels), BF16),
            jax.ShapeDtypeStruct(scan_state.shape, F32),
        ),
        in_specs=[
            pl.BlockSpec(gathered.shape, lambda c: (0, 0, 0)),
            lane_block(seqs), lane_block(seqs), state_block,
            lane_block(low_rank), lane_block(1), lane_block(states), lane_block(1),
        ],
        out_specs=(lane_block(seqs), state_block),
        scratch_shapes=[pltpu.VMEM((LANES, LANES), F32)],
        compiler_params=limit(12),
        cost_estimate=pl.CostEstimate(
            flops=3 * 10**9, bytes_accessed=3 * 10**6, transcendentals=0
        ),
        name="state",
    )(
        gathered, act, mamba_gate, scan_state, step_proj,
        step_bias.reshape(1, channels), decay_log, skip_gain.reshape(1, channels),
    )


def shards(
    mamba_input,
    mamba_gate,
    conv_state,
    scan_state,
    conv_weight,
    conv_bias,
    state_proj,
    step_proj,
    step_bias,
    decay_log,
    skip_gain,
    queries,
    new_entry,
    past_entries,
    lengths,
    expert_input,
    routes,
    slots,
    gates,
    inner_weights,
    outer_weights,
):
    del slots
    peers = lax.axis_size("expert")
    ways = lax.axis_size("tensor")
    seqs, width = expert_input.shape
    tokens = peers * seqs

    hidden_units = inner_weights.shape[2]
    chunk = min(512, hidden_units)
    ready = min(2, hidden_units // chunk)

    packed = exchange([pack(expert_input, routes, gates)] * peers, "expert")
    act, mix, inner_ready, outer_ready = front(
        conv_state, mamba_input, conv_weight, conv_bias, state_proj,
        inner_weights, outer_weights, width, ready, chunk,
    )
    mine = jnp.concatenate([p[:, :width] for p in packed] + [mix], axis=0)
    gathered = lax.all_gather(mine, "tensor", axis=0)
    partial = run_experts(
        gathered, packed, inner_ready, outer_ready, inner_weights, outer_weights
    )

    arrived = exchange(partial, "tensor")
    attention_out = attend(queries, new_entry, past_entries, lengths)
    share = arrived[0]
    for part in arrived[1:]:
        share = share + part.astype(F32)
    mamba_out, next_state = update_state(
        gathered, tokens, act, mamba_gate, scan_state, step_proj, step_bias, decay_log, skip_gain
    )
    blocks = [share[n * seqs : (n + 1) * seqs] for n in range(peers)]
    blocks = [blocks[0]] + [block.astype(BF16) for block in blocks[1:]]
    returned = exchange(blocks, "expert", back=True)
    merged = returned[0]
    for part in returned[1:]:
        merged = merged + part.astype(F32)
    return (mamba_out, next_state, attention_out, merged.astype(BF16))


def solution(mesh):
    return jax.shard_map(
        shards,
        mesh=mesh,
        in_specs=(
            P(("parts", "expert"), "tensor"),
            P(("parts", "expert"), "tensor"),
            P(("parts", "expert"), None, "tensor"),
            P(("parts", "expert"), None, "tensor"),
            P(None, "tensor"),
            P("tensor"),
            P(None, "tensor"),
            P(None, "tensor"),
            P("tensor"),
            P(None, "tensor"),
            P("tensor"),
            P(("parts", "expert"), "tensor", None),
            P(("parts", "expert"), "tensor", None),
            P(("parts", "expert"), "tensor", None, None),
            P(("parts", "expert")),
            P(("parts", "expert"), "tensor"),
            P(("parts", "expert"), None),
            P(("parts", "expert"), None),
            P(("parts", "expert"), None),
            P("expert", None, "tensor", None),
            P("expert", "tensor", None),
        ),
        out_specs=(
            P(("parts", "expert"), "tensor"),
            P(("parts", "expert"), None, "tensor"),
            P(("parts", "expert"), "tensor"),
            P(("parts", "expert"), "tensor"),
        ),
        check_vma=False,
    )
```

time: 63.9 us -> 52.2 us (0.82)
  Pallas kernels: 32.1 us -> 27.6 us
  local copies, waits for them, and re-layouts: 3.96 us -> 0.06 us
  other arithmetic: 2.37 us -> 0.66 us
  waiting for transfers between devices: 5.29 us -> 4.41 us
  blocking collectives: 7.11 us -> 6.44 us
    pallas_call x2 -> x4, Pallas kernels: 28.9 us -> 25.8 us  [the longest x1 16.6 us: run_experts(): pl.pallas_call(functools.partial(expert_kernel, chunk, ready, peers, ways...]
    unnamed x15 -> x18, local copies, waits for them, and re-layouts: 1.67 us -> 0.05 us
    pallas_call x1, Pallas kernels: 3.11 us -> 1.79 us  [update_state(): pl.pallas_call(functools.partial(state_kernel, tokens, seqs, low_rank), g...]
    another operation x1, other arithmetic: 0.94 us -> 0.04 us
    ppermute x9, waiting for transfers between devices: 5.29 us -> 4.41 us  [exchange(): out[step] = lax.ppermute(blocks[step], axis, pairs)]
    concatenate x1, local copies, waits for them, and re-layouts: 0.76 us -> 0.01 us  [shards(): mine = jnp.concatenate([p[:, :width] for p in packed] + [mix], axis=0)]
    eq x1 -> x0, local copies, waits for them, and re-layouts: 0.76 us -> none  [shards(): lane % EXPERTS == routes[:, k:k + 1]]
    broadcast_in_dim x1 -> x0, local copies, waits for them, and re-layouts: 0.76 us -> none  [shards(): jnp.where(lane % EXPERTS == routes[:, k:k + 1], gates[:, k:k + 1], 0.0)]
  transfers between devices with their start and end apart: 9 -> 9, of which waited for: 3 -> 3; matrix products, arithmetic and copies ran while one was open for 3% -> 0% of each run, Pallas kernels for 20% -> 20%
where the time goes in v2:
time: 52.2 us; the launch traced here: 52 us
  Pallas kernels  27.6 us (53%)
  starting transfers between devices  12.1 us (23%)
  blocking collectives  6.44 us (12%)
  waiting for transfers between devices  4.41 us (8%)
  between operations  0.81 us (2%)
  other arithmetic  0.66 us (1%)
    pallas_call x1, Pallas kernels, run_experts(): pl.pallas_call(functools.partial(expert_kernel, chunk, ready, peers, ways...  16.6 us
    ppermute x9, starting transfers between devices, exchange(): out[step] = lax.ppermute(blocks[step], axis, pairs)  12.1 us
    all_gather x1, blocking collectives, shards(): gathered = lax.all_gather(mine, 'tensor', axis=0)  6.44 us
    pallas_call x1, Pallas kernels, front(): pl.pallas_call(functools.partial(front_kernel, width, ready, chunk), out_...  5.02 us
    ppermute x9, waiting for transfers between devices, exchange(): out[step] = lax.ppermute(blocks[step], axis, pairs)  4.41 us
    pallas_call x1, Pallas kernels, attend(): pl.pallas_call(attend_kernel, out_shape=jax.ShapeDtypeStruct((seqs, head_...  3.36 us
    pallas_call x1, Pallas kernels, update_state(): pl.pallas_call(functools.partial(state_kernel, tokens, seqs, low_rank), g...  1.79 us
  transfers between devices with their start and end apart: 9, of which 3 were waited for; matrix products, arithmetic and copies ran while one was open for 0% of the time, Pallas kernels for 20%

profile of v2, /device:TPU:0, one launch (start us, length us, event | category | flops | bytes accessed | tf_op | source)
XLA Modules:
  0.0 52.0 jit_solution(6184433632457208520)
XLA Ops:
  0.6 0.8 %pack.1.rest_0_ = bf16[16,640]{1,0:T(8,128)(2,1)S(1)} custom-call(bf16[16,512]{1,0:T(8,128)(2,1)} %tokens_hbm.1, s32[2,16]{1,0:T(2,128)} %bitcast.14, f32[2,16]{1,0:T(2,128)} %bitcast.15), custom_call_target="tpu_custom_call" | custom-call | tf_op jit(solution)/shard_map/pack/pallas_call | solution.py:97
  1.5 3.1 %collective-permute-start = (bf16[16,640]{1,0:T(8,128)(2,1)S(1)}, bf16[16,640]{1,0:T(8,128)(2,1)S(1)}, u32[]{:S(2)}, u32[]{:S(2)}) collective-permute-start(bf16[16,640]{1,0:T(8,128)(2,1)S(1)} %pack.1.rest_0_), channel_id=1, source_target_pairs={{0,4},{4,0},{8,12},{12,8},{1,5},{5,1},{9,13},{13,9},{2,6},{6,2},{1... | collective-permute-start | bytes 61448 | tf_op jit(solution)/shard_map/ppermute | solution.py:46
  4.6 2.6 %collective-permute-start.1 = (bf16[16,640]{1,0:T(8,128)(2,1)S(1)}, bf16[16,640]{1,0:T(8,128)(2,1)S(1)}, u32[]{:S(2)}, u32[]{:S(2)}) collective-permute-start(bf16[16,640]{1,0:T(8,128)(2,1)S(1)} %pack.1.rest_0_), channel_id=1, source_target_pairs={{0,8},{4,12},{8,0},{12,4},{1,9},{5,13},{9,1},{13,5},{2,10},{6,14},... | collective-permute-start | bytes 61448 | tf_op jit(solution)/shard_map/ppermute | solution.py:46
  7.2 0.0 collective-permute-start.2
  7.2 5.0 %front.1 = (f32[16,1024]{1,0:T(8,128)S(1)}, bf16[32,512]{1,0:T(8,128)(2,1)S(1)}, bf16[2,2,512,2048]{3,2,1,0:T(8,128)(2,1)S(1)}, bf16[2,512,2048]{2,1,0:T(8,128)(2,1)S(1)}) custom-call(bf16[3,16,1024]{2,1,0:T(8,128)(2,1)} %bitcast.12, bf16[16,1024]{1,0:T(8,128)(2,1)} %input_hbm.1, f32[4,1024]{1,0:T(4,128)} %taps_hbm.1, f32[1,1024]{1,0:T(1,128)} %bitcast.13, ...), custom_call_target="tpu_custom_call" | custom-call | flops 4000000000 | bytes 14000000 | tf_op jit(solution)/shard_map/front/pallas_call | solution.py:176
  12.2 0.0 collective-permute-done.rest_1_
  12.2 0.0 collective-permute-done.1.rest_2_
  12.3 0.5 collective-permute-done.2.rest_3_
  12.8 6.4 %all-gather = bf16[384,512]{1,0:T(8,128)(2,1)S(1)} all-gather(bf16[96,512]{1,0:T(8,128)(2,1)S(1)} %constant_dynamic-update-slice_fusion), channel_id=2, replica_groups=mesh['parts'=2,'expert'=4,'tensor'=4] {'tensor'}, dimensions={0}, use_global_device_ids=true | all-gather | bytes 491520 | tf_op jit(solution)/shard_map/all_gather | solution.py:513
  19.2 0.0 copy-start.6
  19.2 16.6 %experts.1 = (f32[64,512]{1,0:T(8,128)S(1)}, bf16[64,512]{1,0:T(8,128)(2,1)S(1)}, bf16[64,512]{1,0:T(8,128)(2,1)S(1)}, bf16[64,512]{1,0:T(8,128)(2,1)S(1)}) custom-call(bf16[4,96,512]{2,1,0:T(8,128)(2,1)S(1)} %bitcast.8, bf16[16,640]{1,0:T(8,128)(2,1)S(1)} %pack.1.rest_0_, bf16[16,640]{1,0:T(8,128)(2,1)S(1)} %collective-permute-done.rest_1_, ...), custom_call_target="tpu_custom_call" | custom-call | flops 3221225472 | bytes 50331648 | tf_op jit(solution)/shard_map/experts/pallas_call | solution.py:375
  35.8 0.0 copy-start
  35.8 0.0 copy-start.1
  35.8 0.0 copy-start.2
  35.8 0.0 copy-start.3
  35.8 0.0 copy-start.4
  35.8 0.0 copy-start.5
  35.8 0.4 collective-permute-start.3
  36.3 1.2 %collective-permute-start.4 = (bf16[64,512]{1,0:T(8,128)(2,1)S(1)}, bf16[64,512]{1,0:T(8,128)(2,1)S(1)}, u32[]{:S(2)}, u32[]{:S(2)}) collective-permute-start(bf16[64,512]{1,0:T(8,128)(2,1)S(1)} %get-tuple-element.22), channel_id=1, source_target_pairs={{0,2},{1,3},{2,0},{3,1},{4,6},{5,7},{6,4},{7,5},{8,10},{9,11},{10,... | collective-permute-start | bytes 196616 | tf_op jit(solution)/shard_map/ppermute | solution.py:46
  37.4 0.3 collective-permute-start.5
  37.8 0.0 copy-done.6
  37.8 3.4 %attend.1 = bf16[16,1024]{1,0:T(8,128)(2,1)} custom-call(bf16[16,256,256]{2,1,0:T(8,128)(2,1)} %bitcast.16, bf16[16,8,128]{2,1,0:T(8,128)(2,1)} %queries_hbm.1, bf16[16,2,256]{2,1,0:T(2,128)(2,1)} %entry_hbm.1, s32[16]{0:T(128)S(1)} %copy-done.6), custom_call_target="tpu_custom_call" | custom-call | flops 4000000000 | bytes 2000000 | tf_op jit(solution)/shard_map/attend/pallas_call | solution.py:280
  41.1 0.0 collective-permute-done.3
  41.2 0.0 collective-permute-done.4
  41.2 0.7 %collective-permute-done.5 = bf16[64,512]{1,0:T(8,128)(2,1)S(1)} collective-permute-done((bf16[64,512]{1,0:T(8,128)(2,1)S(1)}, bf16[64,512]{1,0:T(8,128)(2,1)S(1)}, u32[]{:S(2)}, u32[]{:S(2)}) %collective-permute-start.5) | collective-permute-done | bytes 65568 | tf_op jit(solution)/shard_map/ppermute | solution.py:46
  41.9 0.5 collective-permute-start.6
  42.4 3.5 %collective-permute-start.7 = (bf16[16,512]{1,0:T(8,128)(2,1)S(1)}, bf16[16,512]{1,0:T(8,128)(2,1)S(1)}, u32[]{:S(2)}, u32[]{:S(2)}) collective-permute-start(bf16[16,512]{1,0:T(8,128)(2,1)S(1)} %get-tuple-element.28), channel_id=1, source_target_pairs={{0,8},{4,12},{8,0},{12,4},{1,9},{5,13},{9,1},{13,5},{2,10},{6,14},... | collective-permute-start | bytes 49160 | tf_op jit(solution)/shard_map/ppermute | solution.py:46
  45.9 0.5 collective-permute-start.8
  46.3 0.0 copy-done
  46.3 0.0 copy-done.1
  46.3 0.0 copy-done.2
  46.3 0.0 copy-done.3
  46.3 0.0 copy-done.4
  46.4 0.0 copy-done.5
  46.4 1.8 %state.1 = (bf16[16,1024]{1,0:T(8,128)(2,1)}, f32[16,16,1024]{2,1,0:T(8,128)}) custom-call(bf16[4,96,512]{2,1,0:T(8,128)(2,1)S(1)} %bitcast.9, f32[16,1024]{1,0:T(8,128)S(1)} %get-tuple-element.15.act, bf16[16,1024]{1,0:T(8,128)(2,1)S(1)} %copy-done.3, f32[16,16,1024]{2,1,0:T(8,128)S(1)} %copy-done, bf16[256,1024]{1,0:T(8,128)(2,1)S(1)} %copy-done.1, ...), custom_call_target="tpu_custom_call" | custom-call | flops 3000000000 | bytes 3000000 | tf_op jit(solution)/shard_map/state/pallas_call | solution.py:449
  48.2 0.0 collective-permute-done.6
  48.2 0.0 collective-permute-done.7
  48.2 3.3 %collective-permute-done.8 = bf16[16,512]{1,0:T(8,128)(2,1)S(1)} collective-permute-done((bf16[16,512]{1,0:T(8,128)(2,1)S(1)}, bf16[16,512]{1,0:T(8,128)(2,1)S(1)}, u32[]{:S(2)}, u32[]{:S(2)}) %collective-permute-start.8) | collective-permute-done | bytes 16416 | tf_op jit(solution)/shard_map/ppermute | solution.py:46
  51.4 0.6 %fusion.2 = bf16[16,512]{1,0:T(8,128)(2,1)} fusion(f32[64,512]{1,0:T(8,128)S(1)} %get-tuple-element.25, bf16[16,512]{1,0:T(8,128)(2,1)S(1)} %collective-permute-done.8, bf16[16,512]{1,0:T(8,128)(2,1)S(1)} %collective-permute-done.7, bf16[16,512]{1,0:T(8,128)(2,1)S(1)} %collective-permute-done.6), kind=kLoop, calls=%fused_computation.4 | loop fusion | flops 57344 | bytes 98304 | tf_op jit(solution)/shard_map/convert_element_type | solution.py:532
  (7 shorter events, 0.1 us)
Async XLA Ops:
  1.5 10.8 %collective-permute-start = (bf16[16,640]{1,0:T(8,128)(2,1)S(1)}, bf16[16,640]{1,0:T(8,128)(2,1)S(1)}, u32[]{:S(2)}, u32[]{:S(2)}) collective-permute-start(bf16[16,640]{1,0:T(8,128)(2,1)S(1)} %pack.1.rest_0_), channel_id=1, source_target_pairs={{0,4},{4,0},{8,12},{12,8},{1,5},{5,1},{9,13},{13,9},{2,6},{6,2},{1... | collective-permute-start | bytes 61448 | tf_op jit(solution)/shard_map/ppermute | solution.py:46
  4.6 7.7 %collective-permute-start.1 = (bf16[16,640]{1,0:T(8,128)(2,1)S(1)}, bf16[16,640]{1,0:T(8,128)(2,1)S(1)}, u32[]{:S(2)}, u32[]{:S(2)}) collective-permute-start(bf16[16,640]{1,0:T(8,128)(2,1)S(1)} %pack.1.rest_0_), channel_id=1, source_target_pairs={{0,8},{4,12},{8,0},{12,4},{1,9},{5,13},{9,1},{13,5},{2,10},{6,14},... | collective-permute-start | bytes 61448 | tf_op jit(solution)/shard_map/ppermute | solution.py:46
  7.2 5.6 %collective-permute-start.2 = (bf16[16,640]{1,0:T(8,128)(2,1)S(1)}, bf16[16,640]{1,0:T(8,128)(2,1)S(1)}, u32[]{:S(2)}, u32[]{:S(2)}) collective-permute-start(bf16[16,640]{1,0:T(8,128)(2,1)S(1)} %pack.1.rest_0_), channel_id=1, source_target_pairs={{0,12},{4,8},{8,4},{12,0},{1,13},{5,9},{9,5},{13,1},{2,14},{6,10},... | collective-permute-start | bytes 61448 | tf_op jit(solution)/shard_map/ppermute | solution.py:46
  19.2 18.6 %copy-start.6 = (s32[16]{0:T(128)S(1)}, s32[16]{0:T(128)}, u32[]{:S(2)}) copy-start(s32[16]{0:T(128)} %lengths_ref.1) | copy-start | bytes 196
  35.8 10.6 %copy-start = (f32[16,16,1024]{2,1,0:T(8,128)S(1)}, f32[16,16,1024]{2,1,0:T(8,128)}, u32[]{:S(2)}) copy-start(f32[16,16,1024]{2,1,0:T(8,128)} %scan.1) | copy-start | bytes 3145732
  35.8 10.5 %copy-start.1 = (bf16[256,1024]{1,0:T(8,128)(2,1)S(1)}, bf16[256,1024]{1,0:T(8,128)(2,1)}, u32[]{:S(2)}) copy-start(bf16[256,1024]{1,0:T(8,128)(2,1)} %step_proj.1) | copy-start | bytes 1572868
  35.8 10.5 %copy-start.2 = (f32[16,1024]{1,0:T(8,128)S(1)}, f32[16,1024]{1,0:T(8,128)}, u32[]{:S(2)}) copy-start(f32[16,1024]{1,0:T(8,128)} %decay.1) | copy-start | bytes 196612
  35.8 10.5 %copy-start.3 = (bf16[16,1024]{1,0:T(8,128)(2,1)S(1)}, bf16[16,1024]{1,0:T(8,128)(2,1)}, u32[]{:S(2)}) copy-start(bf16[16,1024]{1,0:T(8,128)(2,1)} %gate.1) | copy-start | bytes 98308
  35.8 10.5 %copy-start.4 = (f32[1024]{0:T(1024)S(1)}, f32[1024]{0:T(1024)}, u32[]{:S(2)}) copy-start(f32[1024]{0:T(1024)} %param.29) | copy-start | bytes 12292
  35.8 10.5 %copy-start.5 = (f32[1024]{0:T(1024)S(1)}, f32[1024]{0:T(1024)}, u32[]{:S(2)}) copy-start(f32[1024]{0:T(1024)} %param.31) | copy-start | bytes 12292
  35.8 5.3 %collective-permute-start.3 = (bf16[64,512]{1,0:T(8,128)(2,1)S(1)}, bf16[64,512]{1,0:T(8,128)(2,1)S(1)}, u32[]{:S(2)}, u32[]{:S(2)}) collective-permute-start(bf16[64,512]{1,0:T(8,128)(2,1)S(1)} %get-tuple-element.21), channel_id=1, source_target_pairs={{0,1},{1,0},{2,3},{3,2},{4,5},{5,4},{6,7},{7,6},{8,9},{9,8},{10,11... | collective-permute-start | bytes 196616 | tf_op jit(solution)/shard_map/ppermute | solution.py:46
  36.3 4.9 %collective-permute-start.4 = (bf16[64,512]{1,0:T(8,128)(2,1)S(1)}, bf16[64,512]{1,0:T(8,128)(2,1)S(1)}, u32[]{:S(2)}, u32[]{:S(2)}) collective-permute-start(bf16[64,512]{1,0:T(8,128)(2,1)S(1)} %get-tuple-element.22), channel_id=1, source_target_pairs={{0,2},{1,3},{2,0},{3,1},{4,6},{5,7},{6,4},{7,5},{8,10},{9,11},{10,... | collective-permute-start | bytes 196616 | tf_op jit(solution)/shard_map/ppermute | solution.py:46
  37.4 4.4 %collective-permute-start.5 = (bf16[64,512]{1,0:T(8,128)(2,1)S(1)}, bf16[64,512]{1,0:T(8,128)(2,1)S(1)}, u32[]{:S(2)}, u32[]{:S(2)}) collective-permute-start(bf16[64,512]{1,0:T(8,128)(2,1)S(1)} %get-tuple-element.23), channel_id=1, source_target_pairs={{0,3},{1,2},{2,1},{3,0},{4,7},{5,6},{6,5},{7,4},{8,11},{9,10},{10,... | collective-permute-start | bytes 196616 | tf_op jit(solution)/shard_map/ppermute | solution.py:46
  41.9 6.3 %collective-permute-start.6 = (bf16[16,512]{1,0:T(8,128)(2,1)S(1)}, bf16[16,512]{1,0:T(8,128)(2,1)S(1)}, u32[]{:S(2)}, u32[]{:S(2)}) collective-permute-start(bf16[16,512]{1,0:T(8,128)(2,1)S(1)} %get-tuple-element.26), channel_id=1, source_target_pairs={{0,4},{4,0},{8,12},{12,8},{1,5},{5,1},{9,13},{13,9},{2,6},{6,2},{1... | collective-permute-start | bytes 49160 | tf_op jit(solution)/shard_map/ppermute | solution.py:46
  42.4 5.8 %collective-permute-start.7 = (bf16[16,512]{1,0:T(8,128)(2,1)S(1)}, bf16[16,512]{1,0:T(8,128)(2,1)S(1)}, u32[]{:S(2)}, u32[]{:S(2)}) collective-permute-start(bf16[16,512]{1,0:T(8,128)(2,1)S(1)} %get-tuple-element.28), channel_id=1, source_target_pairs={{0,8},{4,12},{8,0},{12,4},{1,9},{5,13},{9,1},{13,5},{2,10},{6,14},... | collective-permute-start | bytes 49160 | tf_op jit(solution)/shard_map/ppermute | solution.py:46
  45.9 5.5 %collective-permute-start.8 = (bf16[16,512]{1,0:T(8,128)(2,1)S(1)}, bf16[16,512]{1,0:T(8,128)(2,1)S(1)}, u32[]{:S(2)}, u32[]{:S(2)}) collective-permute-start(bf16[16,512]{1,0:T(8,128)(2,1)S(1)} %get-tuple-element.27), channel_id=1, source_target_pairs={{0,12},{4,8},{8,4},{12,0},{1,13},{5,9},{9,5},{13,1},{2,14},{6,10},... | collective-permute-start | bytes 49160 | tf_op jit(solution)/shard_map/ppermute | solution.py:46

commit v3 on v2

--- a/solution.py
+++ b/solution.py
@@ -102,38 +102,30 @@
         scratch_shapes=scratch_like(*operands) + [
             pltpu.VMEM((LANES, LANES), F32), pltpu.SemaphoreType.DMA((3,)),
         ],
-        compiler_params=limit(4),
+        compiler_params=limit(1),
+        cost_estimate=pl.CostEstimate(
+            flops=60*10**9, bytes_accessed=10**5, transcendentals=0
+        ),
         name="pack",
     )(*off_chip(*operands))
 
 
 def front_kernel(
-    width, ready, chunk,
-    state_hbm, input_hbm, taps_hbm, bias_hbm, proj_hbm, inner_hbm, outer_hbm,
-    act_ref, mix_ref, inner, outer,
+    width,
+    state_hbm, input_hbm, taps_hbm, bias_hbm, proj_hbm,
+    act_ref, mix_ref,
     state, inputs, taps, bias, proj, sems,
 ):
-    small = [
+    copies = [
         pltpu.make_async_copy(src, dst, sems.at[n])
         for n, (src, dst) in enumerate((
             (state_hbm, state), (input_hbm, inputs), (taps_hbm, taps),
             (bias_hbm, bias), (proj_hbm, proj),
         ))
     ]
-    large = []
-    for c in range(ready):
-        span = pl.ds(c * chunk, chunk)
-        for n, (src, dst) in enumerate((
-            (inner_hbm.at[0, 0, span], inner.at[c, 0]),
-            (inner_hbm.at[0, 1, span], inner.at[c, 1]),
-            (outer_hbm.at[0, span], outer.at[c]),
-        )):
-            large.append(
-                pltpu.make_async_copy(src, dst, sems.at[len(small) + 3 * c + n])
-            )
-    for copy in small + large:
+    for copy in copies:
         copy.start()
-    for copy in small[:4]:
+    for copy in copies[:4]:
         copy.wait()
     seqs = inputs.shape[0]
     total = bias[...]
@@ -142,7 +134,7 @@
     total = total + inputs[...].astype(F32) * taps[taps.shape[0] - 1 :, :]
     act = silu(total)
     act_ref[...] = act
-    small[4].wait()
+    copies[4].wait()
     mix = lax.dot_general(
         act.astype(BF16), proj[...], (((1,), (1,)), ((), ())), preferred_element_type=F32
     )
@@ -158,40 +150,54 @@
                 ).astype(BF16)
             mix_ref[row : row + seqs, :] = cut
             row += seqs
-    for copy in large:
-        copy.wait()
-
-
-def front(
-    conv_state, mamba_input, conv_weight, conv_bias, state_proj, inner_weights, outer_weights,
-    width, ready, chunk,
-):
+
+
+def front(conv_state, mamba_input, conv_weight, conv_bias, state_proj, width):
     seqs, channels = mamba_input.shape
-    features = inner_weights.shape[3]
     spans = -(-state_proj.shape[0] // width)
     operands = (
         jnp.swapaxes(conv_state, 0, 1), mamba_input, conv_weight,
         conv_bias.reshape(1, channels), state_proj,
     )
     return pl.pallas_call(
-        functools.partial(front_kernel, width, ready, chunk),
+        functools.partial(front_kernel, width),
         out_shape=(
             pltpu.VMEM((seqs, channels), F32),
             pltpu.VMEM((2 * spans * seqs, width), BF16),
-            pltpu.VMEM((ready, 2, chunk, features), BF16),
-            pltpu.VMEM((ready, chunk, features), BF16),
-        ),
-        in_specs=[HBM_SPEC] * 7,
-        out_specs=(VMEM_SPEC,) * 4,
+        ),
+        in_specs=[HBM_SPEC] * len(operands),
+        out_specs=(VMEM_SPEC,) * 2,
         scratch_shapes=scratch_like(*operands) + [
-            pltpu.SemaphoreType.DMA((len(operands) + 3 * ready,)),
+            pltpu.SemaphoreType.DMA((len(operands),)),
         ],
         compiler_params=limit(4),
         cost_estimate=pl.CostEstimate(
-            flops=4 * 10**9, bytes_accessed=14 * 10**6, transcendentals=0
+            flops=1*10**9, bytes_accessed=10**6, transcendentals=0
         ),
         name="front",
-    )(*off_chip(*operands, inner_weights, outer_weights))
+    )(*off_chip(*operands))
+
+
+def join_kernel(*refs):
+    *blocks, mix, out = refs
+    row = 0
+    for block in blocks:
+        rows = block.shape[0]
+        out[row : row + rows, :] = block[:, : out.shape[1]]
+        row += rows
+    out[row:, :] = mix[...]
+
+
+def join(packed, mix):
+    rows = sum(p.shape[0] for p in packed) + mix.shape[0]
+    return pl.pallas_call(
+        join_kernel,
+        out_shape=pltpu.VMEM((rows, mix.shape[1]), BF16),
+        in_specs=[VMEM_SPEC] * (len(packed) + 1),
+        out_specs=VMEM_SPEC,
+        compiler_params=limit(1),
+        name="join",
+    )(*[on_chip(p) for p in packed], on_chip(mix))
 
 
 def attend_kernel(
@@ -297,61 +303,47 @@
     )(*off_chip(past, queries, new_entry), lengths)
 
 
-def expert_kernel(chunk, ready, peers, ways, gathered, *rest):
+def expert_kernel(chunk, peers, ways, gathered, *rest):
     tables = rest[:peers]
-    inner_ready, outer_ready, inner_hbm, outer_hbm = rest[peers : peers + 4]
-    outs = rest[peers + 4 : peers + 4 + ways]
-    inner, outer, features, hidden, total, sems = rest[peers + 4 + ways :]
-    experts, _, hidden_units, _ = inner_hbm.shape
+    inner, outer = rest[peers : peers + 2]
+    outs = rest[peers + 2 : peers + 2 + ways]
+    features, total = rest[peers + 2 + ways :]
+    experts, _, hidden_units, _ = inner.shape
     count = hidden_units // chunk
+    steps = [(e, slice(c * chunk, (c + 1) * chunk)) for e in range(experts) for c in range(count)]
     tokens = features.shape[0]
     width = gathered.shape[2]
-    copies = []
-    for step in range(ready, experts * count):
-        e, c = divmod(step, count)
-        span = pl.ds(c * chunk, chunk)
-        slot = step - ready
-        copies.append([
-            pltpu.make_async_copy(src, dst, sems.at[slot, n])
-            for n, (src, dst) in enumerate((
-                (inner_hbm.at[e, 0, span], inner.at[slot, 0]),
-                (inner_hbm.at[e, 1, span], inner.at[slot, 1]),
-                (outer_hbm.at[e, span], outer.at[slot]),
-            ))
-        ])
-    for group in copies:
-        for copy in group:
-            copy.start()
     for t in range(ways):
         features[:, t * width : (t + 1) * width] = gathered[t, :tokens, :]
     table = jnp.concatenate([ref[:, width:].astype(F32) for ref in tables], axis=0)
     lane = lax.broadcasted_iota(jnp.int32, table.shape, 1)
     replicas = max(1, peers // EXPERTS)
     first = lax.axis_index("expert") * experts
-    piece = min(256, chunk)
+    gains = []
+    for e in range(experts):
+        name = (first + e) // replicas
+        chosen = (lane == name) | (lane == name + EXPERTS)
+        gains.append(jnp.sum(jnp.where(chosen, table, 0.0), axis=1, keepdims=True))
     contract = (((1,), (1,)), ((), ()))
-    for step in range(experts * count):
-        e, c = divmod(step, count)
-        if c == 0:
-            name = (first + e) // replicas
-            chosen = (lane == name) | (lane == name + EXPERTS)
-            gain = jnp.sum(jnp.where(chosen, table, 0.0), axis=1, keepdims=True)
-        if step < ready:
-            weights, down = inner_ready.at[step], outer_ready.at[step]
-        else:
-            weights, down = inner.at[step - ready], outer.at[step - ready]
-            for copy in copies[step - ready]:
-                copy.wait()
-        for p in range(0, chunk, piece):
-            gate = lax.dot_general(
-                weights[0, p : p + piece], features[...], contract, preferred_element_type=F32
-            )
-            up = lax.dot_general(
-                weights[1, p : p + piece], features[...], contract, preferred_element_type=F32
-            )
-            hidden[p : p + piece, :] = (silu(gate) * up).astype(BF16)
-        value = gain * lax.dot_general(
-            hidden[...], down[...], (((0,), (0,)), ((), ())), preferred_element_type=F32
+
+    def hidden(step):
+        e, span = steps[step]
+        gate = lax.dot_general(
+            inner[e, 0, span], features[...], contract, preferred_element_type=F32
+        )
+        up = lax.dot_general(
+            inner[e, 1, span], features[...], contract, preferred_element_type=F32
+        )
+        return (silu(gate) * up).astype(BF16)
+
+    ahead = hidden(0)
+    for step in range(len(steps)):
+        e, span = steps[step]
+        now = ahead
+        if step + 1 < len(steps):
+            ahead = hidden(step + 1)
+        value = gains[e] * lax.dot_general(
+            now, outer[e, span], (((0,), (0,)), ((), ())), preferred_element_type=F32
         )
         if step == 0:
             total[...] = value
@@ -363,38 +355,33 @@
         outs[step][...] = total[:, pl.ds(start, width)].astype(outs[step].dtype)
 
 
-def run_experts(gathered, packed, inner_ready, outer_ready, inner_weights, outer_weights):
+def run_experts(gathered, packed, inner_weights, outer_weights):
     ways, rows, width = gathered.shape
     peers = len(packed)
     tokens = sum(p.shape[0] for p in packed)
     experts, _, hidden_units, features = inner_weights.shape
-    ready, chunk, _ = outer_ready.shape
-    left = max(1, experts * hidden_units // chunk - ready)
+    chunk = min(512, hidden_units)
     work = 6 * tokens * experts * hidden_units * features
     moved = 2 * (inner_weights.size + outer_weights.size)
     return pl.pallas_call(
-        functools.partial(expert_kernel, chunk, ready, peers, ways),
+        functools.partial(expert_kernel, chunk, peers, ways),
         out_shape=tuple(
             pltpu.VMEM((tokens, width), F32 if step == 0 else BF16) for step in range(ways)
         ),
-        in_specs=[VMEM_SPEC] * (3 + peers) + [HBM_SPEC, HBM_SPEC],
+        in_specs=[VMEM_SPEC] * (3 + peers),
         out_specs=(VMEM_SPEC,) * ways,
         scratch_shapes=[
-            pltpu.VMEM((left, 2, chunk, features), BF16),
-            pltpu.VMEM((left, chunk, features), BF16),
             pltpu.VMEM((tokens, features), BF16),
-            pltpu.VMEM((chunk, tokens), BF16),
             pltpu.VMEM((tokens, features), F32),
-            pltpu.SemaphoreType.DMA((left, 3)),
         ],
-        compiler_params=limit(44),
+        compiler_params=limit(8),
         cost_estimate=pl.CostEstimate(
             flops=work, bytes_accessed=moved, transcendentals=0
         ),
         name="experts",
     )(
-        on_chip(gathered), *[on_chip(p) for p in packed], on_chip(inner_ready),
-        on_chip(outer_ready), *off_chip(inner_weights, outer_weights),
+        on_chip(gathered), *[on_chip(p) for p in packed], on_chip(inner_weights),
+        on_chip(outer_weights),
     )
 
 
@@ -500,20 +487,11 @@
     seqs, width = expert_input.shape
     tokens = peers * seqs
 
-    hidden_units = inner_weights.shape[2]
-    chunk = min(512, hidden_units)
-    ready = min(2, hidden_units // chunk)
-
     packed = exchange([pack(expert_input, routes, gates)] * peers, "expert")
-    act, mix, inner_ready, outer_ready = front(
-        conv_state, mamba_input, conv_weight, conv_bias, state_proj,
-        inner_weights, outer_weights, width, ready, chunk,
-    )
-    mine = jnp.concatenate([p[:, :width] for p in packed] + [mix], axis=0)
+    act, mix = front(conv_state, mamba_input, conv_weight, conv_bias, state_proj, width)
+    mine = join(packed, mix)
     gathered = lax.all_gather(mine, "tensor", axis=0)
-    partial = run_experts(
-        gathered, packed, inner_ready, outer_ready, inner_weights, outer_weights
-    )
+    partial = run_experts(gathered, packed, inner_weights, outer_weights)
 
     arrived = exchange(partial, "tensor")
     attention_out = attend(queries, new_entry, past_entries, lengths)

time: 52.2 us -> 45.9 us (0.88)
  Pallas kernels: 27.6 us -> 20.1 us
  waiting for transfers between devices: 4.41 us -> 5.25 us
    pallas_call x2 -> x3, Pallas kernels: 21.6 us -> 14 us  [the longest x1 11.7 us: run_experts(): pl.pallas_call(functools.partial(expert_kernel, chunk, peers, ways), out_...]
    ppermute x9, waiting for transfers between devices: 4.41 us -> 5.25 us  [exchange(): out[step] = lax.ppermute(blocks[step], axis, pairs)]
  transfers between devices with their start and end apart: 9 -> 9, of which waited for: 3 -> 3; matrix products, arithmetic and copies ran while one was open for 0% -> 0% of each run, Pallas kernels for 20% -> 16%
where the time goes in v3:
time: 45.9 us; the launch traced here: 45.7 us
  Pallas kernels  20.1 us (44%)
  starting transfers between devices  12.1 us (26%)
  blocking collectives  6.59 us (14%)
  waiting for transfers between devices  5.25 us (11%)
  between operations  0.93 us (2%)
  other arithmetic  0.65 us (1%)
    ppermute x9, starting transfers between devices, exchange(): out[step] = lax.ppermute(blocks[step], axis, pairs)  12.1 us
    pallas_call x1, Pallas kernels, run_experts(): pl.pallas_call(functools.partial(expert_kernel, chunk, peers, ways), out_...  11.7 us
    all_gather x1, blocking collectives, shards(): gathered = lax.all_gather(mine, 'tensor', axis=0)  6.59 us
    ppermute x9, waiting for transfers between devices, exchange(): out[step] = lax.ppermute(blocks[step], axis, pairs)  5.25 us
    pallas_call x1, Pallas kernels, attend(): pl.pallas_call(attend_kernel, out_shape=jax.ShapeDtypeStruct((seqs, head_...  3.36 us
    pallas_call x1, Pallas kernels, front(): pl.pallas_call(functools.partial(front_kernel, width), out_shape=(pltpu.V...  2.3 us
    pallas_call x1, Pallas kernels, update_state(): pl.pallas_call(functools.partial(state_kernel, tokens, seqs, low_rank), g...  1.79 us
    pallas_call x1, Pallas kernels, pack(): pl.pallas_call(pack_kernel, out_shape=pltpu.VMEM((seqs, width + LANES), B...  0.95 us
  transfers between devices with their start and end apart: 9, of which 3 were waited for; matrix products, arithmetic and copies ran while one was open for 0% of the time, Pallas kernels for 16%

profile of v3, /device:TPU:0, one launch (start us, length us, event | category | flops | bytes accessed | tf_op | source)
XLA Modules:
  0.0 45.7 jit_solution(9323763575849071211)
XLA Ops:
  0.6 0.0 slice-start
  0.6 0.0 slice-start.1
  0.7 0.0 slice-start.2
  0.7 0.0 slice-start.3
  0.7 0.0 slice-start.4
  0.7 0.0 slice-start.5
  0.7 0.0 slice-start.6
  0.7 0.0 slice-start.7
  0.7 0.0 copy-start
  0.7 1.0 %pack.1.refs_0_.rest_0_ = bf16[16,640]{1,0:T(8,128)(2,1)S(1)} custom-call(bf16[16,512]{1,0:T(8,128)(2,1)} %tokens_hbm.1, s32[2,16]{1,0:T(2,128)} %bitcast.17, f32[2,16]{1,0:T(2,128)} %bitcast.18), custom_call_target="tpu_custom_call" | custom-call | flops 60000002048 | bytes 100000 | tf_op jit(solution)/shard_map/pack/pallas_call | solution.py:97
  1.7 3.1 %collective-permute-start = (bf16[16,640]{1,0:T(8,128)(2,1)S(1)}, bf16[16,640]{1,0:T(8,128)(2,1)S(1)}, u32[]{:S(2)}, u32[]{:S(2)}) collective-permute-start(bf16[16,640]{1,0:T(8,128)(2,1)S(1)} %pack.1.refs_0_.rest_0_), channel_id=1, source_target_pairs={{0,4},{4,0},{8,12},{12,8},{1,5},{5,1},{9,13},{13,9},{2,6},{6,2},{1... | collective-permute-start | bytes 61448 | tf_op jit(solution)/shard_map/ppermute | solution.py:46
  4.8 2.6 %collective-permute-start.1 = (bf16[16,640]{1,0:T(8,128)(2,1)S(1)}, bf16[16,640]{1,0:T(8,128)(2,1)S(1)}, u32[]{:S(2)}, u32[]{:S(2)}) collective-permute-start(bf16[16,640]{1,0:T(8,128)(2,1)S(1)} %pack.1.refs_0_.rest_0_), channel_id=1, source_target_pairs={{0,8},{4,12},{8,0},{12,4},{1,9},{5,13},{9,1},{13,5},{2,10},{6,14},... | collective-permute-start | bytes 61448 | tf_op jit(solution)/shard_map/ppermute | solution.py:46
  7.4 0.0 collective-permute-start.2
  7.4 2.3 %front.1 = (f32[16,1024]{1,0:T(8,128)S(1)}, bf16[32,512]{1,0:T(8,128)(2,1)S(1)}) custom-call(bf16[3,16,1024]{2,1,0:T(8,128)(2,1)} %bitcast.15, bf16[16,1024]{1,0:T(8,128)(2,1)} %input_hbm.1, f32[4,1024]{1,0:T(4,128)} %taps_hbm.1, f32[1,1024]{1,0:T(1,128)} %bitcast.16, bf16[288,1024]{1,0:T(8,128)(2,1)} %proj_hbm.1), custom_call_target="tpu_custom_call" | custom-call | flops 1000000000 | bytes 1000000 | tf_op jit(solution)/shard_map/front/pallas_call | solution.py:162
  9.7 0.0 collective-permute-done.refs_1_.rest_1_
  9.7 0.0 collective-permute-done.1.refs_2_.rest_2_
  9.7 3.2 %collective-permute-done.2.refs_3_.rest_3_ = bf16[16,640]{1,0:T(8,128)(2,1)S(1)} collective-permute-done((bf16[16,640]{1,0:T(8,128)(2,1)S(1)}, bf16[16,640]{1,0:T(8,128)(2,1)S(1)}, u32[]{:S(2)}, u32[]{:S(2)}) %collective-permute-start.2) | collective-permute-done | bytes 20512 | tf_op jit(solution)/shard_map/ppermute | solution.py:46
  13.0 6.6 %all-gather = bf16[384,512]{1,0:T(8,128)(2,1)S(1)} all-gather(bf16[96,512]{1,0:T(8,128)(2,1)S(1)} %join.1), channel_id=2, replica_groups=mesh['parts'=2,'expert'=4,'tensor'=4] {'tensor'}, dimensions={0}, use_global_device_ids=true | all-gather | bytes 491520 | tf_op jit(solution)/shard_map/all_gather | solution.py:493
  19.6 0.0 slice-done
  19.6 0.0 slice-done.1
  19.6 0.0 slice-done.2
  19.6 0.0 slice-done.3
  19.6 0.0 slice-done.4
  19.6 0.0 slice-done.5
  19.6 0.0 slice-done.6
  19.6 0.0 slice-done.7
  19.6 0.0 copy-done
  19.6 0.0 copy-start.7
  19.7 0.0 copy-start.1
  19.7 0.0 copy-start.2
  19.7 0.0 copy-start.3
  19.7 0.0 copy-start.4
  19.7 0.0 copy-start.5
  19.7 0.0 copy-start.6
  19.7 11.7 %experts.1 = (f32[64,512]{1,0:T(8,128)S(1)}, bf16[64,512]{1,0:T(8,128)(2,1)S(1)}, bf16[64,512]{1,0:T(8,128)(2,1)S(1)}, bf16[64,512]{1,0:T(8,128)(2,1)S(1)}) custom-call(bf16[4,96,512]{2,1,0:T(8,128)(2,1)S(1)} %bitcast.10, bf16[16,640]{1,0:T(8,128)(2,1)S(1)} %pack.1.refs_0_.rest_0_, bf16[16,640]{1,0:T(8,128)(2,1)S(1)} %collective-permute-done.refs_1_.rest_1_, ...), custom_call_target="tpu_custom_call" | custom-call | flops 3221225472 | bytes 50331648 | tf_op jit(solution)/shard_map/experts/pallas_call | solution.py:366
  31.5 0.4 collective-permute-start.3
  31.9 1.2 %collective-permute-start.4 = (bf16[64,512]{1,0:T(8,128)(2,1)S(1)}, bf16[64,512]{1,0:T(8,128)(2,1)S(1)}, u32[]{:S(2)}, u32[]{:S(2)}) collective-permute-start(bf16[64,512]{1,0:T(8,128)(2,1)S(1)} %get-tuple-element.18), channel_id=1, source_target_pairs={{0,2},{1,3},{2,0},{3,1},{4,6},{5,7},{6,4},{7,5},{8,10},{9,11},{10,... | collective-permute-start | bytes 196616 | tf_op jit(solution)/shard_map/ppermute | solution.py:46
  33.1 0.3 collective-permute-start.5
  33.4 0.0 copy-done.7
  33.4 3.4 %attend.1 = bf16[16,1024]{1,0:T(8,128)(2,1)} custom-call(bf16[16,256,256]{2,1,0:T(8,128)(2,1)} %bitcast.14, bf16[16,8,128]{2,1,0:T(8,128)(2,1)} %queries_hbm.1, bf16[16,2,256]{2,1,0:T(2,128)(2,1)} %entry_hbm.1, s32[16]{0:T(128)S(1)} %copy-done.7), custom_call_target="tpu_custom_call" | custom-call | flops 4000000000 | bytes 2000000 | tf_op jit(solution)/shard_map/attend/pallas_call | solution.py:286
  36.8 0.0 collective-permute-done.3
  36.8 0.0 collective-permute-done.4
  36.8 0.7 %collective-permute-done.5 = bf16[64,512]{1,0:T(8,128)(2,1)S(1)} collective-permute-done((bf16[64,512]{1,0:T(8,128)(2,1)S(1)}, bf16[64,512]{1,0:T(8,128)(2,1)S(1)}, u32[]{:S(2)}, u32[]{:S(2)}) %collective-permute-start.5) | collective-permute-done | bytes 65568 | tf_op jit(solution)/shard_map/ppermute | solution.py:46
  37.5 0.1 collective-permute-start.6
  37.6 2.0 %collective-permute-start.7 = (bf16[16,512]{1,0:T(8,128)(2,1)S(1)}, bf16[16,512]{1,0:T(8,128)(2,1)S(1)}, u32[]{:S(2)}, u32[]{:S(2)}) collective-permute-start(bf16[16,512]{1,0:T(8,128)(2,1)S(1)} %get-tuple-element.24), channel_id=1, source_target_pairs={{0,8},{4,12},{8,0},{12,4},{1,9},{5,13},{9,1},{13,5},{2,10},{6,14},... | collective-permute-start | bytes 49160 | tf_op jit(solution)/shard_map/ppermute | solution.py:46
  39.6 2.4 %collective-permute-start.8 = (bf16[16,512]{1,0:T(8,128)(2,1)S(1)}, bf16[16,512]{1,0:T(8,128)(2,1)S(1)}, u32[]{:S(2)}, u32[]{:S(2)}) collective-permute-start(bf16[16,512]{1,0:T(8,128)(2,1)S(1)} %get-tuple-element.23), channel_id=1, source_target_pairs={{0,12},{4,8},{8,4},{12,0},{1,13},{5,9},{9,5},{13,1},{2,14},{6,10},... | collective-permute-start | bytes 49160 | tf_op jit(solution)/shard_map/ppermute | solution.py:46
  42.0 0.0 copy-done.1
  42.0 0.0 copy-done.2
  42.0 0.0 copy-done.3
  42.0 0.0 copy-done.4
  42.0 0.0 copy-done.5
  42.0 0.0 copy-done.6
  42.0 1.8 %state.1 = (bf16[16,1024]{1,0:T(8,128)(2,1)}, f32[16,16,1024]{2,1,0:T(8,128)}) custom-call(bf16[4,96,512]{2,1,0:T(8,128)(2,1)S(1)} %bitcast.11, f32[16,1024]{1,0:T(8,128)S(1)} %get-tuple-element.13.act, bf16[16,1024]{1,0:T(8,128)(2,1)S(1)} %copy-done.4, f32[16,16,1024]{2,1,0:T(8,128)S(1)} %copy-done.1, bf16[256,1024]{1,0:T(8,128)(2,1)S(1)} %copy-done.2, ...), custom_call_target="tpu_custom_call" | custom-call | flops 3000000000 | bytes 3000000 | tf_op jit(solution)/shard_map/state/pallas_call | solution.py:436
  43.8 0.0 collective-permute-done.6
  43.8 0.0 collective-permute-done.7
  43.8 1.3 %collective-permute-done.8 = bf16[16,512]{1,0:T(8,128)(2,1)S(1)} collective-permute-done((bf16[16,512]{1,0:T(8,128)(2,1)S(1)}, bf16[16,512]{1,0:T(8,128)(2,1)S(1)}, u32[]{:S(2)}, u32[]{:S(2)}) %collective-permute-start.8) | collective-permute-done | bytes 16416 | tf_op jit(solution)/shard_map/ppermute | solution.py:46
  45.1 0.6 %fusion.2 = bf16[16,512]{1,0:T(8,128)(2,1)} fusion(f32[64,512]{1,0:T(8,128)S(1)} %get-tuple-element.21, bf16[16,512]{1,0:T(8,128)(2,1)S(1)} %collective-permute-done.8, bf16[16,512]{1,0:T(8,128)(2,1)S(1)} %collective-permute-done.7, bf16[16,512]{1,0:T(8,128)(2,1)S(1)} %collective-permute-done.6), kind=kLoop, calls=%fused_computation.4 | loop fusion | flops 57344 | bytes 98304 | tf_op jit(solution)/shard_map/convert_element_type | solution.py:510
  (4 shorter events, 0.1 us)
Async XLA Ops:
  0.6 18.9 %slice-start = ((s8[33554432]{0:T(1024)(128)(4,1)}), s8[4194304]{0:T(1024)(128)(4,1)S(1)}, s32[]{:S(2)}) async-start(s8[33554432]{0:T(1024)(128)(4,1)} %bitcast.8), calls=%async_computation | async-start | bytes 8388608
  0.6 18.9 %slice-start.1 = ((s8[33554432]{0:T(1024)(128)(4,1)}), s8[4194304]{0:T(1024)(128)(4,1)S(1)}, s32[]{:S(2)}) async-start(s8[33554432]{0:T(1024)(128)(4,1)} %bitcast.8), calls=%async_computation.1 | async-start | bytes 8388608
  0.7 18.9 %slice-start.2 = ((s8[33554432]{0:T(1024)(128)(4,1)}), s8[4194304]{0:T(1024)(128)(4,1)S(1)}, s32[]{:S(2)}) async-start(s8[33554432]{0:T(1024)(128)(4,1)} %bitcast.8), calls=%async_computation.2 | async-start | bytes 8388608
  0.7 18.9 %slice-start.3 = ((s8[33554432]{0:T(1024)(128)(4,1)}), s8[4194304]{0:T(1024)(128)(4,1)S(1)}, s32[]{:S(2)}) async-start(s8[33554432]{0:T(1024)(128)(4,1)} %bitcast.8), calls=%async_computation.3 | async-start | bytes 8388608
  0.7 18.9 %slice-start.4 = ((s8[33554432]{0:T(1024)(128)(4,1)}), s8[4194304]{0:T(1024)(128)(4,1)S(1)}, s32[]{:S(2)}) async-start(s8[33554432]{0:T(1024)(128)(4,1)} %bitcast.8), calls=%async_computation.4 | async-start | bytes 8388608
  0.7 18.9 %slice-start.5 = ((s8[33554432]{0:T(1024)(128)(4,1)}), s8[4194304]{0:T(1024)(128)(4,1)S(1)}, s32[]{:S(2)}) async-start(s8[33554432]{0:T(1024)(128)(4,1)} %bitcast.8), calls=%async_computation.5 | async-start | bytes 8388608
  0.7 18.9 %slice-start.6 = ((s8[33554432]{0:T(1024)(128)(4,1)}), s8[4194304]{0:T(1024)(128)(4,1)S(1)}, s32[]{:S(2)}) async-start(s8[33554432]{0:T(1024)(128)(4,1)} %bitcast.8), calls=%async_computation.6 | async-start | bytes 8388608
  0.7 18.9 %slice-start.7 = ((s8[33554432]{0:T(1024)(128)(4,1)}), s8[4194304]{0:T(1024)(128)(4,1)S(1)}, s32[]{:S(2)}) async-start(s8[33554432]{0:T(1024)(128)(4,1)} %bitcast.8), calls=%async_computation.7 | async-start | bytes 8388608
  0.7 18.9 %copy-start = (bf16[2,2048,2048]{2,1,0:T(8,128)(2,1)S(1)}, bf16[2,2048,2048]{2,1,0:T(8,128)(2,1)}, u32[]{:S(2)}) copy-start(bf16[2,2048,2048]{2,1,0:T(8,128)(2,1)} %rest_5_.1) | copy-start | bytes 50331652
  1.7 8.0 %collective-permute-start = (bf16[16,640]{1,0:T(8,128)(2,1)S(1)}, bf16[16,640]{1,0:T(8,128)(2,1)S(1)}, u32[]{:S(2)}, u32[]{:S(2)}) collective-permute-start(bf16[16,640]{1,0:T(8,128)(2,1)S(1)} %pack.1.refs_0_.rest_0_), channel_id=1, source_target_pairs={{0,4},{4,0},{8,12},{12,8},{1,5},{5,1},{9,13},{13,9},{2,6},{6,2},{1... | collective-permute-start | bytes 61448 | tf_op jit(solution)/shard_map/ppermute | solution.py:46
  4.8 4.9 %collective-permute-start.1 = (bf16[16,640]{1,0:T(8,128)(2,1)S(1)}, bf16[16,640]{1,0:T(8,128)(2,1)S(1)}, u32[]{:S(2)}, u32[]{:S(2)}) collective-permute-start(bf16[16,640]{1,0:T(8,128)(2,1)S(1)} %pack.1.refs_0_.rest_0_), channel_id=1, source_target_pairs={{0,8},{4,12},{8,0},{12,4},{1,9},{5,13},{9,1},{13,5},{2,10},{6,14},... | collective-permute-start | bytes 61448 | tf_op jit(solution)/shard_map/ppermute | solution.py:46
  7.4 5.6 %collective-permute-start.2 = (bf16[16,640]{1,0:T(8,128)(2,1)S(1)}, bf16[16,640]{1,0:T(8,128)(2,1)S(1)}, u32[]{:S(2)}, u32[]{:S(2)}) collective-permute-start(bf16[16,640]{1,0:T(8,128)(2,1)S(1)} %pack.1.refs_0_.rest_0_), channel_id=1, source_target_pairs={{0,12},{4,8},{8,4},{12,0},{1,13},{5,9},{9,5},{13,1},{2,14},{6,10},... | collective-permute-start | bytes 61448 | tf_op jit(solution)/shard_map/ppermute | solution.py:46
  19.6 13.7 %copy-start.7 = (s32[16]{0:T(128)S(1)}, s32[16]{0:T(128)}, u32[]{:S(2)}) copy-start(s32[16]{0:T(128)} %lengths_ref.1) | copy-start | bytes 196
  19.7 22.3 %copy-start.1 = (f32[16,16,1024]{2,1,0:T(8,128)S(1)}, f32[16,16,1024]{2,1,0:T(8,128)}, u32[]{:S(2)}) copy-start(f32[16,16,1024]{2,1,0:T(8,128)} %scan.1) | copy-start | bytes 3145732
  19.7 22.3 %copy-start.2 = (bf16[256,1024]{1,0:T(8,128)(2,1)S(1)}, bf16[256,1024]{1,0:T(8,128)(2,1)}, u32[]{:S(2)}) copy-start(bf16[256,1024]{1,0:T(8,128)(2,1)} %step_proj.1) | copy-start | bytes 1572868
  19.7 22.3 %copy-start.3 = (f32[16,1024]{1,0:T(8,128)S(1)}, f32[16,1024]{1,0:T(8,128)}, u32[]{:S(2)}) copy-start(f32[16,1024]{1,0:T(8,128)} %decay.1) | copy-start | bytes 196612
  19.7 22.3 %copy-start.4 = (bf16[16,1024]{1,0:T(8,128)(2,1)S(1)}, bf16[16,1024]{1,0:T(8,128)(2,1)}, u32[]{:S(2)}) copy-start(bf16[16,1024]{1,0:T(8,128)(2,1)} %gate.1) | copy-start | bytes 98308
  19.7 22.3 %copy-start.5 = (f32[1024]{0:T(1024)S(1)}, f32[1024]{0:T(1024)}, u32[]{:S(2)}) copy-start(f32[1024]{0:T(1024)} %param.29) | copy-start | bytes 12292
  19.7 22.3 %copy-start.6 = (f32[1024]{0:T(1024)S(1)}, f32[1024]{0:T(1024)}, u32[]{:S(2)}) copy-start(f32[1024]{0:T(1024)} %param.31) | copy-start | bytes 12292
  31.5 5.3 %collective-permute-start.3 = (bf16[64,512]{1,0:T(8,128)(2,1)S(1)}, bf16[64,512]{1,0:T(8,128)(2,1)S(1)}, u32[]{:S(2)}, u32[]{:S(2)}) collective-permute-start(bf16[64,512]{1,0:T(8,128)(2,1)S(1)} %get-tuple-element.17), channel_id=1, source_target_pairs={{0,1},{1,0},{2,3},{3,2},{4,5},{5,4},{6,7},{7,6},{8,9},{9,8},{10,11... | collective-permute-start | bytes 196616 | tf_op jit(solution)/shard_map/ppermute | solution.py:46
  31.9 4.9 %collective-permute-start.4 = (bf16[64,512]{1,0:T(8,128)(2,1)S(1)}, bf16[64,512]{1,0:T(8,128)(2,1)S(1)}, u32[]{:S(2)}, u32[]{:S(2)}) collective-permute-start(bf16[64,512]{1,0:T(8,128)(2,1)S(1)} %get-tuple-element.18), channel_id=1, source_target_pairs={{0,2},{1,3},{2,0},{3,1},{4,6},{5,7},{6,4},{7,5},{8,10},{9,11},{10,... | collective-permute-start | bytes 196616 | tf_op jit(solution)/shard_map/ppermute | solution.py:46
  33.1 4.4 %collective-permute-start.5 = (bf16[64,512]{1,0:T(8,128)(2,1)S(1)}, bf16[64,512]{1,0:T(8,128)(2,1)S(1)}, u32[]{:S(2)}, u32[]{:S(2)}) collective-permute-start(bf16[64,512]{1,0:T(8,128)(2,1)S(1)} %get-tuple-element.19), channel_id=1, source_target_pairs={{0,3},{1,2},{2,1},{3,0},{4,7},{5,6},{6,5},{7,4},{8,11},{9,10},{10,... | collective-permute-start | bytes 196616 | tf_op jit(solution)/shard_map/ppermute | solution.py:46
  37.5 6.3 %collective-permute-start.6 = (bf16[16,512]{1,0:T(8,128)(2,1)S(1)}, bf16[16,512]{1,0:T(8,128)(2,1)S(1)}, u32[]{:S(2)}, u32[]{:S(2)}) collective-permute-start(bf16[16,512]{1,0:T(8,128)(2,1)S(1)} %get-tuple-element.22), channel_id=1, source_target_pairs={{0,4},{4,0},{8,12},{12,8},{1,5},{5,1},{9,13},{13,9},{2,6},{6,2},{1... | collective-permute-start | bytes 49160 | tf_op jit(solution)/shard_map/ppermute | solution.py:46
  37.6 6.2 %collective-permute-start.7 = (bf16[16,512]{1,0:T(8,128)(2,1)S(1)}, bf16[16,512]{1,0:T(8,128)(2,1)S(1)}, u32[]{:S(2)}, u32[]{:S(2)}) collective-permute-start(bf16[16,512]{1,0:T(8,128)(2,1)S(1)} %get-tuple-element.24), channel_id=1, source_target_pairs={{0,8},{4,12},{8,0},{12,4},{1,9},{5,13},{9,1},{13,5},{2,10},{6,14},... | collective-permute-start | bytes 49160 | tf_op jit(solution)/shard_map/ppermute | solution.py:46
  39.6 5.5 %collective-permute-start.8 = (bf16[16,512]{1,0:T(8,128)(2,1)S(1)}, bf16[16,512]{1,0:T(8,128)(2,1)S(1)}, u32[]{:S(2)}, u32[]{:S(2)}) collective-permute-start(bf16[16,512]{1,0:T(8,128)(2,1)S(1)} %get-tuple-element.23), channel_id=1, source_target_pairs={{0,12},{4,8},{8,4},{12,0},{1,13},{5,9},{9,5},{13,1},{2,14},{6,10},... | collective-permute-start | bytes 49160 | tf_op jit(solution)/shard_map/ppermute | solution.py:46

commit v4 on v3

--- a/solution.py
+++ b/solution.py
@@ -7,6 +7,7 @@
 from jax.experimental.pallas import tpu as pltpu
 from jax.sharding import PartitionSpec as P
 
+
 EXPERTS = 8
 LANES = 128
 F32 = jnp.float32
@@ -18,11 +19,6 @@
 
 def silu(v):
     return v / (1.0 + jnp.exp(-v))
-
-
-def split_bf16(v):
-    high = v.astype(BF16)
-    return high, (v - high.astype(F32)).astype(BF16)
 
 
 def partner(index, step, count):
@@ -141,7 +137,7 @@
     outputs = mix.shape[1]
     spans = -(-outputs // width)
     row = 0
-    for piece in split_bf16(mix):
+    for piece in (mix.astype(BF16),):
         for span in range(spans):
             cut = piece[:, span * width : min(outputs, (span + 1) * width)]
             if cut.shape[1] < width:
@@ -163,7 +159,7 @@
         functools.partial(front_kernel, width),
         out_shape=(
             pltpu.VMEM((seqs, channels), F32),
-            pltpu.VMEM((2 * spans * seqs, width), BF16),
+            pltpu.VMEM((spans * seqs, width), BF16),
         ),
         in_specs=[HBM_SPEC] * len(operands),
         out_specs=(VMEM_SPEC,) * 2,
@@ -201,27 +197,13 @@
 
 
 def attend_kernel(
-    past_hbm, queries_hbm, entry_hbm, lengths_ref, out_hbm,
-    past, queries, entry, scores, own, heads, out, sems,
+    past, queries, entry, lengths_ref, out_hbm,
+    scores, own, heads, out, sem,
 ):
     seqs, head_count, size = queries.shape
     groups = entry.shape[1]
     per_group = head_count // groups
     positions = past.shape[1] // groups
-    parts = 4 if seqs % 4 == 0 else 1
-    part = seqs // parts
-    small = [
-        pltpu.make_async_copy(queries_hbm, queries, sems.at[parts]),
-        pltpu.make_async_copy(entry_hbm, entry, sems.at[parts + 1]),
-    ]
-    large = [
-        pltpu.make_async_copy(
-            past_hbm.at[pl.ds(n * part, part)], past.at[pl.ds(n * part, part)], sems.at[n]
-        )
-        for n in range(parts)
-    ]
-    for copy in small + large:
-        copy.start()
     scaling = size ** (-0.5)
     group_of = lambda lanes: lax.broadcasted_iota(jnp.int32, (head_count, lanes), 0) // per_group
     position = lax.broadcasted_iota(jnp.int32, (head_count, positions), 1)
@@ -241,21 +223,17 @@
             group_of(size),
         )
 
-    for copy in small:
-        copy.wait()
-    for n in range(parts):
-        large[n].wait()
-        for s in range(n * part, (n + 1) * part):
-            every = lax.dot_general(
-                queries[s], past[s, :, :size], (((1,), (1,)), ((), ())),
-                preferred_element_type=F32,
-            )
-            mine = pick(
-                [every[:, g * positions : (g + 1) * positions] for g in range(groups)],
-                group_of(positions),
-            )
-            scores[s] = jnp.where(position < lengths_ref[s], mine * scaling, -jnp.inf)
-            own[s] = queries[s].astype(F32) * entry_rows(s, slice(0, size))
+    for s in range(seqs):
+        every = lax.dot_general(
+            queries[s], past[s, :, :size], (((1,), (1,)), ((), ())),
+            preferred_element_type=F32,
+        )
+        mine = pick(
+            [every[:, g * positions : (g + 1) * positions] for g in range(groups)],
+            group_of(positions),
+        )
+        scores[s] = jnp.where(position < lengths_ref[s], mine * scaling, -jnp.inf)
+        own[s] = queries[s].astype(F32) * entry_rows(s, slice(0, size))
     score = scores[...]
     own_score = jnp.sum(own[...], axis=2, keepdims=True) * scaling
     highest = jnp.maximum(jnp.max(score, axis=2, keepdims=True), own_score)
@@ -274,7 +252,7 @@
         heads[s] = mixed + own[s].astype(BF16).astype(F32) * entry_rows(s, slice(size, None))
     for h in range(head_count):
         out[:, h * size : (h + 1) * size] = heads[:, h, :].astype(BF16)
-    store = pltpu.make_async_copy(out, out_hbm, sems.at[parts + 2])
+    store = pltpu.make_async_copy(out, out_hbm, sem)
     store.start()
     store.wait()
 
@@ -286,103 +264,115 @@
     return pl.pallas_call(
         attend_kernel,
         out_shape=jax.ShapeDtypeStruct((seqs, head_count * size), BF16),
-        in_specs=[HBM_SPEC, HBM_SPEC, HBM_SPEC, pl.BlockSpec(memory_space=pltpu.SMEM)],
+        in_specs=[VMEM_SPEC] * 3 + [pl.BlockSpec(memory_space=pltpu.SMEM)],
         out_specs=HBM_SPEC,
-        scratch_shapes=scratch_like(past, queries, new_entry) + [
+        scratch_shapes=[
             pltpu.VMEM((seqs, head_count, positions), F32),
             pltpu.VMEM((seqs, head_count, size), F32),
             pltpu.VMEM((seqs, head_count, size), F32),
             pltpu.VMEM((seqs, head_count * size), BF16),
-            pltpu.SemaphoreType.DMA((8,)),
+            pltpu.SemaphoreType.DMA,
         ],
-        compiler_params=limit(8),
+        compiler_params=limit(4),
         cost_estimate=pl.CostEstimate(
             flops=4 * 10**9, bytes_accessed=2 * 10**6, transcendentals=0
         ),
         name="attend",
-    )(*off_chip(past, queries, new_entry), lengths)
-
-
-def expert_kernel(chunk, peers, ways, gathered, *rest):
-    tables = rest[:peers]
-    inner, outer = rest[peers : peers + 2]
-    outs = rest[peers + 2 : peers + 2 + ways]
-    features, total = rest[peers + 2 + ways :]
-    experts, _, hidden_units, _ = inner.shape
-    count = hidden_units // chunk
-    steps = [(e, slice(c * chunk, (c + 1) * chunk)) for e in range(experts) for c in range(count)]
-    tokens = features.shape[0]
-    width = gathered.shape[2]
-    for t in range(ways):
-        features[:, t * width : (t + 1) * width] = gathered[t, :tokens, :]
+    )(on_chip(past), on_chip(queries), on_chip(new_entry), lengths)
+
+
+def weight_columns(tables, width, experts, peers):
     table = jnp.concatenate([ref[:, width:].astype(F32) for ref in tables], axis=0)
     lane = lax.broadcasted_iota(jnp.int32, table.shape, 1)
     replicas = max(1, peers // EXPERTS)
     first = lax.axis_index("expert") * experts
-    gains = []
+    columns = []
     for e in range(experts):
         name = (first + e) // replicas
         chosen = (lane == name) | (lane == name + EXPERTS)
-        gains.append(jnp.sum(jnp.where(chosen, table, 0.0), axis=1, keepdims=True))
+        columns.append(jnp.sum(jnp.where(chosen, table, 0.0), axis=1, keepdims=True))
+    return columns
+
+
+def project_down(hidden, outer, gains, outs, steps, ways, width):
+    me = lax.axis_index("tensor")
+    for out, step in zip(outs, steps):
+        start = pl.multiple_of(partner(me, step, ways) * width, LANES)
+        total = None
+        for e, gain in enumerate(gains):
+            value = gain * lax.dot_general(
+                hidden[e], outer[e, :, pl.ds(start, width)], (((0,), (0,)), ((), ())),
+                preferred_element_type=F32,
+            )
+            total = value if total is None else total + value
+        out[...] = total.astype(out.dtype)
+
+
+def hidden_kernel(chunk, gathered, inner, hidden, features):
+    experts, _, hidden_units, _ = inner.shape
+    ways, _, width = gathered.shape
+    tokens = features.shape[0]
+    for t in range(ways):
+        features[:, t * width : (t + 1) * width] = gathered[t, :tokens, :]
     contract = (((1,), (1,)), ((), ()))
-
-    def hidden(step):
-        e, span = steps[step]
-        gate = lax.dot_general(
-            inner[e, 0, span], features[...], contract, preferred_element_type=F32
-        )
-        up = lax.dot_general(
-            inner[e, 1, span], features[...], contract, preferred_element_type=F32
-        )
-        return (silu(gate) * up).astype(BF16)
-
-    ahead = hidden(0)
-    for step in range(len(steps)):
-        e, span = steps[step]
-        now = ahead
-        if step + 1 < len(steps):
-            ahead = hidden(step + 1)
-        value = gains[e] * lax.dot_general(
-            now, outer[e, span], (((0,), (0,)), ((), ())), preferred_element_type=F32
-        )
-        if step == 0:
-            total[...] = value
-        else:
-            total[...] += value
-    me = lax.axis_index("tensor")
-    for step in range(ways):
-        start = pl.multiple_of(partner(me, step, ways) * width, LANES)
-        outs[step][...] = total[:, pl.ds(start, width)].astype(outs[step].dtype)
+    for e in range(experts):
+        for c in range(0, hidden_units, chunk):
+            span = slice(c, c + chunk)
+            gate = lax.dot_general(
+                inner[e, 0, span], features[...], contract, preferred_element_type=F32
+            )
+            up = lax.dot_general(
+                inner[e, 1, span], features[...], contract, preferred_element_type=F32
+            )
+            hidden[e, span] = (silu(gate) * up).astype(BF16)
+
+
+def down_kernel(peers, ways, steps, hidden, outer, *rest):
+    tables, outs = rest[:peers], rest[peers:]
+    width = outs[0].shape[1]
+    gains = weight_columns(tables, width, outer.shape[0], peers)
+    project_down(hidden, outer, gains, outs, steps, ways, width)
 
 
 def run_experts(gathered, packed, inner_weights, outer_weights):
-    ways, rows, width = gathered.shape
+    ways, _, width = gathered.shape
     peers = len(packed)
     tokens = sum(p.shape[0] for p in packed)
     experts, _, hidden_units, features = inner_weights.shape
     chunk = min(512, hidden_units)
-    work = 6 * tokens * experts * hidden_units * features
-    moved = 2 * (inner_weights.size + outer_weights.size)
-    return pl.pallas_call(
-        functools.partial(expert_kernel, chunk, peers, ways),
-        out_shape=tuple(
-            pltpu.VMEM((tokens, width), F32 if step == 0 else BF16) for step in range(ways)
-        ),
-        in_specs=[VMEM_SPEC] * (3 + peers),
-        out_specs=(VMEM_SPEC,) * ways,
-        scratch_shapes=[
-            pltpu.VMEM((tokens, features), BF16),
-            pltpu.VMEM((tokens, features), F32),
-        ],
-        compiler_params=limit(8),
+    work = 2 * tokens * experts * hidden_units * features
+    hidden = pl.pallas_call(
+        functools.partial(hidden_kernel, chunk),
+        out_shape=pltpu.VMEM((experts, hidden_units, tokens), BF16),
+        in_specs=[VMEM_SPEC] * 2,
+        out_specs=VMEM_SPEC,
+        scratch_shapes=[pltpu.VMEM((tokens, features), BF16)],
+        compiler_params=limit(6),
         cost_estimate=pl.CostEstimate(
-            flops=work, bytes_accessed=moved, transcendentals=0
-        ),
-        name="experts",
-    )(
-        on_chip(gathered), *[on_chip(p) for p in packed], on_chip(inner_weights),
-        on_chip(outer_weights),
-    )
+            flops=10**8, bytes_accessed=10**5, transcendentals=0
+        ),
+        name="hidden",
+    )(on_chip(gathered), on_chip(inner_weights))
+    operands = (on_chip(hidden), on_chip(outer_weights), *[on_chip(p) for p in packed])
+
+    def down(steps):
+        return pl.pallas_call(
+            functools.partial(down_kernel, peers, ways, steps),
+            out_shape=tuple(
+                pltpu.VMEM((tokens, width), F32 if step == 0 else BF16) for step in steps
+            ),
+            in_specs=[VMEM_SPEC] * len(operands),
+            out_specs=(VMEM_SPEC,) * len(steps),
+            compiler_params=limit(6),
+            cost_estimate=pl.CostEstimate(
+                flops=work // 2, bytes_accessed=outer_weights.size, transcendentals=0
+            ),
+        )(*operands)
+
+    half = max(1, ways // 2)
+    far = down(list(range(half, ways)))
+    near = down(list(range(half)))
+    return [*near, *far]
 
 
 def state_kernel(
@@ -391,17 +381,16 @@
     out, next_state,
     square,
 ):
-    ways, rows, width = gathered.shape
+    ways, rows, _ = gathered.shape
     states = decay.shape[0]
-    spans = (rows - tokens) // (2 * seqs)
+    spans = (rows - tokens) // seqs
     pieces = []
     for span in range(spans):
         piece = None
         for t in range(ways):
-            for half in range(2):
-                row = tokens + (half * spans + span) * seqs
-                part = gathered[t, row : row + seqs, :].astype(F32)
-                piece = part if piece is None else piece + part
+            row = tokens + span * seqs
+            part = gathered[t, row : row + seqs, :].astype(F32)
+            piece = part if piece is None else piece + part
         pieces.append(piece)
     mixing = pieces[0] if spans == 1 else jnp.concatenate(pieces, axis=1)
     square[...] = jnp.zeros_like(square)
@@ -483,7 +472,6 @@
 ):
     del slots
     peers = lax.axis_size("expert")
-    ways = lax.axis_size("tensor")
     seqs, width = expert_input.shape
     tokens = peers * seqs
 

time: 45.9 us -> 45.3 us (0.987)
  Pallas kernels: 20.1 us -> 18.9 us
  waiting for transfers between devices: 5.25 us -> 6.04 us
    pallas_call x1, Pallas kernels: 3.36 us -> 1.86 us  [attend(): pl.pallas_call(attend_kernel, out_shape=jax.ShapeDtypeStruct((seqs, head_...]
    ppermute x9, waiting for transfers between devices: 5.25 us -> 6.04 us  [exchange(): out[step] = lax.ppermute(blocks[step], axis, pairs)]
    pallas_call x1 -> x3, Pallas kernels: 11.7 us -> 12 us  [the longest x1 8.81 us: run_experts(): pl.pallas_call(functools.partial(hidden_kernel, chunk), out_shape=pltpu.V...]
  transfers between devices with their start and end apart: 9 -> 9, of which waited for: 3 -> 4; matrix products, arithmetic and copies ran while one was open for 0% -> 0% of each run, Pallas kernels for 16% -> 17%
where the time goes in v4:
time: 45.3 us; the launch traced here: 45.1 us
  Pallas kernels  18.9 us (42%)
  starting transfers between devices  12.2 us (27%)
  blocking collectives  6.22 us (14%)
  waiting for transfers between devices  6.04 us (13%)
  between operations  1 us (2%)
  other arithmetic  0.65 us (1%)
    ppermute x9, starting transfers between devices, exchange(): out[step] = lax.ppermute(blocks[step], axis, pairs)  12.2 us
    pallas_call x1, Pallas kernels, run_experts(): pl.pallas_call(functools.partial(hidden_kernel, chunk), out_shape=pltpu.V...  8.81 us
    all_gather x1, blocking collectives, shards(): gathered = lax.all_gather(mine, 'tensor', axis=0)  6.22 us
    ppermute x9, waiting for transfers between devices, exchange(): out[step] = lax.ppermute(blocks[step], axis, pairs)  6.04 us
    pallas_call x2, Pallas kernels, down(): pl.pallas_call(functools.partial(down_kernel, peers, ways, steps), out_sh...  3.22 us
    pallas_call x1, Pallas kernels, front(): pl.pallas_call(functools.partial(front_kernel, width), out_shape=(pltpu.V...  2.3 us
    pallas_call x1, Pallas kernels, attend(): pl.pallas_call(attend_kernel, out_shape=jax.ShapeDtypeStruct((seqs, head_...  1.86 us
    pallas_call x1, Pallas kernels, update_state(): pl.pallas_call(functools.partial(state_kernel, tokens, seqs, low_rank), g...  1.79 us
  transfers between devices with their start and end apart: 9, of which 4 were waited for; matrix products, arithmetic and copies ran while one was open for 0% of the time, Pallas kernels for 17%

profile of v4, /device:TPU:0, one launch (start us, length us, event | category | flops | bytes accessed | tf_op | source)
XLA Modules:
  0.0 45.1 jit_solution(5681220595189843417)
XLA Ops:
  0.6 0.0 slice-start.4
  0.6 0.0 slice-start.5
  0.7 0.0 slice-start.6
  0.7 0.0 slice-start.7
  0.7 0.0 slice-start.8
  0.7 0.0 slice-start.9
  0.7 0.0 slice-start.10
  0.7 0.0 slice-start.11
  0.7 1.0 %pack.1.refs_0_.rest_0_ = bf16[16,640]{1,0:T(8,128)(2,1)S(1)} custom-call(bf16[16,512]{1,0:T(8,128)(2,1)} %tokens_hbm.1, s32[2,16]{1,0:T(2,128)} %bitcast.19, f32[2,16]{1,0:T(2,128)} %bitcast.20), custom_call_target="tpu_custom_call" | custom-call | flops 60000002048 | bytes 100000 | tf_op jit(solution)/shard_map/pack/pallas_call | solution.py:93
  1.7 3.1 %collective-permute-start = (bf16[16,640]{1,0:T(8,128)(2,1)S(1)}, bf16[16,640]{1,0:T(8,128)(2,1)S(1)}, u32[]{:S(2)}, u32[]{:S(2)}) collective-permute-start(bf16[16,640]{1,0:T(8,128)(2,1)S(1)} %pack.1.refs_0_.rest_0_), channel_id=1, source_target_pairs={{0,4},{4,0},{8,12},{12,8},{1,5},{5,1},{9,13},{13,9},{2,6},{6,2},{1... | collective-permute-start | bytes 61448 | tf_op jit(solution)/shard_map/ppermute | solution.py:42
  4.8 2.6 %collective-permute-start.1 = (bf16[16,640]{1,0:T(8,128)(2,1)S(1)}, bf16[16,640]{1,0:T(8,128)(2,1)S(1)}, u32[]{:S(2)}, u32[]{:S(2)}) collective-permute-start(bf16[16,640]{1,0:T(8,128)(2,1)S(1)} %pack.1.refs_0_.rest_0_), channel_id=1, source_target_pairs={{0,8},{4,12},{8,0},{12,4},{1,9},{5,13},{9,1},{13,5},{2,10},{6,14},... | collective-permute-start | bytes 61448 | tf_op jit(solution)/shard_map/ppermute | solution.py:42
  7.4 0.0 collective-permute-start.2
  7.4 2.3 %front.1 = (f32[16,1024]{1,0:T(8,128)S(1)}, bf16[16,512]{1,0:T(8,128)(2,1)S(1)}) custom-call(bf16[3,16,1024]{2,1,0:T(8,128)(2,1)} %bitcast.17, bf16[16,1024]{1,0:T(8,128)(2,1)} %input_hbm.1, f32[4,1024]{1,0:T(4,128)} %taps_hbm.1, f32[1,1024]{1,0:T(1,128)} %bitcast.18, bf16[288,1024]{1,0:T(8,128)(2,1)} %proj_hbm.1), custom_call_target="tpu_custom_call" | custom-call | flops 1000000000 | bytes 1000000 | tf_op jit(solution)/shard_map/front/pallas_call | solution.py:158
  9.7 0.0 collective-permute-done.refs_1_.rest_1_
  9.7 0.0 collective-permute-done.1.refs_2_.rest_2_
  9.7 3.2 %collective-permute-done.2.refs_3_.rest_3_ = bf16[16,640]{1,0:T(8,128)(2,1)S(1)} collective-permute-done((bf16[16,640]{1,0:T(8,128)(2,1)S(1)}, bf16[16,640]{1,0:T(8,128)(2,1)S(1)}, u32[]{:S(2)}, u32[]{:S(2)}) %collective-permute-start.2) | collective-permute-done | bytes 20512 | tf_op jit(solution)/shard_map/ppermute | solution.py:42
  13.0 6.2 %all-gather = bf16[320,512]{1,0:T(8,128)(2,1)S(1)} all-gather(bf16[80,512]{1,0:T(8,128)(2,1)S(1)} %join.1), channel_id=2, replica_groups=mesh['parts'=2,'expert'=4,'tensor'=4] {'tensor'}, dimensions={0}, use_global_device_ids=true | all-gather | bytes 409600 | tf_op jit(solution)/shard_map/all_gather | solution.py:481
  19.2 0.0 slice-done.4
  19.2 0.0 slice-done.5
  19.2 0.0 slice-done.6
  19.2 0.0 slice-done.7
  19.2 0.0 slice-done.8
  19.2 0.0 slice-done.9
  19.2 0.0 slice-done.10
  19.2 0.0 slice-done.11
  19.3 0.0 slice-start.1
  19.3 0.0 slice-start.2
  19.3 0.0 slice-start.3
  19.3 8.8 %hidden.1 = bf16[2,2048,64]{2,1,0:T(8,128)(2,1)S(1)} custom-call(bf16[4,80,512]{2,1,0:T(8,128)(2,1)S(1)} %bitcast.12, bf16[2,2,2048,2048]{3,2,1,0:T(8,128)(2,1)S(1)} %bitcast.11), custom_call_target="tpu_custom_call" | custom-call | flops 100000000 | bytes 100000 | tf_op jit(solution)/shard_map/hidden/pallas_call | solution.py:344
  28.1 0.0 slice-done
  28.1 0.0 slice-done.1
  28.1 0.0 slice-done.2
  28.1 0.0 slice-done.3
  28.2 0.0 copy-start
  28.2 0.0 copy-start.4
  28.2 0.0 copy-start.6
  28.2 0.0 copy-start.9
  28.2 1.6 %shard_map.219 = (f32[64,512]{1,0:T(8,128)S(1)}, bf16[64,512]{1,0:T(8,128)(2,1)S(1)}) custom-call(bf16[2,2048,64]{2,1,0:T(8,128)(2,1)S(1)} %hidden.1, bf16[2,2048,2048]{2,1,0:T(8,128)(2,1)S(1)} %bitcast.9, bf16[16,640]{1,0:T(8,128)(2,1)S(1)} %pack.1.refs_0_.rest_0_, bf16[16,640]{1,0:T(8,128)(2,1)S(1)} %collective-permute-done.refs_1_.rest_1_, ...), custom_call_target="tpu_custom_call" | custom-call | flops 536870912 | bytes 8388608 | tf_op jit(solution)/shard_map/pallas_call | solution.py:359
  29.8 0.0 copy-start.1
  29.8 0.0 copy-start.2
  29.8 0.0 copy-start.3
  29.9 0.0 copy-start.5
  29.9 0.0 copy-start.7
  29.9 0.0 copy-start.8
  29.9 0.4 collective-permute-start.3
  30.3 1.6 %shard_map.220 = (bf16[64,512]{1,0:T(8,128)(2,1)S(1)}, bf16[64,512]{1,0:T(8,128)(2,1)S(1)}) custom-call(bf16[2,2048,64]{2,1,0:T(8,128)(2,1)S(1)} %hidden.1, bf16[2,2048,2048]{2,1,0:T(8,128)(2,1)S(1)} %bitcast.9, bf16[16,640]{1,0:T(8,128)(2,1)S(1)} %pack.1.refs_0_.rest_0_, bf16[16,640]{1,0:T(8,128)(2,1)S(1)} %collective-permute-done.refs_1_.rest_1_, ...), custom_call_target="tpu_custom_call" | custom-call | flops 536870912 | bytes 8388608 | tf_op jit(solution)/shard_map/pallas_call | solution.py:359
  32.0 1.4 %collective-permute-start.4 = (bf16[64,512]{1,0:T(8,128)(2,1)S(1)}, bf16[64,512]{1,0:T(8,128)(2,1)S(1)}, u32[]{:S(2)}, u32[]{:S(2)}) collective-permute-start(bf16[64,512]{1,0:T(8,128)(2,1)S(1)} %get-tuple-element.18), channel_id=1, source_target_pairs={{0,2},{1,3},{2,0},{3,1},{4,6},{5,7},{6,4},{7,5},{8,10},{9,11},{10,... | collective-permute-start | bytes 196616 | tf_op jit(solution)/shard_map/ppermute | solution.py:42
  33.4 0.2 collective-permute-start.5
  33.5 0.0 copy-done
  33.5 1.9 %attend.1 = bf16[16,1024]{1,0:T(8,128)(2,1)} custom-call(bf16[16,256,256]{2,1,0:T(8,128)(2,1)S(1)} %bitcast.14, bf16[16,8,128]{2,1,0:T(8,128)(2,1)S(1)} %copy-done.4, bf16[16,2,256]{2,1,0:T(2,128)(2,1)S(1)} %copy-done.6, s32[16]{0:T(128)S(1)} %copy-done.9), custom_call_target="tpu_custom_call" | custom-call | flops 4000000000 | bytes 2000000 | tf_op jit(solution)/shard_map/attend/pallas_call | solution.py:264
  35.4 0.0 collective-permute-done.3
  35.4 0.9 %collective-permute-done.4 = bf16[64,512]{1,0:T(8,128)(2,1)S(1)} collective-permute-done((bf16[64,512]{1,0:T(8,128)(2,1)S(1)}, bf16[64,512]{1,0:T(8,128)(2,1)S(1)}, u32[]{:S(2)}, u32[]{:S(2)}) %collective-permute-start.4) | collective-permute-done | bytes 65568 | tf_op jit(solution)/shard_map/ppermute | solution.py:42
  36.3 1.4 %collective-permute-done.5 = bf16[64,512]{1,0:T(8,128)(2,1)S(1)} collective-permute-done((bf16[64,512]{1,0:T(8,128)(2,1)S(1)}, bf16[64,512]{1,0:T(8,128)(2,1)S(1)}, u32[]{:S(2)}, u32[]{:S(2)}) %collective-permute-start.5) | collective-permute-done | bytes 65568 | tf_op jit(solution)/shard_map/ppermute | solution.py:42
  37.8 0.1 collective-permute-start.6
  37.8 1.1 %collective-permute-start.7 = (bf16[16,512]{1,0:T(8,128)(2,1)S(1)}, bf16[16,512]{1,0:T(8,128)(2,1)S(1)}, u32[]{:S(2)}, u32[]{:S(2)}) collective-permute-start(bf16[16,512]{1,0:T(8,128)(2,1)S(1)} %get-tuple-element.24), channel_id=1, source_target_pairs={{0,8},{4,12},{8,0},{12,4},{1,9},{5,13},{9,1},{13,5},{2,10},{6,14},... | collective-permute-start | bytes 49160 | tf_op jit(solution)/shard_map/ppermute | solution.py:42
  39.0 3.2 %collective-permute-start.8 = (bf16[16,512]{1,0:T(8,128)(2,1)S(1)}, bf16[16,512]{1,0:T(8,128)(2,1)S(1)}, u32[]{:S(2)}, u32[]{:S(2)}) collective-permute-start(bf16[16,512]{1,0:T(8,128)(2,1)S(1)} %get-tuple-element.23), channel_id=1, source_target_pairs={{0,12},{4,8},{8,4},{12,0},{1,13},{5,9},{9,5},{13,1},{2,14},{6,10},... | collective-permute-start | bytes 49160 | tf_op jit(solution)/shard_map/ppermute | solution.py:42
  42.2 0.0 copy-done.1
  42.2 0.0 copy-done.7
  42.2 0.0 copy-done.8
  42.3 1.8 %state.1 = (bf16[16,1024]{1,0:T(8,128)(2,1)}, f32[16,16,1024]{2,1,0:T(8,128)}) custom-call(bf16[4,80,512]{2,1,0:T(8,128)(2,1)S(1)} %bitcast.13, f32[16,1024]{1,0:T(8,128)S(1)} %get-tuple-element.13.act, bf16[16,1024]{1,0:T(8,128)(2,1)S(1)} %copy-done.5, f32[16,16,1024]{2,1,0:T(8,128)S(1)} %copy-done.1, bf16[256,1024]{1,0:T(8,128)(2,1)S(1)} %copy-done.2, ...), custom_call_target="tpu_custom_call" | custom-call | flops 3000000000 | bytes 3000000 | tf_op jit(solution)/shard_map/state/pallas_call | solution.py:425
  44.0 0.0 collective-permute-done.6
  44.0 0.0 collective-permute-done.7
  44.0 0.5 %collective-permute-done.8 = bf16[16,512]{1,0:T(8,128)(2,1)S(1)} collective-permute-done((bf16[16,512]{1,0:T(8,128)(2,1)S(1)}, bf16[16,512]{1,0:T(8,128)(2,1)S(1)}, u32[]{:S(2)}, u32[]{:S(2)}) %collective-permute-start.8) | collective-permute-done | bytes 16416 | tf_op jit(solution)/shard_map/ppermute | solution.py:42
  44.5 0.6 %fusion.2 = bf16[16,512]{1,0:T(8,128)(2,1)} fusion(f32[64,512]{1,0:T(8,128)S(1)} %get-tuple-element.21, bf16[16,512]{1,0:T(8,128)(2,1)S(1)} %collective-permute-done.8, bf16[16,512]{1,0:T(8,128)(2,1)S(1)} %collective-permute-done.7, bf16[16,512]{1,0:T(8,128)(2,1)S(1)} %collective-permute-done.6), kind=kLoop, calls=%fused_computation.4 | loop fusion | flops 57344 | bytes 98304 | tf_op jit(solution)/shard_map/convert_element_type | solution.py:498
  (12 shorter events, 0.1 us)
Async XLA Ops:
  0.6 18.6 %slice-start.4 = ((s8[33554432]{0:T(1024)(128)(4,1)}), s8[4194304]{0:T(1024)(128)(4,1)S(1)}, s32[]{:S(2)}) async-start(s8[33554432]{0:T(1024)(128)(4,1)} %bitcast.10), calls=%async_computation.4 | async-start | bytes 8388608
  0.6 18.6 %slice-start.5 = ((s8[33554432]{0:T(1024)(128)(4,1)}), s8[4194304]{0:T(1024)(128)(4,1)S(1)}, s32[]{:S(2)}) async-start(s8[33554432]{0:T(1024)(128)(4,1)} %bitcast.10), calls=%async_computation.5 | async-start | bytes 8388608
  0.7 18.5 %slice-start.6 = ((s8[33554432]{0:T(1024)(128)(4,1)}), s8[4194304]{0:T(1024)(128)(4,1)S(1)}, s32[]{:S(2)}) async-start(s8[33554432]{0:T(1024)(128)(4,1)} %bitcast.10), calls=%async_computation.6 | async-start | bytes 8388608
  0.7 18.5 %slice-start.7 = ((s8[33554432]{0:T(1024)(128)(4,1)}), s8[4194304]{0:T(1024)(128)(4,1)S(1)}, s32[]{:S(2)}) async-start(s8[33554432]{0:T(1024)(128)(4,1)} %bitcast.10), calls=%async_computation.7 | async-start | bytes 8388608
  0.7 18.5 %slice-start.8 = ((s8[33554432]{0:T(1024)(128)(4,1)}), s8[4194304]{0:T(1024)(128)(4,1)S(1)}, s32[]{:S(2)}) async-start(s8[33554432]{0:T(1024)(128)(4,1)} %bitcast.10), calls=%async_computation.8 | async-start | bytes 8388608
  0.7 18.5 %slice-start.9 = ((s8[33554432]{0:T(1024)(128)(4,1)}), s8[4194304]{0:T(1024)(128)(4,1)S(1)}, s32[]{:S(2)}) async-start(s8[33554432]{0:T(1024)(128)(4,1)} %bitcast.10), calls=%async_computation.9 | async-start | bytes 8388608
  0.7 18.5 %slice-start.10 = ((s8[33554432]{0:T(1024)(128)(4,1)}), s8[4194304]{0:T(1024)(128)(4,1)S(1)}, s32[]{:S(2)}) async-start(s8[33554432]{0:T(1024)(128)(4,1)} %bitcast.10), calls=%async_computation.10 | async-start | bytes 8388608
  0.7 18.5 %slice-start.11 = ((s8[33554432]{0:T(1024)(128)(4,1)}), s8[4194304]{0:T(1024)(128)(4,1)S(1)}, s32[]{:S(2)}) async-start(s8[33554432]{0:T(1024)(128)(4,1)} %bitcast.10), calls=%async_computation.11 | async-start | bytes 8388608
  1.7 8.0 %collective-permute-start = (bf16[16,640]{1,0:T(8,128)(2,1)S(1)}, bf16[16,640]{1,0:T(8,128)(2,1)S(1)}, u32[]{:S(2)}, u32[]{:S(2)}) collective-permute-start(bf16[16,640]{1,0:T(8,128)(2,1)S(1)} %pack.1.refs_0_.rest_0_), channel_id=1, source_target_pairs={{0,4},{4,0},{8,12},{12,8},{1,5},{5,1},{9,13},{13,9},{2,6},{6,2},{1... | collective-permute-start | bytes 61448 | tf_op jit(solution)/shard_map/ppermute | solution.py:42
  4.8 4.9 %collective-permute-start.1 = (bf16[16,640]{1,0:T(8,128)(2,1)S(1)}, bf16[16,640]{1,0:T(8,128)(2,1)S(1)}, u32[]{:S(2)}, u32[]{:S(2)}) collective-permute-start(bf16[16,640]{1,0:T(8,128)(2,1)S(1)} %pack.1.refs_0_.rest_0_), channel_id=1, source_target_pairs={{0,8},{4,12},{8,0},{12,4},{1,9},{5,13},{9,1},{13,5},{2,10},{6,14},... | collective-permute-start | bytes 61448 | tf_op jit(solution)/shard_map/ppermute | solution.py:42
  7.4 5.6 %collective-permute-start.2 = (bf16[16,640]{1,0:T(8,128)(2,1)S(1)}, bf16[16,640]{1,0:T(8,128)(2,1)S(1)}, u32[]{:S(2)}, u32[]{:S(2)}) collective-permute-start(bf16[16,640]{1,0:T(8,128)(2,1)S(1)} %pack.1.refs_0_.rest_0_), channel_id=1, source_target_pairs={{0,12},{4,8},{8,4},{12,0},{1,13},{5,9},{9,5},{13,1},{2,14},{6,10},... | collective-permute-start | bytes 61448 | tf_op jit(solution)/shard_map/ppermute | solution.py:42
  7.4 20.7 %slice-start = ((s8[16777216]{0:T(1024)(128)(4,1)}), s8[4194304]{0:T(1024)(128)(4,1)S(1)}, s32[]{:S(2)}) async-start(s8[16777216]{0:T(1024)(128)(4,1)} %bitcast.8), calls=%async_computation | async-start | bytes 8388608
  19.3 8.9 %slice-start.1 = ((s8[16777216]{0:T(1024)(128)(4,1)}), s8[4194304]{0:T(1024)(128)(4,1)S(1)}, s32[]{:S(2)}) async-start(s8[16777216]{0:T(1024)(128)(4,1)} %bitcast.8), calls=%async_computation.1 | async-start | bytes 8388608
  19.3 8.9 %slice-start.2 = ((s8[16777216]{0:T(1024)(128)(4,1)}), s8[4194304]{0:T(1024)(128)(4,1)S(1)}, s32[]{:S(2)}) async-start(s8[16777216]{0:T(1024)(128)(4,1)} %bitcast.8), calls=%async_computation.2 | async-start | bytes 8388608
  19.3 8.9 %slice-start.3 = ((s8[16777216]{0:T(1024)(128)(4,1)}), s8[4194304]{0:T(1024)(128)(4,1)S(1)}, s32[]{:S(2)}) async-start(s8[16777216]{0:T(1024)(128)(4,1)} %bitcast.8), calls=%async_computation.3 | async-start | bytes 8388608
  28.2 5.4 %copy-start = (bf16[16,2,128,256]{3,2,1,0:T(8,128)(2,1)S(1)}, bf16[16,2,128,256]{3,2,1,0:T(8,128)(2,1)}, u32[]{:S(2)}) copy-start(bf16[16,2,128,256]{3,2,1,0:T(8,128)(2,1)} %param.34) | copy-start | bytes 6291460
  28.2 5.4 %copy-start.4 = (bf16[16,8,128]{2,1,0:T(8,128)(2,1)S(1)}, bf16[16,8,128]{2,1,0:T(8,128)(2,1)}, u32[]{:S(2)}) copy-start(bf16[16,8,128]{2,1,0:T(8,128)(2,1)} %queries.1) | copy-start | bytes 98308
  28.2 5.4 %copy-start.6 = (bf16[16,2,256]{2,1,0:T(2,128)(2,1)S(1)}, bf16[16,2,256]{2,1,0:T(2,128)(2,1)}, u32[]{:S(2)}) copy-start(bf16[16,2,256]{2,1,0:T(2,128)(2,1)} %entry.1) | copy-start | bytes 49156
  28.2 5.3 %copy-start.9 = (s32[16]{0:T(128)S(1)}, s32[16]{0:T(128)}, u32[]{:S(2)}) copy-start(s32[16]{0:T(128)} %lengths_ref.1) | copy-start | bytes 196
  29.8 12.4 %copy-start.1 = (f32[16,16,1024]{2,1,0:T(8,128)S(1)}, f32[16,16,1024]{2,1,0:T(8,128)}, u32[]{:S(2)}) copy-start(f32[16,16,1024]{2,1,0:T(8,128)} %scan.1) | copy-start | bytes 3145732
  29.8 12.4 %copy-start.2 = (bf16[256,1024]{1,0:T(8,128)(2,1)S(1)}, bf16[256,1024]{1,0:T(8,128)(2,1)}, u32[]{:S(2)}) copy-start(bf16[256,1024]{1,0:T(8,128)(2,1)} %step_proj.1) | copy-start | bytes 1572868
  29.8 12.4 %copy-start.3 = (f32[16,1024]{1,0:T(8,128)S(1)}, f32[16,1024]{1,0:T(8,128)}, u32[]{:S(2)}) copy-start(f32[16,1024]{1,0:T(8,128)} %decay.1) | copy-start | bytes 196612
  29.9 12.4 %copy-start.5 = (bf16[16,1024]{1,0:T(8,128)(2,1)S(1)}, bf16[16,1024]{1,0:T(8,128)(2,1)}, u32[]{:S(2)}) copy-start(bf16[16,1024]{1,0:T(8,128)(2,1)} %gate.1) | copy-start | bytes 98308
  29.9 12.4 %copy-start.7 = (f32[1024]{0:T(1024)S(1)}, f32[1024]{0:T(1024)}, u32[]{:S(2)}) copy-start(f32[1024]{0:T(1024)} %param.29) | copy-start | bytes 12292
  29.9 12.4 %copy-start.8 = (f32[1024]{0:T(1024)S(1)}, f32[1024]{0:T(1024)}, u32[]{:S(2)}) copy-start(f32[1024]{0:T(1024)} %param.31) | copy-start | bytes 12292
  29.9 5.5 %collective-permute-start.3 = (bf16[64,512]{1,0:T(8,128)(2,1)S(1)}, bf16[64,512]{1,0:T(8,128)(2,1)S(1)}, u32[]{:S(2)}, u32[]{:S(2)}) collective-permute-start(bf16[64,512]{1,0:T(8,128)(2,1)S(1)} %get-tuple-element.17), channel_id=1, source_target_pairs={{0,1},{1,0},{2,3},{3,2},{4,5},{5,4},{6,7},{7,6},{8,9},{9,8},{10,11... | collective-permute-start | bytes 196616 | tf_op jit(solution)/shard_map/ppermute | solution.py:42
  32.0 4.3 %collective-permute-start.4 = (bf16[64,512]{1,0:T(8,128)(2,1)S(1)}, bf16[64,512]{1,0:T(8,128)(2,1)S(1)}, u32[]{:S(2)}, u32[]{:S(2)}) collective-permute-start(bf16[64,512]{1,0:T(8,128)(2,1)S(1)} %get-tuple-element.18), channel_id=1, source_target_pairs={{0,2},{1,3},{2,0},{3,1},{4,6},{5,7},{6,4},{7,5},{8,10},{9,11},{10,... | collective-permute-start | bytes 196616 | tf_op jit(solution)/shard_map/ppermute | solution.py:42
  33.4 4.3 %collective-permute-start.5 = (bf16[64,512]{1,0:T(8,128)(2,1)S(1)}, bf16[64,512]{1,0:T(8,128)(2,1)S(1)}, u32[]{:S(2)}, u32[]{:S(2)}) collective-permute-start(bf16[64,512]{1,0:T(8,128)(2,1)S(1)} %get-tuple-element.19), channel_id=1, source_target_pairs={{0,3},{1,2},{2,1},{3,0},{4,7},{5,6},{6,5},{7,4},{8,11},{9,10},{10,... | collective-permute-start | bytes 196616 | tf_op jit(solution)/shard_map/ppermute | solution.py:42
  37.8 6.3 %collective-permute-start.6 = (bf16[16,512]{1,0:T(8,128)(2,1)S(1)}, bf16[16,512]{1,0:T(8,128)(2,1)S(1)}, u32[]{:S(2)}, u32[]{:S(2)}) collective-permute-start(bf16[16,512]{1,0:T(8,128)(2,1)S(1)} %get-tuple-element.22), channel_id=1, source_target_pairs={{0,4},{4,0},{8,12},{12,8},{1,5},{5,1},{9,13},{13,9},{2,6},{6,2},{1... | collective-permute-start | bytes 49160 | tf_op jit(solution)/shard_map/ppermute | solution.py:42
  37.8 6.2 %collective-permute-start.7 = (bf16[16,512]{1,0:T(8,128)(2,1)S(1)}, bf16[16,512]{1,0:T(8,128)(2,1)S(1)}, u32[]{:S(2)}, u32[]{:S(2)}) collective-permute-start(bf16[16,512]{1,0:T(8,128)(2,1)S(1)} %get-tuple-element.24), channel_id=1, source_target_pairs={{0,8},{4,12},{8,0},{12,4},{1,9},{5,13},{9,1},{13,5},{2,10},{6,14},... | collective-permute-start | bytes 49160 | tf_op jit(solution)/shard_map/ppermute | solution.py:42
  39.0 5.5 %collective-permute-start.8 = (bf16[16,512]{1,0:T(8,128)(2,1)S(1)}, bf16[16,512]{1,0:T(8,128)(2,1)S(1)}, u32[]{:S(2)}, u32[]{:S(2)}) collective-permute-start(bf16[16,512]{1,0:T(8,128)(2,1)S(1)} %get-tuple-element.23), channel_id=1, source_target_pairs={{0,12},{4,8},{8,4},{12,0},{1,13},{5,9},{9,5},{13,1},{2,14},{6,10},... | collective-permute-start | bytes 49160 | tf_op jit(solution)/shard_map/ppermute | solution.py:42

commit v5 on v4

--- a/solution.py
+++ b/solution.py
@@ -168,7 +168,7 @@
         ],
         compiler_params=limit(4),
         cost_estimate=pl.CostEstimate(
-            flops=1*10**9, bytes_accessed=10**6, transcendentals=0
+            flops=10*10**9, bytes_accessed=10**6, transcendentals=0
         ),
         name="front",
     )(*off_chip(*operands))
@@ -197,8 +197,8 @@
 
 
 def attend_kernel(
-    past, queries, entry, lengths_ref, out_hbm,
-    scores, own, heads, out, sem,
+    past, queries, entry, lengths_ref, out,
+    scores, own, heads,
 ):
     seqs, head_count, size = queries.shape
     groups = entry.shape[1]
@@ -252,9 +252,6 @@
         heads[s] = mixed + own[s].astype(BF16).astype(F32) * entry_rows(s, slice(size, None))
     for h in range(head_count):
         out[:, h * size : (h + 1) * size] = heads[:, h, :].astype(BF16)
-    store = pltpu.make_async_copy(out, out_hbm, sem)
-    store.start()
-    store.wait()
 
 
 def attend(queries, new_entry, past_entries, lengths):
@@ -263,15 +260,13 @@
     positions = past_entries.shape[2]
     return pl.pallas_call(
         attend_kernel,
-        out_shape=jax.ShapeDtypeStruct((seqs, head_count * size), BF16),
+        out_shape=pltpu.VMEM((seqs, head_count * size), BF16),
         in_specs=[VMEM_SPEC] * 3 + [pl.BlockSpec(memory_space=pltpu.SMEM)],
-        out_specs=HBM_SPEC,
+        out_specs=VMEM_SPEC,
         scratch_shapes=[
             pltpu.VMEM((seqs, head_count, positions), F32),
             pltpu.VMEM((seqs, head_count, size), F32),
             pltpu.VMEM((seqs, head_count, size), F32),
-            pltpu.VMEM((seqs, head_count * size), BF16),
-            pltpu.SemaphoreType.DMA,
         ],
         compiler_params=limit(4),
         cost_estimate=pl.CostEstimate(
@@ -339,7 +334,7 @@
     peers = len(packed)
     tokens = sum(p.shape[0] for p in packed)
     experts, _, hidden_units, features = inner_weights.shape
-    chunk = min(512, hidden_units)
+    chunk = min(1024, hidden_units)
     work = 2 * tokens * experts * hidden_units * features
     hidden = pl.pallas_call(
         functools.partial(hidden_kernel, chunk),
@@ -377,10 +372,11 @@
 
 def state_kernel(
     tokens, seqs, low_rank,
-    gathered, act, gate, scan, step_proj, step_bias, decay, skip,
-    out, next_state,
+    gathered, act, gate, scan, step_proj, step_bias, decay, skip, attended,
+    out, next_state, attended_out,
     square,
 ):
+    attended_out[...] = attended[...]
     ways, rows, _ = gathered.shape
     states = decay.shape[0]
     spans = (rows - tokens) // seqs
@@ -415,26 +411,32 @@
 
 
 def update_state(
-    gathered, tokens, act, mamba_gate, scan_state, step_proj, step_bias, decay_log, skip_gain
+    gathered, tokens, act, mamba_gate, scan_state, step_proj, step_bias, decay_log, skip_gain,
+    attended,
 ):
     seqs, states, channels = scan_state.shape
     low_rank = step_proj.shape[0]
     block = min(512, channels)
     lane_block = lambda rows: pl.BlockSpec((rows, block), lambda c: (0, c))
     state_block = pl.BlockSpec((seqs, states, block), lambda c: (0, 0, c))
+    attended_block = pl.BlockSpec(
+        (seqs, attended.shape[1] // (channels // block)), lambda c: (0, c)
+    )
     return pl.pallas_call(
         functools.partial(state_kernel, tokens, seqs, low_rank),
         grid=(channels // block,),
         out_shape=(
             jax.ShapeDtypeStruct((seqs, channels), BF16),
             jax.ShapeDtypeStruct(scan_state.shape, F32),
+            jax.ShapeDtypeStruct(attended.shape, BF16),
         ),
         in_specs=[
             pl.BlockSpec(gathered.shape, lambda c: (0, 0, 0)),
             lane_block(seqs), lane_block(seqs), state_block,
             lane_block(low_rank), lane_block(1), lane_block(states), lane_block(1),
+            attended_block,
         ],
-        out_specs=(lane_block(seqs), state_block),
+        out_specs=(lane_block(seqs), state_block, attended_block),
         scratch_shapes=[pltpu.VMEM((LANES, LANES), F32)],
         compiler_params=limit(12),
         cost_estimate=pl.CostEstimate(
@@ -444,6 +446,7 @@
     )(
         gathered, act, mamba_gate, scan_state, step_proj,
         step_bias.reshape(1, channels), decay_log, skip_gain.reshape(1, channels),
+        on_chip(attended),
     )
 
 
@@ -482,12 +485,13 @@
     partial = run_experts(gathered, packed, inner_weights, outer_weights)
 
     arrived = exchange(partial, "tensor")
-    attention_out = attend(queries, new_entry, past_entries, lengths)
+    attended = attend(queries, new_entry, past_entries, lengths)
     share = arrived[0]
     for part in arrived[1:]:
         share = share + part.astype(F32)
-    mamba_out, next_state = update_state(
-        gathered, tokens, act, mamba_gate, scan_state, step_proj, step_bias, decay_log, skip_gain
+    mamba_out, next_state, attention_out = update_state(
+        gathered, tokens, act, mamba_gate, scan_state, step_proj, step_bias, decay_log, skip_gain,
+        attended,
     )
     blocks = [share[n * seqs : (n + 1) * seqs] for n in range(peers)]
     blocks = [blocks[0]] + [block.astype(BF16) for block in blocks[1:]]

time: 45.3 us -> 45.3 us (level)
  Pallas kernels: 18.9 us -> 18.3 us
  waiting for transfers between devices: 6.04 us -> 6.6 us
    pallas_call x1, Pallas kernels: 1.86 us -> 1.23 us  [attend(): pl.pallas_call(attend_kernel, out_shape=pltpu.VMEM((seqs, head_count * si...]
    ppermute x9, waiting for transfers between devices: 6.04 us -> 6.6 us  [exchange(): out[step] = lax.ppermute(blocks[step], axis, pairs)]
  transfers between devices with their start and end apart: 9 -> 9, of which waited for: 4 -> 4; matrix products, arithmetic and copies ran while one was open for 0% -> 0% of each run, Pallas kernels for 17% -> 15%
where the time goes in v5:
time: 45.3 us; the launch traced here: 45.1 us
  Pallas kernels  18.3 us (40%)
  starting transfers between devices  12.2 us (27%)
  waiting for transfers between devices  6.6 us (15%)
  blocking collectives  6.22 us (14%)
  between operations  0.99 us (2%)
  other arithmetic  0.65 us (1%)
    ppermute x9, starting transfers between devices, exchange(): out[step] = lax.ppermute(blocks[step], axis, pairs)  12.2 us
    pallas_call x1, Pallas kernels, run_experts(): pl.pallas_call(functools.partial(hidden_kernel, chunk), out_shape=pltpu.V...  8.81 us
    ppermute x9, waiting for transfers between devices, exchange(): out[step] = lax.ppermute(blocks[step], axis, pairs)  6.6 us
    all_gather x1, blocking collectives, shards(): gathered = lax.all_gather(mine, 'tensor', axis=0)  6.22 us
    pallas_call x2, Pallas kernels, down(): pl.pallas_call(functools.partial(down_kernel, peers, ways, steps), out_sh...  3.22 us
    pallas_call x1, Pallas kernels, front(): pl.pallas_call(functools.partial(front_kernel, width), out_shape=(pltpu.V...  2.28 us
    pallas_call x1, Pallas kernels, update_state(): pl.pallas_call(functools.partial(state_kernel, tokens, seqs, low_rank), g...  1.83 us
    pallas_call x1, Pallas kernels, attend(): pl.pallas_call(attend_kernel, out_shape=pltpu.VMEM((seqs, head_count * si...  1.23 us
  transfers between devices with their start and end apart: 9, of which 4 were waited for; matrix products, arithmetic and copies ran while one was open for 0% of the time, Pallas kernels for 15%

profile of v5, /device:TPU:0, one launch (start us, length us, event | category | flops | bytes accessed | tf_op | source)
XLA Modules:
  0.0 45.1 jit_solution(5927191832872812056)
XLA Ops:
  0.6 0.0 slice-start.4
  0.6 0.0 slice-start.5
  0.7 0.0 slice-start.6
  0.7 0.0 slice-start.7
  0.7 0.0 slice-start.8
  0.7 0.0 slice-start.9
  0.7 0.0 slice-start.10
  0.7 1.0 %pack.1.refs_0_.rest_0_ = bf16[16,640]{1,0:T(8,128)(2,1)S(1)} custom-call(bf16[16,512]{1,0:T(8,128)(2,1)} %tokens_hbm.1, s32[2,16]{1,0:T(2,128)} %bitcast.19, f32[2,16]{1,0:T(2,128)} %bitcast.20), custom_call_target="tpu_custom_call" | custom-call | flops 60000002048 | bytes 100000 | tf_op jit(solution)/shard_map/pack/pallas_call | solution.py:93
  1.7 3.1 %collective-permute-start = (bf16[16,640]{1,0:T(8,128)(2,1)S(1)}, bf16[16,640]{1,0:T(8,128)(2,1)S(1)}, u32[]{:S(2)}, u32[]{:S(2)}) collective-permute-start(bf16[16,640]{1,0:T(8,128)(2,1)S(1)} %pack.1.refs_0_.rest_0_), channel_id=1, source_target_pairs={{0,4},{4,0},{8,12},{12,8},{1,5},{5,1},{9,13},{13,9},{2,6},{6,2},{1... | collective-permute-start | bytes 61448 | tf_op jit(solution)/shard_map/ppermute | solution.py:42
  4.8 2.6 %collective-permute-start.1 = (bf16[16,640]{1,0:T(8,128)(2,1)S(1)}, bf16[16,640]{1,0:T(8,128)(2,1)S(1)}, u32[]{:S(2)}, u32[]{:S(2)}) collective-permute-start(bf16[16,640]{1,0:T(8,128)(2,1)S(1)} %pack.1.refs_0_.rest_0_), channel_id=1, source_target_pairs={{0,8},{4,12},{8,0},{12,4},{1,9},{5,13},{9,1},{13,5},{2,10},{6,14},... | collective-permute-start | bytes 61448 | tf_op jit(solution)/shard_map/ppermute | solution.py:42
  7.4 0.0 collective-permute-start.2
  7.4 0.0 slice-start.2
  7.4 2.3 %front.1 = (f32[16,1024]{1,0:T(8,128)S(1)}, bf16[16,512]{1,0:T(8,128)(2,1)S(1)}) custom-call(bf16[3,16,1024]{2,1,0:T(8,128)(2,1)} %bitcast.17, bf16[16,1024]{1,0:T(8,128)(2,1)} %input_hbm.1, f32[4,1024]{1,0:T(4,128)} %taps_hbm.1, f32[1,1024]{1,0:T(1,128)} %bitcast.18, bf16[288,1024]{1,0:T(8,128)(2,1)} %proj_hbm.1), custom_call_target="tpu_custom_call" | custom-call | flops 10000000000 | bytes 1000000 | tf_op jit(solution)/shard_map/front/pallas_call | solution.py:158
  9.7 0.0 collective-permute-done.refs_1_.rest_1_
  9.7 0.0 collective-permute-done.1.refs_2_.rest_2_
  9.7 3.2 %collective-permute-done.2.refs_3_.rest_3_ = bf16[16,640]{1,0:T(8,128)(2,1)S(1)} collective-permute-done((bf16[16,640]{1,0:T(8,128)(2,1)S(1)}, bf16[16,640]{1,0:T(8,128)(2,1)S(1)}, u32[]{:S(2)}, u32[]{:S(2)}) %collective-permute-start.2) | collective-permute-done | bytes 20512 | tf_op jit(solution)/shard_map/ppermute | solution.py:42
  13.0 6.2 %all-gather = bf16[320,512]{1,0:T(8,128)(2,1)S(1)} all-gather(bf16[80,512]{1,0:T(8,128)(2,1)S(1)} %join.1), channel_id=2, replica_groups=mesh['parts'=2,'expert'=4,'tensor'=4] {'tensor'}, dimensions={0}, use_global_device_ids=true | all-gather | bytes 409600 | tf_op jit(solution)/shard_map/all_gather | solution.py:484
  19.2 0.0 slice-done.4
  19.2 0.0 slice-done.5
  19.2 0.0 slice-done.6
  19.2 0.0 slice-done.7
  19.2 0.0 slice-done.8
  19.2 0.0 slice-done.9
  19.2 0.0 slice-done.10
  19.2 0.0 slice-done.11
  19.3 0.0 slice-start.3
  19.3 8.8 %hidden.1 = bf16[2,2048,64]{2,1,0:T(8,128)(2,1)S(1)} custom-call(bf16[4,80,512]{2,1,0:T(8,128)(2,1)S(1)} %bitcast.12, bf16[2,2,2048,2048]{3,2,1,0:T(8,128)(2,1)S(1)} %bitcast.11), custom_call_target="tpu_custom_call" | custom-call | flops 100000000 | bytes 100000 | tf_op jit(solution)/shard_map/hidden/pallas_call | solution.py:339
  28.1 0.0 slice-done
  28.1 0.0 slice-done.1
  28.1 0.0 slice-done.2
  28.1 0.0 slice-done.3
  28.1 0.0 copy-start
  28.1 0.0 copy-start.4
  28.2 0.0 copy-start.6
  28.2 0.0 copy-start.9
  28.2 1.6 %shard_map.219 = (f32[64,512]{1,0:T(8,128)S(1)}, bf16[64,512]{1,0:T(8,128)(2,1)S(1)}) custom-call(bf16[2,2048,64]{2,1,0:T(8,128)(2,1)S(1)} %hidden.1, bf16[2,2048,2048]{2,1,0:T(8,128)(2,1)S(1)} %bitcast.9, bf16[16,640]{1,0:T(8,128)(2,1)S(1)} %pack.1.refs_0_.rest_0_, bf16[16,640]{1,0:T(8,128)(2,1)S(1)} %collective-permute-done.refs_1_.rest_1_, ...), custom_call_target="tpu_custom_call" | custom-call | flops 536870912 | bytes 8388608 | tf_op jit(solution)/shard_map/pallas_call | solution.py:354
  29.8 0.0 copy-start.1
  29.8 0.0 copy-start.2
  29.8 0.0 copy-start.3
  29.8 0.0 copy-start.5
  29.8 0.0 copy-start.7
  29.9 0.0 copy-start.8
  29.9 0.4 collective-permute-start.3
  30.3 1.6 %shard_map.220 = (bf16[64,512]{1,0:T(8,128)(2,1)S(1)}, bf16[64,512]{1,0:T(8,128)(2,1)S(1)}) custom-call(bf16[2,2048,64]{2,1,0:T(8,128)(2,1)S(1)} %hidden.1, bf16[2,2048,2048]{2,1,0:T(8,128)(2,1)S(1)} %bitcast.9, bf16[16,640]{1,0:T(8,128)(2,1)S(1)} %pack.1.refs_0_.rest_0_, bf16[16,640]{1,0:T(8,128)(2,1)S(1)} %collective-permute-done.refs_1_.rest_1_, ...), custom_call_target="tpu_custom_call" | custom-call | flops 536870912 | bytes 8388608 | tf_op jit(solution)/shard_map/pallas_call | solution.py:354
  31.9 1.4 %collective-permute-start.4 = (bf16[64,512]{1,0:T(8,128)(2,1)S(1)}, bf16[64,512]{1,0:T(8,128)(2,1)S(1)}, u32[]{:S(2)}, u32[]{:S(2)}) collective-permute-start(bf16[64,512]{1,0:T(8,128)(2,1)S(1)} %get-tuple-element.20), channel_id=1, source_target_pairs={{0,2},{1,3},{2,0},{3,1},{4,6},{5,7},{6,4},{7,5},{8,10},{9,11},{10,... | collective-permute-start | bytes 196616 | tf_op jit(solution)/shard_map/ppermute | solution.py:42
  33.3 0.2 collective-permute-start.5
  33.5 0.0 copy-done
  33.5 0.0 copy-done.4
  33.5 0.0 copy-done.6
  33.5 0.0 copy-done.9
  33.5 1.2 %attend.1.attended = bf16[16,1024]{1,0:T(8,128)(2,1)S(1)} custom-call(bf16[16,256,256]{2,1,0:T(8,128)(2,1)S(1)} %bitcast.14, bf16[16,8,128]{2,1,0:T(8,128)(2,1)S(1)} %copy-done.4, bf16[16,2,256]{2,1,0:T(2,128)(2,1)S(1)} %copy-done.6, s32[16]{0:T(128)S(1)} %copy-done.9), custom_call_target="tpu_custom_call" | custom-call | flops 4000000000 | bytes 2000000 | tf_op jit(solution)/shard_map/attend/pallas_call | solution.py:261
  34.8 0.0 collective-permute-done.3
  34.8 1.5 %collective-permute-done.4 = bf16[64,512]{1,0:T(8,128)(2,1)S(1)} collective-permute-done((bf16[64,512]{1,0:T(8,128)(2,1)S(1)}, bf16[64,512]{1,0:T(8,128)(2,1)S(1)}, u32[]{:S(2)}, u32[]{:S(2)}) %collective-permute-start.4) | collective-permute-done | bytes 65568 | tf_op jit(solution)/shard_map/ppermute | solution.py:42
  36.3 1.4 %collective-permute-done.5 = bf16[64,512]{1,0:T(8,128)(2,1)S(1)} collective-permute-done((bf16[64,512]{1,0:T(8,128)(2,1)S(1)}, bf16[64,512]{1,0:T(8,128)(2,1)S(1)}, u32[]{:S(2)}, u32[]{:S(2)}) %collective-permute-start.5) | collective-permute-done | bytes 65568 | tf_op jit(solution)/shard_map/ppermute | solution.py:42
  37.7 0.1 collective-permute-start.6
  37.8 1.1 %collective-permute-start.7 = (bf16[16,512]{1,0:T(8,128)(2,1)S(1)}, bf16[16,512]{1,0:T(8,128)(2,1)S(1)}, u32[]{:S(2)}, u32[]{:S(2)}) collective-permute-start(bf16[16,512]{1,0:T(8,128)(2,1)S(1)} %get-tuple-element.26), channel_id=1, source_target_pairs={{0,8},{4,12},{8,0},{12,4},{1,9},{5,13},{9,1},{13,5},{2,10},{6,14},... | collective-permute-start | bytes 49160 | tf_op jit(solution)/shard_map/ppermute | solution.py:42
  39.0 3.2 %collective-permute-start.8 = (bf16[16,512]{1,0:T(8,128)(2,1)S(1)}, bf16[16,512]{1,0:T(8,128)(2,1)S(1)}, u32[]{:S(2)}, u32[]{:S(2)}) collective-permute-start(bf16[16,512]{1,0:T(8,128)(2,1)S(1)} %get-tuple-element.25), channel_id=1, source_target_pairs={{0,12},{4,8},{8,4},{12,0},{1,13},{5,9},{9,5},{13,1},{2,14},{6,10},... | collective-permute-start | bytes 49160 | tf_op jit(solution)/shard_map/ppermute | solution.py:42
  42.2 0.0 copy-done.1
  42.2 0.0 copy-done.3
  42.2 1.8 %state.1 = (bf16[16,1024]{1,0:T(8,128)(2,1)}, f32[16,16,1024]{2,1,0:T(8,128)}, bf16[16,1024]{1,0:T(8,128)(2,1)}) custom-call(bf16[4,80,512]{2,1,0:T(8,128)(2,1)S(1)} %bitcast.13, f32[16,1024]{1,0:T(8,128)S(1)} %get-tuple-element.14.act, bf16[16,1024]{1,0:T(8,128)(2,1)S(1)} %copy-done.5, f32[16,16,1024]{2,1,0:T(8,128)S(1)} %copy-done.1, ...), custom_call_target="tpu_custom_call" | custom-call | flops 3000000000 | bytes 3000000 | tf_op jit(solution)/shard_map/state/pallas_call | solution.py:425
  44.1 0.0 collective-permute-done.6
  44.1 0.0 collective-permute-done.7
  44.1 0.4 collective-permute-done.8
  44.5 0.6 %fusion.2 = bf16[16,512]{1,0:T(8,128)(2,1)} fusion(f32[64,512]{1,0:T(8,128)S(1)} %get-tuple-element.23, bf16[16,512]{1,0:T(8,128)(2,1)S(1)} %collective-permute-done.8, bf16[16,512]{1,0:T(8,128)(2,1)S(1)} %collective-permute-done.7, bf16[16,512]{1,0:T(8,128)(2,1)S(1)} %collective-permute-done.6), kind=kLoop, calls=%fused_computation.4 | loop fusion | flops 57344 | bytes 98304 | tf_op jit(solution)/shard_map/convert_element_type | solution.py:502
  (12 shorter events, 0.1 us)
Async XLA Ops:
  0.6 18.6 %slice-start.4 = ((s8[33554432]{0:T(1024)(128)(4,1)}), s8[4194304]{0:T(1024)(128)(4,1)S(1)}, s32[]{:S(2)}) async-start(s8[33554432]{0:T(1024)(128)(4,1)} %bitcast.10), calls=%async_computation.4 | async-start | bytes 8388608
  0.6 18.6 %slice-start.5 = ((s8[33554432]{0:T(1024)(128)(4,1)}), s8[4194304]{0:T(1024)(128)(4,1)S(1)}, s32[]{:S(2)}) async-start(s8[33554432]{0:T(1024)(128)(4,1)} %bitcast.10), calls=%async_computation.5 | async-start | bytes 8388608
  0.7 18.5 %slice-start.6 = ((s8[33554432]{0:T(1024)(128)(4,1)}), s8[4194304]{0:T(1024)(128)(4,1)S(1)}, s32[]{:S(2)}) async-start(s8[33554432]{0:T(1024)(128)(4,1)} %bitcast.10), calls=%async_computation.6 | async-start | bytes 8388608
  0.7 18.5 %slice-start.7 = ((s8[33554432]{0:T(1024)(128)(4,1)}), s8[4194304]{0:T(1024)(128)(4,1)S(1)}, s32[]{:S(2)}) async-start(s8[33554432]{0:T(1024)(128)(4,1)} %bitcast.10), calls=%async_computation.7 | async-start | bytes 8388608
  0.7 18.5 %slice-start.8 = ((s8[33554432]{0:T(1024)(128)(4,1)}), s8[4194304]{0:T(1024)(128)(4,1)S(1)}, s32[]{:S(2)}) async-start(s8[33554432]{0:T(1024)(128)(4,1)} %bitcast.10), calls=%async_computation.8 | async-start | bytes 8388608
  0.7 18.5 %slice-start.9 = ((s8[33554432]{0:T(1024)(128)(4,1)}), s8[4194304]{0:T(1024)(128)(4,1)S(1)}, s32[]{:S(2)}) async-start(s8[33554432]{0:T(1024)(128)(4,1)} %bitcast.10), calls=%async_computation.9 | async-start | bytes 8388608
  0.7 18.5 %slice-start.10 = ((s8[33554432]{0:T(1024)(128)(4,1)}), s8[4194304]{0:T(1024)(128)(4,1)S(1)}, s32[]{:S(2)}) async-start(s8[33554432]{0:T(1024)(128)(4,1)} %bitcast.10), calls=%async_computation.10 | async-start | bytes 8388608
  1.7 8.0 %collective-permute-start = (bf16[16,640]{1,0:T(8,128)(2,1)S(1)}, bf16[16,640]{1,0:T(8,128)(2,1)S(1)}, u32[]{:S(2)}, u32[]{:S(2)}) collective-permute-start(bf16[16,640]{1,0:T(8,128)(2,1)S(1)} %pack.1.refs_0_.rest_0_), channel_id=1, source_target_pairs={{0,4},{4,0},{8,12},{12,8},{1,5},{5,1},{9,13},{13,9},{2,6},{6,2},{1... | collective-permute-start | bytes 61448 | tf_op jit(solution)/shard_map/ppermute | solution.py:42
  4.8 4.9 %collective-permute-start.1 = (bf16[16,640]{1,0:T(8,128)(2,1)S(1)}, bf16[16,640]{1,0:T(8,128)(2,1)S(1)}, u32[]{:S(2)}, u32[]{:S(2)}) collective-permute-start(bf16[16,640]{1,0:T(8,128)(2,1)S(1)} %pack.1.refs_0_.rest_0_), channel_id=1, source_target_pairs={{0,8},{4,12},{8,0},{12,4},{1,9},{5,13},{9,1},{13,5},{2,10},{6,14},... | collective-permute-start | bytes 61448 | tf_op jit(solution)/shard_map/ppermute | solution.py:42
  7.4 5.6 %collective-permute-start.2 = (bf16[16,640]{1,0:T(8,128)(2,1)S(1)}, bf16[16,640]{1,0:T(8,128)(2,1)S(1)}, u32[]{:S(2)}, u32[]{:S(2)}) collective-permute-start(bf16[16,640]{1,0:T(8,128)(2,1)S(1)} %pack.1.refs_0_.rest_0_), channel_id=1, source_target_pairs={{0,12},{4,8},{8,4},{12,0},{1,13},{5,9},{9,5},{13,1},{2,14},{6,10},... | collective-permute-start | bytes 61448 | tf_op jit(solution)/shard_map/ppermute | solution.py:42
  7.4 11.8 %slice-start.11 = ((s8[33554432]{0:T(1024)(128)(4,1)}), s8[4194304]{0:T(1024)(128)(4,1)S(1)}, s32[]{:S(2)}) async-start(s8[33554432]{0:T(1024)(128)(4,1)} %bitcast.10), calls=%async_computation.11 | async-start | bytes 8388608
  7.4 20.7 %slice-start = ((s8[16777216]{0:T(1024)(128)(4,1)}), s8[4194304]{0:T(1024)(128)(4,1)S(1)}, s32[]{:S(2)}) async-start(s8[16777216]{0:T(1024)(128)(4,1)} %bitcast.8), calls=%async_computation | async-start | bytes 8388608
  7.4 20.7 %slice-start.1 = ((s8[16777216]{0:T(1024)(128)(4,1)}), s8[4194304]{0:T(1024)(128)(4,1)S(1)}, s32[]{:S(2)}) async-start(s8[16777216]{0:T(1024)(128)(4,1)} %bitcast.8), calls=%async_computation.1 | async-start | bytes 8388608
  7.4 20.7 %slice-start.2 = ((s8[16777216]{0:T(1024)(128)(4,1)}), s8[4194304]{0:T(1024)(128)(4,1)S(1)}, s32[]{:S(2)}) async-start(s8[16777216]{0:T(1024)(128)(4,1)} %bitcast.8), calls=%async_computation.2 | async-start | bytes 8388608
  19.3 8.9 %slice-start.3 = ((s8[16777216]{0:T(1024)(128)(4,1)}), s8[4194304]{0:T(1024)(128)(4,1)S(1)}, s32[]{:S(2)}) async-start(s8[16777216]{0:T(1024)(128)(4,1)} %bitcast.8), calls=%async_computation.3 | async-start | bytes 8388608
  28.1 5.4 %copy-start = (bf16[16,2,128,256]{3,2,1,0:T(8,128)(2,1)S(1)}, bf16[16,2,128,256]{3,2,1,0:T(8,128)(2,1)}, u32[]{:S(2)}) copy-start(bf16[16,2,128,256]{3,2,1,0:T(8,128)(2,1)} %param.34) | copy-start | bytes 6291460
  28.1 5.4 %copy-start.4 = (bf16[16,8,128]{2,1,0:T(8,128)(2,1)S(1)}, bf16[16,8,128]{2,1,0:T(8,128)(2,1)}, u32[]{:S(2)}) copy-start(bf16[16,8,128]{2,1,0:T(8,128)(2,1)} %queries.1) | copy-start | bytes 98308
  28.2 5.4 %copy-start.6 = (bf16[16,2,256]{2,1,0:T(2,128)(2,1)S(1)}, bf16[16,2,256]{2,1,0:T(2,128)(2,1)}, u32[]{:S(2)}) copy-start(bf16[16,2,256]{2,1,0:T(2,128)(2,1)} %entry.1) | copy-start | bytes 49156
  28.2 5.4 %copy-start.9 = (s32[16]{0:T(128)S(1)}, s32[16]{0:T(128)}, u32[]{:S(2)}) copy-start(s32[16]{0:T(128)} %lengths_ref.1) | copy-start | bytes 196
  29.8 12.4 %copy-start.1 = (f32[16,16,1024]{2,1,0:T(8,128)S(1)}, f32[16,16,1024]{2,1,0:T(8,128)}, u32[]{:S(2)}) copy-start(f32[16,16,1024]{2,1,0:T(8,128)} %scan.1) | copy-start | bytes 3145732
  29.8 12.4 %copy-start.2 = (bf16[256,1024]{1,0:T(8,128)(2,1)S(1)}, bf16[256,1024]{1,0:T(8,128)(2,1)}, u32[]{:S(2)}) copy-start(bf16[256,1024]{1,0:T(8,128)(2,1)} %step_proj.1) | copy-start | bytes 1572868
  29.8 12.4 %copy-start.3 = (f32[16,1024]{1,0:T(8,128)S(1)}, f32[16,1024]{1,0:T(8,128)}, u32[]{:S(2)}) copy-start(f32[16,1024]{1,0:T(8,128)} %decay.1) | copy-start | bytes 196612
  29.8 12.4 %copy-start.5 = (bf16[16,1024]{1,0:T(8,128)(2,1)S(1)}, bf16[16,1024]{1,0:T(8,128)(2,1)}, u32[]{:S(2)}) copy-start(bf16[16,1024]{1,0:T(8,128)(2,1)} %gate.1) | copy-start | bytes 98308
  29.8 12.4 %copy-start.7 = (f32[1024]{0:T(1024)S(1)}, f32[1024]{0:T(1024)}, u32[]{:S(2)}) copy-start(f32[1024]{0:T(1024)} %param.29) | copy-start | bytes 12292
  29.9 12.4 %copy-start.8 = (f32[1024]{0:T(1024)S(1)}, f32[1024]{0:T(1024)}, u32[]{:S(2)}) copy-start(f32[1024]{0:T(1024)} %param.31) | copy-start | bytes 12292
  29.9 4.9 %collective-permute-start.3 = (bf16[64,512]{1,0:T(8,128)(2,1)S(1)}, bf16[64,512]{1,0:T(8,128)(2,1)S(1)}, u32[]{:S(2)}, u32[]{:S(2)}) collective-permute-start(bf16[64,512]{1,0:T(8,128)(2,1)S(1)} %get-tuple-element.19), channel_id=1, source_target_pairs={{0,1},{1,0},{2,3},{3,2},{4,5},{5,4},{6,7},{7,6},{8,9},{9,8},{10,11... | collective-permute-start | bytes 196616 | tf_op jit(solution)/shard_map/ppermute | solution.py:42
  31.9 4.3 %collective-permute-start.4 = (bf16[64,512]{1,0:T(8,128)(2,1)S(1)}, bf16[64,512]{1,0:T(8,128)(2,1)S(1)}, u32[]{:S(2)}, u32[]{:S(2)}) collective-permute-start(bf16[64,512]{1,0:T(8,128)(2,1)S(1)} %get-tuple-element.20), channel_id=1, source_target_pairs={{0,2},{1,3},{2,0},{3,1},{4,6},{5,7},{6,4},{7,5},{8,10},{9,11},{10,... | collective-permute-start | bytes 196616 | tf_op jit(solution)/shard_map/ppermute | solution.py:42
  33.3 4.3 %collective-permute-start.5 = (bf16[64,512]{1,0:T(8,128)(2,1)S(1)}, bf16[64,512]{1,0:T(8,128)(2,1)S(1)}, u32[]{:S(2)}, u32[]{:S(2)}) collective-permute-start(bf16[64,512]{1,0:T(8,128)(2,1)S(1)} %get-tuple-element.21), channel_id=1, source_target_pairs={{0,3},{1,2},{2,1},{3,0},{4,7},{5,6},{6,5},{7,4},{8,11},{9,10},{10,... | collective-permute-start | bytes 196616 | tf_op jit(solution)/shard_map/ppermute | solution.py:42
  37.7 6.3 %collective-permute-start.6 = (bf16[16,512]{1,0:T(8,128)(2,1)S(1)}, bf16[16,512]{1,0:T(8,128)(2,1)S(1)}, u32[]{:S(2)}, u32[]{:S(2)}) collective-permute-start(bf16[16,512]{1,0:T(8,128)(2,1)S(1)} %get-tuple-element.24), channel_id=1, source_target_pairs={{0,4},{4,0},{8,12},{12,8},{1,5},{5,1},{9,13},{13,9},{2,6},{6,2},{1... | collective-permute-start | bytes 49160 | tf_op jit(solution)/shard_map/ppermute | solution.py:42
  37.8 6.2 %collective-permute-start.7 = (bf16[16,512]{1,0:T(8,128)(2,1)S(1)}, bf16[16,512]{1,0:T(8,128)(2,1)S(1)}, u32[]{:S(2)}, u32[]{:S(2)}) collective-permute-start(bf16[16,512]{1,0:T(8,128)(2,1)S(1)} %get-tuple-element.26), channel_id=1, source_target_pairs={{0,8},{4,12},{8,0},{12,4},{1,9},{5,13},{9,1},{13,5},{2,10},{6,14},... | collective-permute-start | bytes 49160 | tf_op jit(solution)/shard_map/ppermute | solution.py:42
  39.0 5.5 %collective-permute-start.8 = (bf16[16,512]{1,0:T(8,128)(2,1)S(1)}, bf16[16,512]{1,0:T(8,128)(2,1)S(1)}, u32[]{:S(2)}, u32[]{:S(2)}) collective-permute-start(bf16[16,512]{1,0:T(8,128)(2,1)S(1)} %get-tuple-element.25), channel_id=1, source_target_pairs={{0,12},{4,8},{8,4},{12,0},{1,13},{5,9},{9,5},{13,1},{2,14},{6,10},... | collective-permute-start | bytes 49160 | tf_op jit(solution)/shard_map/ppermute | solution.py:42
